TPU v7x, 32 devices: a whole 2x2x4 slice. The times are simulated.
32 devices in a mesh: wa: 8 (over z, x), ta: 4 (over y, core).
Axes of the slice: x: 2, y: 2, z: 4, core: 2. Of those that a mesh axis runs over, the one named last changes fastest.
Arguments:
- tokens: bfloat16 [12544, 512], P('wa', 'ta'), may hold values from -6 to 6
- gain_one: float32 [512], P('ta'), may hold values from 0.5 to 1.5
- shift_one: float32 [512], P('ta'), may hold values from -3 to 3
- w_query: bfloat16 [512, 512], P('wa', 'ta'), may hold values from -1 to 1
- w_key: bfloat16 [512, 512], P('wa', 'ta'), may hold values from -0.25 to 0.25
- w_value: bfloat16 [512, 512], P('wa', 'ta'), may hold values from -0.25 to 0.25
- b_query: float32 [512], P('ta'), may hold values from -3 to 3
- b_value: float32 [512], P('ta'), may hold values from -3 to 3
- w_out: bfloat16 [512, 512], P('ta', 'wa'), may hold values from -0.75 to 0.75
- b_out: float32 [512], P('ta'), may hold values from -3 to 3
- gain_two: float32 [512], P('ta'), may hold values from 0.5 to 1.5
- shift_two: float32 [512], P('ta'), may hold values from -3 to 3
- w_hidden: bfloat16 [512, 2048], P('wa', 'ta'), may hold values from -0.25 to 0.25
- b_hidden: float32 [2048], P('ta'), may hold values from -3 to 3
- w_down: bfloat16 [2048, 512], P('ta', 'wa'), may hold values from -0.125 to 0.125
- b_down: float32 [512], P('ta'), may hold values from -3 to 3
- bias_table: float32 [169, 16], P(None, 'ta'), may hold values from -4 to 4
- rel_index: int32 [49, 49], replicated, may hold values from 0 to 168, as said below
- region: int32 [256, 49], P('wa'), may hold values from 0 to 3, as said below
- win_count: int32 [8], P('wa'), may hold values from 16 to 32, as said below
- cotangent: bfloat16 [12544, 512], P('wa', 'ta'), may hold values from -6 to 6
Outputs:
- y_out: float32 [12544, 512], P('wa', 'ta')
- grad_tokens: float32 [12544, 512], P('wa', 'ta')
- grad_gain_one: float32 [512], P('ta')
- grad_shift_one: float32 [512], P('ta')
- grad_w_query: float32 [512, 512], P('wa', 'ta')
- grad_w_key: float32 [512, 512], P('wa', 'ta')
- grad_w_value: float32 [512, 512], P('wa', 'ta')
- grad_b_query: float32 [512], P('ta')
- grad_b_value: float32 [512], P('ta')
- grad_w_out: float32 [512, 512], P('ta', 'wa')
- grad_b_out: float32 [512], P('ta')
- grad_gain_two: float32 [512], P('ta')
- grad_shift_two: float32 [512], P('ta')
- grad_w_hidden: float32 [512, 2048], P('wa', 'ta')
- grad_b_hidden: float32 [2048], P('ta')
- grad_w_down: float32 [2048, 512], P('ta', 'wa')
- grad_b_down: float32 [512], P('ta')
- grad_table: float32 [169, 16], P(None, 'ta')
Inputs may be any that keep to these rules, and one draw needn't show every extreme that they name: `rel_index`: pairs (i, j) of window positions with the same offset of rows and of columns share an entry, and every entry is used. Within a window slot, region is constant on rectangular blocks of positions cut by at most one row and one column. `win_count`: some index of wa has all 32 slots live.
All inputs are finite; a program needn't handle non-finite values.
Results may differ from a plain program's by a relative error of at most 0.012.
Values may be sent and summed in bfloat16 or wider, within the bound.
A program may use at most 128 MiB of HBM per device.

v0:
```python
import jax
import jax.numpy as jnp
from jax import lax
from jax.sharding import PartitionSpec as P

C = 512
HDIM = 32
WT = 49
TABLE = 169


eps_norm = 1e-05
mask_value = -100.0


def row_sums(first, second):
    return lax.psum((jnp.sum(first, axis=1), jnp.sum(second, axis=1)), "ta")


def full_rows(value):
    return lax.all_gather(value, "ta", axis=1, tiled=True)


def share(value):
    return lax.psum_scatter(value, "ta", scatter_dimension=1, tiled=True)


def gather_inputs(weight):
    return lax.all_gather(weight, "wa", axis=0, tiled=True)


def gather_outputs(weight):
    return lax.all_gather(weight, "wa", axis=1, tiled=True)


def gather_inputs_again(weight):
    return lax.all_gather(weight, "wa", axis=0, tiled=True)


def gather_outputs_again(weight):
    return lax.all_gather(weight, "wa", axis=1, tiled=True)


def output_grads(value):
    return lax.psum_scatter(value, "wa", scatter_dimension=1, tiled=True)


def cross(left, right):
    return lax.dot_general(
        left, right, (((0,), (0,)), ((), ())), preferred_element_type=jnp.float32
    )


def against(left, right):
    return lax.dot_general(
        left, right, (((1,), (1,)), ((), ())), preferred_element_type=jnp.float32
    )


def input_grads(acts_full, grads_low):
    return lax.psum_scatter(cross(acts_full, grads_low), "wa", scatter_dimension=0, tiled=True)


def norm_forward(value, gain, shift):
    sums = row_sums(value, value * value)
    mean = sums[0][:, None] / C
    spread = sums[1][:, None] / C - mean * mean
    rstd = lax.rsqrt(spread + eps_norm)
    normed = (value - mean) * rstd
    return (normed, rstd, normed * gain + shift)


def norm_backward(grad_out, normed, rstd, gain):
    scaled = grad_out * gain
    sums = row_sums(scaled, scaled * normed)
    grad_in = rstd * (scaled - sums[0][:, None] / C - normed * (sums[1][:, None] / C))
    return (grad_in, jnp.sum(grad_out * normed, axis=0), jnp.sum(grad_out, axis=0))


def window_scores(query_view, key_view, rel_bias, allowed):
    scores = jnp.einsum("wihd,wjhd->whij", query_view, key_view, preferred_element_type=jnp.float32)
    return scores + rel_bias[None] + allowed[:, None]


def exact_gelu(value):
    return jax.nn.gelu(value, approximate=False)


def per_device(
    tokens,
    gain_one,
    shift_one,
    w_query,
    w_key,
    w_value,
    b_query,
    b_value,
    w_out,
    b_out,
    gain_two,
    shift_two,
    w_hidden,
    b_hidden,
    w_down,
    b_down,
    bias_table,
    rel_index,
    region,
    win_count,
    cotangent,
):
    slots = region.shape[0]
    rows = tokens.shape[0]
    heads = bias_table.shape[1]
    width = w_query.shape[1]
    scale = HDIM ** (-0.5)
    within = jnp.arange(rows, dtype=jnp.int32) // WT
    live = (within < win_count[0]).astype(jnp.float32)[:, None]
    onehot = (rel_index.reshape(-1)[:, None] == jnp.arange(TABLE, dtype=jnp.int32)[None, :]).astype(
        jnp.float32
    )
    rel_bias = jnp.dot(
        onehot, bias_table, precision=lax.Precision.HIGHEST, preferred_element_type=jnp.float32
    ).T.reshape(heads, WT, WT)
    allowed = jnp.where(region[:, :, None] == region[:, None, :], 0.0, mask_value).astype(
        jnp.float32
    )
    start_value = tokens.astype(jnp.float32)
    normed_one, rstd_one, pre_one = norm_forward(start_value, gain_one, shift_one)
    h_one = full_rows(pre_one.astype(jnp.bfloat16))
    qkv_cols = gather_inputs(jnp.concatenate((w_query, w_key, w_value), axis=1))
    projected = jnp.dot(h_one, qkv_cols, preferred_element_type=jnp.float32)
    query = ((projected[:, :width] + b_query) * scale).astype(jnp.bfloat16)
    keyset = projected[:, width : 2 * width].astype(jnp.bfloat16)
    values = (projected[:, 2 * width :] + b_value).astype(jnp.bfloat16)
    query_view = query.reshape(slots, WT, heads, HDIM)
    key_view = keyset.reshape(slots, WT, heads, HDIM)
    value_view = values.reshape(slots, WT, heads, HDIM)
    scores = window_scores(query_view, key_view, rel_bias, allowed)
    top = jnp.max(scores, axis=-1, keepdims=True)
    log_total = top + jnp.log(jnp.sum(jnp.exp(scores - top), axis=-1, keepdims=True))
    probs_low = jnp.exp(scores - log_total).astype(jnp.bfloat16)
    attended = jnp.einsum(
        "whij,wjhd->wihd", probs_low, value_view, preferred_element_type=jnp.float32
    )
    attended = attended.reshape(rows, width).astype(jnp.bfloat16)
    out_rows = gather_outputs(w_out)
    mixed = (
        start_value + share(jnp.dot(attended, out_rows, preferred_element_type=jnp.float32)) + b_out
    )
    normed_two, rstd_two, pre_two = norm_forward(mixed, gain_two, shift_two)
    h_two = full_rows(pre_two.astype(jnp.bfloat16))
    hidden_cols = gather_inputs(w_hidden)
    hidden = jnp.dot(h_two, hidden_cols, preferred_element_type=jnp.float32) + b_hidden
    act, gelu_pull = jax.vjp(exact_gelu, hidden)
    act_low = act.astype(jnp.bfloat16)
    down_rows = gather_outputs(w_down)
    result = mixed + share(jnp.dot(act_low, down_rows, preferred_element_type=jnp.float32)) + b_down
    y_out = result * live
    qkv_back = gather_inputs_again(jnp.concatenate((w_query, w_key, w_value), axis=1))
    hidden_back = gather_inputs_again(w_hidden)
    out_back = gather_outputs_again(w_out)
    down_back = gather_outputs_again(w_down)
    grad_y = cotangent.astype(jnp.float32) * live
    grad_full = full_rows(grad_y.astype(jnp.bfloat16))
    grad_w_down = output_grads(cross(act_low, grad_full))
    grad_act = against(grad_full, down_back)
    grad_hid = gelu_pull(grad_act)[0]
    grad_hid_low = grad_hid.astype(jnp.bfloat16)
    grad_w_hidden = input_grads(h_two, grad_hid_low)
    grad_h_two = share(against(grad_hid_low, hidden_back))
    grad_mixed, gain_two_part, shift_two_part = norm_backward(
        grad_h_two, normed_two, rstd_two, gain_two
    )
    grad_mixed = grad_mixed + grad_y
    grad_mixed_full = full_rows(grad_mixed.astype(jnp.bfloat16))
    grad_w_out = output_grads(cross(attended, grad_mixed_full))
    grad_att = against(grad_mixed_full, out_back).astype(jnp.bfloat16)
    grad_att_view = grad_att.reshape(slots, WT, heads, HDIM)
    again_scores = window_scores(query_view, key_view, rel_bias, allowed)
    probs = jnp.exp(again_scores - log_total)
    grad_probs = jnp.einsum(
        "wihd,wjhd->whij", grad_att_view, value_view, preferred_element_type=jnp.float32
    )
    grad_scores = probs * (grad_probs - jnp.sum(probs * grad_probs, axis=-1, keepdims=True))
    grad_scores_low = grad_scores.astype(jnp.bfloat16)
    pair_sums = jnp.sum(grad_scores_low.astype(jnp.float32), axis=0).reshape(heads, WT * WT)
    table_part = lax.dot_general(
        onehot,
        pair_sums,
        (((0,), (1,)), ((), ())),
        precision=lax.Precision.HIGHEST,
        preferred_element_type=jnp.float32,
    )
    grad_q = (
        jnp.einsum("whij,wjhd->wihd", grad_scores_low, key_view, preferred_element_type=jnp.float32)
        .reshape(rows, width)
        .astype(jnp.bfloat16)
    )
    grad_k = (
        jnp.einsum(
            "whij,wihd->wjhd", grad_scores_low, query_view, preferred_element_type=jnp.float32
        )
        .reshape(rows, width)
        .astype(jnp.bfloat16)
    )
    grad_v = (
        jnp.einsum("whij,wihd->wjhd", probs_low, grad_att_view, preferred_element_type=jnp.float32)
        .reshape(rows, width)
        .astype(jnp.bfloat16)
    )
    grad_qkv = jnp.concatenate((grad_q, grad_k, grad_v), axis=1)
    qkv_grad = input_grads(h_one, grad_qkv)
    grad_h_one = share(
        scale * against(grad_q, qkv_back[:, :width])
        + against(grad_qkv[:, width:], qkv_back[:, width:])
    )
    grad_start, gain_one_part, shift_one_part = norm_backward(
        grad_h_one, normed_one, rstd_one, gain_one
    )
    grad_tokens = grad_start + grad_mixed
    summed = lax.psum(
        (
            gain_one_part,
            shift_one_part,
            scale * jnp.sum(grad_q.astype(jnp.float32), axis=0),
            jnp.sum(grad_v.astype(jnp.float32), axis=0),
            jnp.sum(grad_mixed, axis=0),
            gain_two_part,
            shift_two_part,
            jnp.sum(grad_hid, axis=0),
            jnp.sum(grad_y, axis=0),
            table_part,
        ),
        "wa",
    )
    return (
        y_out,
        grad_tokens,
        summed[0],
        summed[1],
        scale * qkv_grad[:, :width],
        qkv_grad[:, width : 2 * width],
        qkv_grad[:, 2 * width :],
        summed[2],
        summed[3],
        grad_w_out,
        summed[4],
        summed[5],
        summed[6],
        grad_w_hidden,
        summed[7],
        grad_w_down,
        summed[8],
        summed[9],
    )


def solution(mesh):
    return jax.shard_map(
        per_device,
        mesh=mesh,
        in_specs=(
            P("wa", "ta"),
            P("ta"),
            P("ta"),
            P("wa", "ta"),
            P("wa", "ta"),
            P("wa", "ta"),
            P("ta"),
            P("ta"),
            P("ta", "wa"),
            P("ta"),
            P("ta"),
            P("ta"),
            P("wa", "ta"),
            P("ta"),
            P("ta", "wa"),
            P("ta"),
            P(None, "ta"),
            P(),
            P("wa", None),
            P("wa"),
            P("wa", "ta"),
        ),
        out_specs=(
            P("wa", "ta"),
            P("wa", "ta"),
            P("ta"),
            P("ta"),
            P("wa", "ta"),
            P("wa", "ta"),
            P("wa", "ta"),
            P("ta"),
            P("ta"),
            P("ta", "wa"),
            P("ta"),
            P("ta"),
            P("ta"),
            P("wa", "ta"),
            P("ta"),
            P("ta", "wa"),
            P("ta"),
            P(None, "ta"),
        ),
        check_vma=False,
    )
```

profile of v0, /device:TPU:0, one launch (start us, length us, event | category | flops | bytes accessed | tf_op | source)
XLA Modules:
  0.0 712.9 jit_solution(9164277731949525365)
XLA Ops:
  8.7 12.7 %all-reduce.4 = (f32[1568]{0:T(1024)S(1)}, f32[1568]{0:T(1024)S(1)}) all-reduce(f32[1568]{0:T(1024)S(1)} %get-tuple-element.29, f32[1568]{0:T(1024)S(1)} %get-tuple-element.28), channel_id=1, replica_groups=mesh['wa'=8,'ta'=4] {'ta'}, use_global_device_ids=true, to_apply=%region_3.4 | all-reduce | flops 3136 | bytes 25088 | tf_op jit(solution)/shard_map/psum | solution.py:17
  21.4 2.3 fusion.30
  26.7 31.1 %all_gather.30 = bf16[128,512]{0,1:T(8,128)(2,1)S(1)} all-gather(bf16[128,64]{0,1:T(8,128)(2,1)} %param.29), channel_id=1, replica_groups=mesh['wa'=8,'ta'=4] {'wa'}, dimensions={1}, use_global_device_ids=true | all-gather | bytes 147456 | tf_op jit(solution)/shard_map/all_gather | solution.py:33
  58.7 31.3 %all_gather.29 = bf16[512,384]{1,0:T(8,128)(2,1)S(1)} all-gather(bf16[64,384]{1,0:T(8,128)(2,1)S(1)} %pad_maximum_fusion), channel_id=1, replica_groups=mesh['wa'=8,'ta'=4] {'wa'}, dimensions={0}, use_global_device_ids=true | all-gather | bytes 442368 | tf_op jit(solution)/shard_map/all_gather | solution.py:29
  90.3 2.4 fusion.64
  95.5 3.3 copy.76
  100.7 3.3 copy.77
  104.0 3.7 reshape.132
  107.7 3.6 copy.79
  118.4 2.3 fusion.65
  120.8 38.0 %reduce-scatter.9.cloned.1.call-done = f32[1568,128]{1,0:T(8,128)} async-done(((f32[1568,512]{1,0:T(8,128)}), f32[1568,128]{1,0:T(8,128)}) %reduce-scatter.9.cloned.1.call-update) | async-done | bytes 802832 | tf_op jit(solution)/shard_map/reduce_scatter | solution.py:25
  160.5 10.4 %all-reduce.3 = (f32[1568]{0:T(1024)S(1)}, f32[1568]{0:T(1024)S(1)}) all-reduce(f32[1568]{0:T(1024)S(1)} %get-tuple-element.27, f32[1568]{0:T(1024)S(1)} %get-tuple-element.26), channel_id=1, replica_groups=mesh['wa'=8,'ta'=4] {'ta'}, use_global_device_ids=true, to_apply=%region_10.11 | all-reduce | flops 3136 | bytes 25088 | tf_op jit(solution)/shard_map/psum | solution.py:17
  174.1 31.6 %all_gather.32 = bf16[512,512]{1,0:T(8,128)(2,1)S(1)} all-gather(bf16[64,512]{1,0:T(8,128)(2,1)S(1)} %copy-done.28), channel_id=1, replica_groups=mesh['wa'=8,'ta'=4] {'wa'}, dimensions={0}, use_global_device_ids=true | all-gather | bytes 589824 | tf_op jit(solution)/shard_map/all_gather | solution.py:29
  205.6 33.2 %all_gather.33 = bf16[512,512]{0,1:T(8,128)(2,1)} all-gather(bf16[512,64]{0,1:T(8,128)(2,1)S(1)} %copy-done.29), channel_id=1, replica_groups=mesh['wa'=8,'ta'=4] {'wa'}, dimensions={1}, use_global_device_ids=true | all-gather | bytes 589824 | tf_op jit(solution)/shard_map/all_gather | solution.py:33
  238.8 4.1 convolution_add_fusion
  243.0 11.7 %fusion.59 = (f32[512]{0:T(512)}, bf16[1568,512]{1,0:T(8,128)(2,1)S(1)}, f32[1568,512]{1,0:T(8,128)}) fusion(f32[1568,512]{1,0:T(8,128)} %convolution_add_fusion, bf16[1568,512]{1,0:T(8,128)(2,1)} %all-gather.9.cloned.1.call-done, bf16[512,512]{0,1:T(8,128)(2,1)} %all_gather.33), kind=kOutput, calls=%fused_computation.119 | convolution fusion | flops 880688640 | bytes 10160128 | tf_op jit(solution)/shard_map/dot_general | solution.py:55
  254.7 2.7 fusion.43
  257.6 3.8 multiply_convert_fusion.1
  262.5 2.8 fusion.66
  265.3 31.0 %reduce-scatter.13.cloned.1.call-done = f32[1568,128]{1,0:T(8,128)} async-done(((f32[1568,512]{1,0:T(8,128)}), f32[1568,128]{1,0:T(8,128)}) %reduce-scatter.13.cloned.1.call-update) | async-done | bytes 802832 | tf_op jit(solution)/shard_map/reduce_scatter | solution.py:25
  296.3 2.7 multiply_reduce_fusion.1
  299.0 11.3 %all-reduce.2 = (f32[1568]{0:T(1024)}, f32[1568]{0:T(1024)}) all-reduce(f32[1568]{0:T(1024)} %get-tuple-element.19, f32[1568]{0:T(1024)} %get-tuple-element.23), channel_id=1, replica_groups=mesh['wa'=8,'ta'=4] {'ta'}, use_global_device_ids=true, to_apply=%region_16.17 | all-reduce | flops 3136 | bytes 25088 | tf_op jit(solution)/shard_map/psum | solution.py:17
  311.7 25.2 %reduce-scatter.11.cloned.1.call-done = f32[1568,128]{1,0:T(8,128)} async-done(((f32[1568,512]{1,0:T(8,128)}), f32[1568,128]{1,0:T(8,128)}) %reduce-scatter.11.cloned.1.call-update) | async-done | bytes 802832 | tf_op jit(solution)/shard_map/reduce_scatter | solution.py:25
  336.9 4.8 fusion.61
  343.4 20.1 %all-gather.11.cloned.1.call-done = bf16[1568,512]{1,0:T(8,128)(2,1)} async-done(((bf16[1568,128]{1,0:T(8,128)(2,1)}), bf16[1568,512]{1,0:T(8,128)(2,1)}) %all-gather.11.cloned.1.call-update) | async-done | bytes 1605648 | tf_op jit(solution)/shard_map/all_gather | solution.py:21
  367.4 4.0 copy.83
  371.4 3.7 convert_reduce_fusion.1
  377.1 2.2 convert_reduce_fusion
  379.3 2.1 fusion.11
  383.7 2.7 convert_element_type.126
  386.4 3.1 copy.87
  389.5 3.4 convert_element_type.120
  392.9 2.9 copy.90
  395.7 3.5 convert_element_type.123
  399.3 3.3 fusion.12
  404.6 3.2 fusion
  409.2 3.6 fusion.68
  412.9 3.6 fusion.41
  418.0 2.9 fusion.67
  420.9 45.2 %reduce-scatter.17.cloned.1.call-done = f32[64,384]{1,0:T(8,128)} async-done(((f32[512,384]{1,0:T(8,128)}), f32[64,384]{1,0:T(8,128)}) %reduce-scatter.17.cloned.1.call-update) | async-done | bytes 98320 | tf_op jit(solution)/shard_map/reduce_scatter | solution.py:61
  467.5 38.4 %reduce-scatter.15.cloned.1.call-done = f32[1568,128]{1,0:T(8,128)} async-done(((f32[1568,512]{1,0:T(8,128)}), f32[1568,128]{1,0:T(8,128)}) %reduce-scatter.15.cloned.1.call-update) | async-done | bytes 802832 | tf_op jit(solution)/shard_map/reduce_scatter | solution.py:25
  505.8 2.1 fusion.35
  507.9 10.1 %all-reduce.1 = (f32[1568]{0:T(1024)S(1)}, f32[1568]{0:T(1024)S(1)}) all-reduce(f32[1568]{0:T(1024)S(1)} %get-tuple-element.21, f32[1568]{0:T(1024)S(1)} %get-tuple-element.22), channel_id=1, replica_groups=mesh['wa'=8,'ta'=4] {'ta'}, use_global_device_ids=true, to_apply=%region_22.23 | all-reduce | flops 3136 | bytes 25088 | tf_op jit(solution)/shard_map/psum | solution.py:17
  518.1 37.3 %all-reduce = (f32[128]{0:T(128)}, f32[128]{0:T(128)}, f32[128]{0:T(128)}, f32[128]{0:T(128)}, f32[128]{0:T(128)}, /*index=5*/f32[128]{0:T(128)}, f32[128]{0:T(1...) all-reduce(f32[128]{0:T(128)S(1)} %get-tuple-element.20, ...), channel_id=1, replica_groups=mesh['wa'=8,'ta'=4] {'wa'}, use_global_device_ids=true, to_apply=%region_24.25 | all-reduce | flops 2212 | bytes 17696 | tf_op jit(solution)/shard_map/psum | solution.py:222
  555.4 3.0 fusion.34
  558.4 15.6 %reduce-scatter.23.cloned.1.call-done = f32[512,64]{0,1:T(8,128)} async-done(((f32[512,512]{0,1:T(8,128)}), f32[512,64]{0,1:T(8,128)}) %reduce-scatter.23.cloned.1.call-update) | async-done | bytes 131088 | tf_op jit(solution)/shard_map/reduce_scatter | solution.py:45
  574.0 67.1 %reduce-scatter.21.cloned.1.call-done = f32[64,512]{1,0:T(8,128)} async-done(((f32[512,512]{1,0:T(8,128)}), f32[64,512]{1,0:T(8,128)}) %reduce-scatter.21.cloned.1.call-update) | async-done | bytes 131088 | tf_op jit(solution)/shard_map/reduce_scatter | solution.py:61
  641.1 64.8 %reduce-scatter.19.cloned.1.call-done = f32[128,64]{0,1:T(8,128)} async-done(((f32[128,512]{0,1:T(8,128)}), f32[128,64]{0,1:T(8,128)}) %reduce-scatter.19.cloned.1.call-update) | async-done | bytes 32784 | tf_op jit(solution)/shard_map/reduce_scatter | solution.py:45
  (155 shorter events, 40.1 us)
Async XLA Ops:
  7.2 18.0 %copy-start = (f32[169,4]{0,1:T(4,128)S(1)}, f32[169,4]{0,1:T(4,128)}, u32[]{:S(2)}) copy-start(f32[169,4]{0,1:T(4,128)} %param.37) | copy-start | bytes 8116
  7.2 82.7 %copy-start.30 = (s32[32,49]{1,0:T(8,128)S(1)}, s32[32,49]{1,0:T(8,128)}, u32[]{:S(2)}) copy-start(s32[32,49]{1,0:T(8,128)} %param.39) | copy-start | bytes 18820
  7.2 83.1 %all-gather.5.cloned.1.call-start = ((), (), s32[]{:S(2)}) async-start(), calls=%async_computation.8 | async-start | bytes 2007040 | tf_op jit(solution)/shard_map/all_gather | solution.py:21
  23.7 135.1 %reduce-scatter.9.cloned.1.call-start = ((), (), s32[]{:S(2)}) async-start(), calls=%async_computation.9 | async-start | bytes 4014080 | tf_op jit(solution)/shard_map/reduce_scatter | solution.py:25
  57.9 60.5 %copy-start.26 = (bf16[128,512]{0,1:T(8,128)(2,1)}, bf16[128,512]{0,1:T(8,128)(2,1)S(1)}, u32[]{:S(2)}) copy-start(bf16[128,512]{0,1:T(8,128)(2,1)S(1)} %all_gather.30) | copy-start | bytes 393220
  89.9 2.8 copy-start.20
  90.2 2.5 copy-start.39
  90.3 2.5 copy-start.40
  98.9 12.5 %copy-start.10 = (bf16[32,49,4,32]{1,3,2,0:T(8,128)(2,1)}, bf16[32,49,4,32]{1,3,2,0:T(8,128)(2,1)S(1)}, u32[]{:S(2)}) copy-start(bf16[32,49,4,32]{1,3,2,0:T(8,128)(2,1)S(1)} %copy.76) | copy-start | bytes 1204228
  104.0 8.6 %copy-start.8 = (bf16[32,49,4,32]{1,3,2,0:T(8,128)(2,1)}, bf16[32,49,4,32]{1,3,2,0:T(8,128)(2,1)S(1)}, u32[]{:S(2)}) copy-start(bf16[32,49,4,32]{1,3,2,0:T(8,128)(2,1)S(1)} %copy.77) | copy-start | bytes 1204228
  112.6 3.1 copy-start.2
  118.4 2.4 copy-start.18
  118.4 40.5 %copy-start.6 = (bf16[1568,128]{1,0:T(8,128)(2,1)S(1)}, bf16[1568,128]{1,0:T(8,128)(2,1)}, u32[]{:S(2)}) copy-start(bf16[1568,128]{1,0:T(8,128)(2,1)} %param.21) | copy-start | bytes 1204228
  118.4 40.5 %copy-start.41 = (f32[128]{0:T(128)S(1)}, f32[128]{0:T(128)}, u32[]{:S(2)}) copy-start(f32[128]{0:T(128)} %param.30) | copy-start | bytes 1540
  120.7 50.2 %copy-start.33 = (f32[128]{0:T(128)S(1)}, f32[128]{0:T(128)}, u32[]{:S(2)}) copy-start(f32[128]{0:T(128)} %param.31) | copy-start | bytes 1540
  120.7 50.2 %copy-start.42 = (f32[128]{0:T(128)S(1)}, f32[128]{0:T(128)}, u32[]{:S(2)}) copy-start(f32[128]{0:T(128)} %param.32) | copy-start | bytes 1540
  120.7 52.2 %copy-start.25 = (bf16[1568,128]{1,0:T(8,128)(2,1)S(1)}, bf16[1568,128]{1,0:T(8,128)(2,1)}, u32[]{:S(2)}) copy-start(bf16[1568,128]{1,0:T(8,128)(2,1)} %param.41) | copy-start | bytes 1204228
  120.7 53.3 %copy-start.28 = (bf16[64,512]{1,0:T(8,128)(2,1)S(1)}, bf16[64,512]{1,0:T(8,128)(2,1)}, u32[]{:S(2)}) copy-start(bf16[64,512]{1,0:T(8,128)(2,1)} %param.33) | copy-start | bytes 196612
  120.8 84.9 %copy-start.29 = (bf16[512,64]{0,1:T(8,128)(2,1)S(1)}, bf16[512,64]{0,1:T(8,128)(2,1)}, u32[]{:S(2)}) copy-start(bf16[512,64]{0,1:T(8,128)(2,1)} %param.35) | copy-start | bytes 196612
  120.8 118.1 %copy-start.43 = (f32[512]{0:T(512)S(1)}, f32[512]{0:T(512)}, u32[]{:S(2)}) copy-start(f32[512]{0:T(512)} %param.34) | copy-start | bytes 6148
  120.8 118.0 %all-gather.7.cloned.1.call-start = ((), (), s32[]{:S(2)}) async-start(), calls=%async_computation.10 | async-start | bytes 2007040 | tf_op jit(solution)/shard_map/all_gather | solution.py:21
  172.2 70.8 %all-gather.9.cloned.1.call-start = ((), (), s32[]{:S(2)}) async-start(), calls=%async_computation.12 | async-start | bytes 2007040 | tf_op jit(solution)/shard_map/all_gather | solution.py:21
  174.0 122.3 %reduce-scatter.13.cloned.1.call-start = ((), (), s32[]{:S(2)}) async-start(), calls=%async_computation.13 | async-start | bytes 4014080 | tf_op jit(solution)/shard_map/reduce_scatter | solution.py:25
  205.6 37.4 %copy-start.22 = (bf16[512,512]{1,0:T(8,128)(2,1)}, bf16[512,512]{1,0:T(8,128)(2,1)S(1)}, u32[]{:S(2)}) copy-start(bf16[512,512]{1,0:T(8,128)(2,1)S(1)} %all_gather.32) | copy-start | bytes 1572868
  243.0 11.7 %copy-start.23 = (bf16[512,512]{1,0:T(8,128)(2,1)S(1)}, bf16[512,512]{1,0:T(8,128)(2,1)}, u32[]{:S(2)}) copy-start(bf16[512,512]{1,0:T(8,128)(2,1)} %copy-done.22) | copy-start | bytes 1572868
  257.5 79.4 %reduce-scatter.11.cloned.1.call-start = ((), (), s32[]{:S(2)}) async-start(), calls=%async_computation.11 | async-start | bytes 4014080 | tf_op jit(solution)/shard_map/reduce_scatter | solution.py:25
  257.5 4.9 copy-start.21
  265.3 98.3 %all-gather.11.cloned.1.call-start = ((), (), s32[]{:S(2)}) async-start(), calls=%async_computation.14 | async-start | bytes 2007040 | tf_op jit(solution)/shard_map/all_gather | solution.py:21
  343.4 122.7 %reduce-scatter.17.cloned.1.call-start = ((), (), s32[]{:S(2)}) async-start(), calls=%async_computation.16 | async-start | bytes 884736 | tf_op jit(solution)/shard_map/reduce_scatter | solution.py:61
  371.4 3.8 copy-start.3
  371.4 3.8 copy-start.12
  371.4 4.1 copy-start.14
  386.4 12.8 %copy-start.17 = (bf16[1568,512]{1,0:T(8,128)(2,1)S(1)}, bf16[1568,512]{1,0:T(8,128)(2,1)}, u32[]{:S(2)}) copy-start(bf16[1568,512]{1,0:T(8,128)(2,1)} %all-gather.5.cloned.1.call-done) | copy-start | bytes 4816900
  402.6 103.2 %reduce-scatter.15.cloned.1.call-start = ((), (), s32[]{:S(2)}) async-start(), calls=%async_computation.15 | async-start | bytes 4014080 | tf_op jit(solution)/shard_map/reduce_scatter | solution.py:25
  407.8 166.2 %reduce-scatter.23.cloned.1.call-start = ((), (), s32[]{:S(2)}) async-start(), calls=%async_computation.19 | async-start | bytes 1179648 | tf_op jit(solution)/shard_map/reduce_scatter | solution.py:45
  412.8 3.9 copy-start.27
  412.8 4.3 copy-start.32
  412.8 5.2 copy-start.19
  412.8 228.3 %reduce-scatter.21.cloned.1.call-start = ((), (), s32[]{:S(2)}) async-start(), calls=%async_computation.18 | async-start | bytes 1179648 | tf_op jit(solution)/shard_map/reduce_scatter | solution.py:61
  416.5 89.3 %copy-start.7 = (bf16[1568,128]{1,0:T(8,128)(2,1)S(1)}, bf16[1568,128]{1,0:T(8,128)(2,1)}, u32[]{:S(2)}) copy-start(bf16[1568,128]{1,0:T(8,128)(2,1)} %param.21) | copy-start | bytes 1204228
  416.5 89.3 %copy-start.34 = (f32[128]{0:T(128)S(1)}, f32[128]{0:T(128)}, u32[]{:S(2)}) copy-start(f32[128]{0:T(128)} %param.22) | copy-start | bytes 1540
  416.5 101.6 %copy-start.35 = (f32[128]{0:T(128)S(1)}, f32[128]{0:T(128)}, u32[]{:S(2)}) copy-start(f32[128]{0:T(128)} %get-tuple-element.24) | copy-start | bytes 1540
  416.5 101.6 %copy-start.36 = (f32[128]{0:T(128)S(1)}, f32[128]{0:T(128)}, u32[]{:S(2)}) copy-start(f32[128]{0:T(128)} %get-tuple-element.53) | copy-start | bytes 1540
  416.5 101.6 %copy-start.37 = (f32[128]{0:T(128)S(1)}, f32[128]{0:T(128)}, u32[]{:S(2)}) copy-start(f32[128]{0:T(128)} %get-tuple-element.59) | copy-start | bytes 1540
  416.5 101.6 %copy-start.38 = (f32[512]{0:T(512)S(1)}, f32[512]{0:T(512)}, u32[]{:S(2)}) copy-start(f32[512]{0:T(512)} %get-tuple-element.50) | copy-start | bytes 6148
  416.5 138.9 %copy-start.16 = (f32[1568,128]{1,0:T(8,128)S(1)}, f32[1568,128]{1,0:T(8,128)}, u32[]{:S(2)}) copy-start(f32[1568,128]{1,0:T(8,128)} %copy-done.15) | copy-start | bytes 2408452
  416.6 289.3 %reduce-scatter.19.cloned.1.call-start = ((), (), s32[]{:S(2)}) async-start(), calls=%async_computation.17 | async-start | bytes 294912 | tf_op jit(solution)/shard_map/reduce_scatter | solution.py:45
  417.1 288.8 %copy-start.1 = (f32[169,4]{0,1:T(4,128)S(1)}, f32[169,4]{0,1:T(4,128)}, u32[]{:S(2)}) copy-start(f32[169,4]{0,1:T(4,128)} %param.37) | copy-start | bytes 8116
  (8 other events, 12.3 us)
Sparse Core Ops, SparseCore 0:
  23.8 20.2 all-gather.4
  120.8 37.9 reduce-scatter.8
  172.3 20.6 all-gather.6
  194.4 19.9 all-gather.8
  257.6 38.6 reduce-scatter.12
  298.7 38.1 reduce-scatter.10
  343.5 19.9 all-gather.10
  402.8 63.2 reduce-scatter.16
  468.6 37.1 reduce-scatter.14
  509.7 64.2 reduce-scatter.22
  578.0 63.0 reduce-scatter.20
  644.8 61.0 reduce-scatter.18
where the time goes:
time: 717 us; the launch traced here: 713 us
  waiting for transfers between devices  346 us (48%)
  blocking collectives  209 us (29%)
  matrix products  60.3 us (8%)
  local copies, waits for them, and re-layouts  49 us (7%)
  other arithmetic  33 us (5%)
  between operations  15.6 us (2%)
    reduce_scatter x4, waiting for transfers between devices, share(): return lax.psum_scatter(value, 'ta', scatter_dimension=1, tiled=True)  133 us
    reduce_scatter x2, waiting for transfers between devices, input_grads(): lax.psum_scatter(cross(acts_full, grads_low), 'wa', scatter_dimension=0,...  112 us
    reduce_scatter x2, waiting for transfers between devices, output_grads(): return lax.psum_scatter(value, 'wa', scatter_dimension=1, tiled=True)  80.4 us
    all_gather x2, blocking collectives, gather_outputs(): return lax.all_gather(weight, 'wa', axis=1, tiled=True)  64.3 us
    all_gather x2, blocking collectives, gather_inputs(): return lax.all_gather(weight, 'wa', axis=0, tiled=True)  62.8 us
    psum x4, blocking collectives, row_sums(): return lax.psum((jnp.sum(first, axis=1), jnp.sum(second, axis=1)), 'ta')  44.6 us
    psum x1, blocking collectives, per_device(): lax.psum((gain_one_part, shift_one_part, scale * jnp.sum(grad_q.astype(jn...  37.3 us
    dot_general x5, matrix products, against(): lax.dot_general(left, right, (((1,), (1,)), ((), ())), preferred_element_...  21.5 us
  transfers between devices with their start and end apart: 12, of which 9 were waited for; matrix products, arithmetic and copies ran while one was open for 6% of the time, Pallas kernels for 0%

commit v1 on v0

v1 whole, which is shorter than its diff:
```python
import functools

import jax
import jax.numpy as jnp
from jax import lax
from jax.experimental import pallas as pl
from jax.experimental.pallas import tpu as pltpu
from jax.sharding import PartitionSpec as P

C = 512
HDIM = 32
WT = 49
PAD = 64
TABLE = 169
TPAD = 256
NCH = 6
CW = 256
LANES = 128
SROWS = 24
SCALE = HDIM ** (-0.5)
EPS = 1e-05
F32 = jnp.float32
BF16 = jnp.bfloat16
MESH = pl.DeviceIdType.MESH
ANY = pl.BlockSpec(memory_space=pl.ANY)
VM = pl.BlockSpec(memory_space=pltpu.VMEM)


def place():
    a, t = lax.axis_index("wa"), lax.axis_index("ta")
    return a, t, lax.rem(a, 2), lax.div(a, 2), lax.rem(t, 2), lax.div(t, 2)


def greet(peers):
    barrier = pltpu.get_barrier_semaphore()
    for peer in peers:
        pl.semaphore_signal(barrier, inc=1, device_id=peer, device_id_type=MESH)
    pl.semaphore_wait(barrier, len(peers))


def remote(src, dst, send, recv, peer):
    copy = pltpu.make_async_remote_copy(
        src_ref=src, dst_ref=dst, send_sem=send, recv_sem=recv, device_id=peer, device_id_type=MESH
    )
    copy.start()
    return copy


def bring(nt, nz, tok, cot, wp, vec, rb, xg, cg, gw, vg, rg, b0, b1, b2, b3, b4, *sems):
    loc, ta_s, ta_r, z_s, z_r, p_s, p_r, q_s, q_r, k_s, k_r = sems
    a, t, x, z, c, y = place()
    xp = (z * 2 + (1 - x), t)
    yp = (a, (1 - y) * 2 + c)
    cp = (a, y * 2 + (1 - c))
    ty = (1 - y) * 2 + c
    zs = [(lax.rem(z + d, nz) * 2 + x, t) for d in range(1, nz)]
    ts = [(a, lax.rem(t + d, nt)) for d in range(1, nt)]
    own = [(tok.at[t], b0, xg.at[t]), (cot.at[t], b1, cg.at[t]), (wp, b2, gw.at[:, t, z, x])]
    own += [(vec, b3, vg.at[t]), (rb, b4, rg.at[t])]
    ins = [pltpu.make_async_copy(s, m, loc.at[i]) for i, (s, m, _) in enumerate(own)]
    for copy in ins:
        copy.start()
    greet(zs + ts + [xp])
    waits = []
    for ch in range(NCH):
        for d, peer in enumerate(zs):
            waits.append(
                remote(wp.at[ch], gw.at[ch, t, z, x], z_s.at[ch, d], z_r.at[ch, d], peer)
            )
    for d, peer in enumerate(ts):
        other = peer[1]
        for i, (s, g) in enumerate(((tok.at[other], xg), (cot.at[other], cg), (vec, vg), (rb, rg))):
            waits.append(remote(s, g.at[t], ta_s.at[i, d], ta_r.at[i, d], peer))
    outs = []
    for i, (_, m, o) in enumerate(own):
        ins[i].wait()
        outs.append(pltpu.make_async_copy(m, o, loc.at[i]))
        outs[-1].start()
    outs[2].wait()

    def got(ref, sem):
        pltpu.make_async_copy(ref, ref, sem).wait()

    zw = 0
    for ch in range(NCH):
        for d in range(1, nz):
            waits[zw].wait_recv()
            zw += 1
        if ch % 2 == 0:
            ref = gw.at[ch, t, :, x]
            waits.append(remote(ref, ref, p_s.at[ch], p_r.at[ch], xp))
        else:
            ref = gw.at[ch, t, :, x]
            waits.append(remote(ref, ref, p_s.at[ch], p_r.at[ch], yp))
    first = waits[-NCH:]
    second = []
    for ch in range(NCH):
        first[ch].wait_recv()
        if ch % 2 == 0:
            ref = gw.at[ch, t]
            second.append((remote(ref, ref, q_s.at[ch, 0], q_r.at[ch, 0], yp),))
            waits.append(remote(ref, ref, k_s.at[ch, 0], k_r.at[ch, 0], cp))
        else:
            pair = []
            for i, tt in enumerate((t, ty)):
                ref = gw.at[ch, tt, :, x]
                pair.append(remote(ref, ref, q_s.at[ch, i], q_r.at[ch, i], xp))
            second.append(tuple(pair))
    for ch in range(NCH):
        for copy in second[ch]:
            copy.wait_recv()
        if ch % 2 == 1:
            ref = gw.at[ch, t]
            waits.append(remote(ref, ref, k_s.at[ch, 0], k_r.at[ch, 0], cp))
        ref = gw.at[ch, ty]
        waits.append(remote(ref, ref, k_s.at[ch, 1], k_r.at[ch, 1], cp))
    nzc = NCH * (nz - 1)
    for copy in waits[nzc : nzc + 4 * (nt - 1)]:
        copy.wait_recv()
    for copy in waits[nzc + 4 * (nt - 1) + NCH :]:
        copy.wait_recv()
    for copy in waits:
        copy.wait_send()
    for group in second:
        for copy in group:
            copy.wait_send()
    for i, copy in enumerate(outs):
        if i != 2:
            copy.wait()


def bring_call(nt, nz, tok, cot, wp, vec, rb):
    rows = tok.shape[1]
    deep = wp.shape[1]
    sem = pltpu.SemaphoreType.DMA
    return pl.pallas_call(
        functools.partial(bring, nt, nz),
        name="bring",
        out_shape=(
            jax.ShapeDtypeStruct((nt, rows, LANES), BF16),
            jax.ShapeDtypeStruct((nt, rows, LANES), BF16),
            jax.ShapeDtypeStruct((NCH, nt, nz, 2, deep, CW), BF16),
            jax.ShapeDtypeStruct((nt,) + vec.shape, F32),
            jax.ShapeDtypeStruct((nt,) + rb.shape, F32),
        ),
        in_specs=[ANY] * 5,
        out_specs=(ANY,) * 5,
        scratch_shapes=[
            pltpu.VMEM(tok.shape[1:], BF16),
            pltpu.VMEM(tok.shape[1:], BF16),
            pltpu.VMEM(wp.shape, BF16),
            pltpu.VMEM(vec.shape, F32),
            pltpu.VMEM(rb.shape, F32),
            sem((5,)),
            sem((4, nt - 1)),
            sem((4, nt - 1)),
            sem((NCH, nz - 1)),
            sem((NCH, nz - 1)),
            sem((NCH,)),
            sem((NCH,)),
            sem((NCH, 2)),
            sem((NCH, 2)),
            sem((NCH, 2)),
            sem((NCH, 2)),
        ],
        compiler_params=pltpu.CompilerParams(collective_id=0, has_side_effects=True),
    )(tok, cot, wp, vec, rb)


def nn(left, right):
    return jnp.dot(left, right, preferred_element_type=F32)


def nt_dot(left, right):
    return lax.dot_general(left, right, (((1,), (1,)), ((), ())), preferred_element_type=F32)


def tn_dot(left, right):
    return lax.dot_general(left, right, (((0,), (0,)), ((), ())), preferred_element_type=F32)


def norm(value):
    mean = jnp.mean(value, axis=1, keepdims=True)
    spread = jnp.mean(value * value, axis=1, keepdims=True) - mean * mean
    rstd = lax.rsqrt(spread + EPS)
    return (value - mean) * rstd, rstd


def norm_back(scaled, normed, rstd):
    first = jnp.mean(scaled, axis=1, keepdims=True)
    second = jnp.mean(scaled * normed, axis=1, keepdims=True)
    return rstd * (scaled - first - normed * second)


def gelu_pair(u):
    cdf = 0.5 + 0.5 * lax.erf(u * (0.5**0.5))
    pdf = jnp.exp(-0.5 * u * u) * ((2.0 * jnp.pi) ** -0.5)
    return u * cdf, cdf + u * pdf


def rowsum(value):
    return jnp.sum(value, axis=0, keepdims=True)


def work(
    nt, slots, live, x_in, c_in, gw, vec, rb, mask,
    y_out, g_out, dw, small, pairs,
    xs, xp, gy, h1, h1t, h2t, gyt, qs, kvs, probs, att, acc, acc2, n1, r1, n2, r2, low, gkv, gq,
):
    heads = LANES // HDIM
    rows = slots * PAD
    half = 2 * PAD
    nhalf = rows // half

    def wide(i):
        return jnp.concatenate([vec[t, i : i + 1, :] for t in range(nt)], axis=1)

    def put_small(i, value):
        for t in range(nt):
            small[t, i : i + 1, :] = value[:, t * LANES : (t + 1) * LANES]

    def spread(source, target):
        for t in range(nt):
            xs[:, t * LANES : (t + 1) * LANES] = source[t].astype(F32)
        zero = jnp.zeros((PAD - WT, C), F32)
        for w in range(slots):
            target[w * PAD : w * PAD + WT, :] = xs[w * WT : (w + 1) * WT, :]
            target[w * PAD + WT : (w + 1) * PAD, :] = zero

    def gather(source, target):
        for w in range(slots):
            xs[w * WT : (w + 1) * WT, :] = source[w * PAD : w * PAD + WT, :]
        for t in range(nt):
            target[t] = xs[:, t * LANES : (t + 1) * LANES].astype(BF16)

    small[...] = jnp.zeros_like(small)
    pairs[...] = jnp.zeros_like(pairs)
    spread(x_in, xp)
    spread(c_in, gy)
    gain1, shift1 = wide(0), wide(1)
    n_live = live[0]

    def each(body, init=0):
        def step(i, carry):
            return body(i, pl.ds(pl.multiple_of(i * half, half), half), carry)

        return lax.fori_loop(0, nhalf, step, init)

    def start(i, at, carry):
        normed, rstd = norm(xp[at, :])
        n1[at, :] = normed
        r1[at, :] = rstd
        h = normed * gain1 + shift1
        h1[at, :] = h.astype(BF16)
        h1t[:, at] = h.T.astype(BF16)
        slot = lax.div(i * half + lax.broadcasted_iota(jnp.int32, (half, 1), 0), PAD)
        g = jnp.where(slot < n_live, gy[at, :], 0.0)
        gy[at, :] = g
        gyt[:, at] = g.T.astype(BF16)
        return carry

    each(start)
    lane_head = lax.broadcasted_iota(jnp.int32, (PAD, LANES), 1) // HDIM
    ones = [(lane_head == h).astype(F32).astype(BF16) for h in range(heads)]

    def stack(value):
        return jnp.concatenate([value * ones[h] for h in range(heads)], axis=0)

    def pick(value):
        out = value[0:PAD]
        for h in range(1, heads):
            out = jnp.where(lane_head == h, value[h * PAD : (h + 1) * PAD], out)
        return out

    acc[...] = jnp.zeros_like(acc)

    def attend(t, carry):
        q = (nn(h1[...], gw[0, t][:, :LANES]) + vec[t, 2:3, :]) * SCALE
        qs[t] = q.astype(BF16)
        kv = nn(h1[...], gw[1, t])
        kvs[t, :, :LANES] = kv[:, :LANES].astype(BF16)
        kvs[t, :, LANES:] = (kv[:, LANES:] + vec[t, 3:4, :]).astype(BF16)

        def window(w, carry):
            at = pl.ds(pl.multiple_of(w * PAD, PAD), PAD)
            s = nt_dot(kvs[t, at, :LANES], stack(qs[t, at, :])) + rb[t] + mask[w]
            e = jnp.exp(s - jnp.max(s, axis=0, keepdims=True))
            p = e / rowsum(e)
            probs[t, w] = p
            att[t, at, :] = pick(tn_dot(p.astype(BF16), kvs[t, at, LANES:])).astype(BF16)
            return carry

        lax.fori_loop(0, slots, window, 0, unroll=2)
        acc[...] += nt_dot(att[t], gw[0, t][:, LANES:])
        return carry

    lax.fori_loop(0, nt, attend, 0)
    b_out, gain2, shift2 = wide(4), wide(5), wide(6)

    def middle(i, at, carry):
        x1 = xp[at, :] + acc[at, :] + b_out
        xp[at, :] = x1
        normed, rstd = norm(x1)
        n2[at, :] = normed
        r2[at, :] = rstd
        h = normed * gain2 + shift2
        low[at, :] = h.astype(BF16)
        h2t[:, at] = h.T.astype(BF16)
        return carry

    each(middle)
    acc[...] = jnp.zeros_like(acc)
    acc2[...] = jnp.zeros_like(acc2)
    gy_low = gkv
    gy_low[...] = gy[...].astype(BF16)

    def mlp(k, carry):
        t, s = lax.div(k, 2), lax.rem(k, 2)
        up, down = gw.at[2 + s, t], gw.at[4 + s, t]
        bias = vec[t, pl.ds(8 + 2 * s, 2), :]
        bias = jnp.concatenate([bias[0:1], bias[1:2]], axis=1)
        hidden = nn(low[...], up[...]) + bias
        act, slope = gelu_pair(hidden)
        act_low = act.astype(BF16)
        acc[...] += nt_dot(act_low, down[...])
        dw[4 + s, t] = nn(gyt[...], act_low).astype(BF16)
        grad = nn(gy_low[...], down[...]) * slope
        total = rowsum(grad)
        small[t, pl.ds(8 + 2 * s, 1), :] = total[:, :LANES]
        small[t, pl.ds(9 + 2 * s, 1), :] = total[:, LANES:]
        grad_low = grad.astype(BF16)
        dw[2 + s, t] = nn(h2t[...], grad_low).astype(BF16)
        acc2[...] += nt_dot(grad_low, up[...])
        return carry

    lax.fori_loop(0, 2 * nt, mlp, 0)
    b_down = wide(7)
    zero_row = jnp.zeros((1, C), F32)

    def turn(i, at, carry):
        slot = lax.div(i * half + lax.broadcasted_iota(jnp.int32, (half, 1), 0), PAD)
        xp[at, :] = jnp.where(slot < n_live, xp[at, :] + acc[at, :] + b_down, 0.0)
        e, normed, g = acc2[at, :], n2[at, :], gy[at, :]
        gx = norm_back(e * gain2, normed, r2[at, :]) + g
        gy[at, :] = gx
        low[at, :] = gx.astype(BF16)
        h2t[:, at] = gx.T.astype(BF16)
        sums = (rowsum(e * normed), rowsum(e), rowsum(gx), rowsum(g))
        return tuple(a + b for a, b in zip(carry, sums))

    sums = each(turn, (zero_row,) * 4)
    put_small(5, sums[0])
    put_small(6, sums[1])
    put_small(4, sums[2])
    put_small(7, sums[3])
    gather(xp, y_out)
    acc[...] = jnp.zeros_like(acc)

    def back(t, carry):
        gatt = gq
        dw[0, t, :, LANES:] = nn(h2t[...], att[t]).astype(BF16)
        gatt[...] = nn(low[...], gw[0, t][:, LANES:]).astype(BF16)

        def window(w, carry):
            at = pl.ds(pl.multiple_of(w * PAD, PAD), PAD)
            q4, g4 = stack(qs[t, at, :]), stack(gatt[at, :])
            p = probs[t, w]
            dp = nt_dot(kvs[t, at, LANES:], g4)
            ds = p * (dp - rowsum(p * dp))
            ds_low = ds.astype(BF16)
            pairs[t] += ds_low.astype(F32)
            gkv[at, :LANES] = nn(ds_low, q4).astype(BF16)
            gkv[at, LANES:CW] = nn(p.astype(BF16), g4).astype(BF16)
            gatt[at, :] = pick(tn_dot(ds_low, kvs[t, at, :LANES])).astype(BF16)
            return carry

        lax.fori_loop(0, slots, window, 0, unroll=2)
        gk_gv = gkv[:, :CW]
        dw[0, t, :, :LANES] = (nn(h1t[...], gatt[...]) * SCALE).astype(BF16)
        dw[1, t] = nn(h1t[...], gk_gv).astype(BF16)
        small[t, 2:3, :] = rowsum(gatt[...].astype(F32)) * SCALE
        small[t, 3:4, :] = rowsum(gkv[:, LANES:CW].astype(F32))
        acc[...] += nt_dot(gatt[...], gw[0, t][:, :LANES]) * SCALE + nt_dot(gk_gv, gw[1, t])
        return carry

    lax.fori_loop(0, nt, back, 0)

    def finish(i, at, carry):
        e, normed = acc[at, :], n1[at, :]
        xp[at, :] = norm_back(e * gain1, normed, r1[at, :]) + gy[at, :]
        sums = (rowsum(e * normed), rowsum(e))
        return tuple(a + b for a, b in zip(carry, sums))

    sums = each(finish, (zero_row,) * 2)
    put_small(0, sums[0])
    put_small(1, sums[1])
    gather(xp, g_out)


def work_call(nt, slots, live, xg, cg, gw, vg, rg, mask):
    rows, real = slots * PAD, xg.shape[1]
    heads4 = rg.shape[2]
    return pl.pallas_call(
        functools.partial(work, nt, slots),
        name="work",
        out_shape=(
            jax.ShapeDtypeStruct((nt, real, LANES), BF16),
            jax.ShapeDtypeStruct((nt, real, LANES), BF16),
            jax.ShapeDtypeStruct((NCH, nt, C, CW), BF16),
            jax.ShapeDtypeStruct((nt, SROWS, LANES), F32),
            jax.ShapeDtypeStruct((nt, PAD, heads4), F32),
        ),
        in_specs=[pl.BlockSpec(memory_space=pltpu.SMEM)] + [VM] * 6,
        out_specs=(VM,) * 5,
        scratch_shapes=[
            pltpu.VMEM((real, C), F32),
            pltpu.VMEM((rows, C), F32),
            pltpu.VMEM((rows, C), F32),
            pltpu.VMEM((rows, C), BF16),
            pltpu.VMEM((C, rows), BF16),
            pltpu.VMEM((C, rows), BF16),
            pltpu.VMEM((C, rows), BF16),
            pltpu.VMEM((nt, rows, LANES), BF16),
            pltpu.VMEM((nt, rows, CW), BF16),
            pltpu.VMEM((nt, slots, PAD, heads4), F32),
            pltpu.VMEM((nt, rows, LANES), BF16),
            pltpu.VMEM((rows, C), F32),
            pltpu.VMEM((rows, C), F32),
            pltpu.VMEM((rows, C), F32),
            pltpu.VMEM((rows, 1), F32),
            pltpu.VMEM((rows, C), F32),
            pltpu.VMEM((rows, 1), F32),
            pltpu.VMEM((rows, C), BF16),
            pltpu.VMEM((rows, C), BF16),
            pltpu.VMEM((rows, LANES), BF16),
        ],
        compiler_params=pltpu.CompilerParams(vmem_limit_bytes=56 * 2**20),
    )(live, xg, cg, gw, vg, rg, mask)


def send_back(nt, nz, nbits, y_in, g_in, dw, small, y_out, g_out, fin, tot, b0, b1, *rest):
    (dv, rc, r1a, r2a, r3, rz, sb, sc_r, sy_r, sx_r), sems = rest[:10], rest[10:]
    loc, ta_s, ta_r, k_s, k_r, p_s, p_r, q_s, q_r, z_s, z_r, s_s, s_r = sems
    a, t, x, z, c, y = place()
    xp = (z * 2 + (1 - x), t)
    yp = (a, (1 - y) * 2 + c)
    cp = (a, y * 2 + (1 - c))
    zs = [(lax.rem(z + d, nz) * 2 + x, t) for d in range(1, nz)]
    ts = [(a, lax.rem(t + d, nt)) for d in range(1, nt)]
    flips = []
    for b in range(nbits):
        bit = 2**b
        flips.append((a + bit - 2 * bit * lax.rem(lax.div(a, bit), 2), t))
    ins = [pltpu.make_async_copy(y_in.at[t], b0, loc.at[0])]
    ins.append(pltpu.make_async_copy(g_in.at[t], b1, loc.at[1]))
    for i in range(2):
        ins.append(pltpu.make_async_copy(dw.at[:, 2 * i + c], dv.at[:, i], loc.at[2 + i]))
    for copy in ins:
        copy.start()
    greet(zs + ts + flips)
    sends = []
    core = []
    for ch in range(NCH):
        for i in range(2):
            core.append(
                remote(dw.at[ch, 2 * i + 1 - c], rc.at[ch, i], k_s.at[ch, i], k_r.at[ch, i], cp)
            )
    for i in range(2):
        core.append(remote(small.at[2 * i + 1 - c], sc_r.at[i], s_s.at[i], s_r.at[i], cp))
    back = []
    for d, peer in enumerate(ts):
        for i, (src, dst) in enumerate(((y_in, y_out), (g_in, g_out))):
            back.append(remote(src.at[peer[1]], dst.at[t], ta_s.at[i, d], ta_r.at[i, d], peer))
    outs = []
    for i, (m, o) in enumerate(((b0, y_out), (b1, g_out))):
        ins[i].wait()
        outs.append(pltpu.make_async_copy(m, o.at[t], loc.at[i]))
        outs[-1].start()
    ins[2].wait()
    ins[3].wait()

    def add(left, right):
        return (left.astype(F32) + right.astype(F32)).astype(BF16)

    for i in range(2):
        core[2 * NCH + i].wait_recv()
    own_small = pltpu.make_async_copy(small, sb, loc.at[2])
    own_small.start()
    own_small.wait()
    sx_r[0] = sb[1 - y + 1 - y + c] + sc_r[1 - y]
    sx_r[1] = sb[y + y + c] + sc_r[y]
    sends.append(remote(sx_r.at[0], sy_r.at[0], s_s.at[2], s_r.at[2], yp))
    small_copy = sends[-1]
    first = []
    for ch in range(NCH):
        core[2 * ch].wait_recv()
        core[2 * ch + 1].wait_recv()
        for i in range(2):
            dv[ch, i] = add(dv[ch, i], rc[ch, i])
        if ch % 2 == 0:
            h = ch // 2
            first.append(
                (remote(dv.at[ch, 1 - y], r1a.at[h], p_s.at[ch, 0], p_r.at[ch, 0], yp),)
            )
        else:
            h = ch // 2
            first.append(
                tuple(
                    remote(
                        dv.at[ch, i, :, 1 - x], r2a.at[h, i], p_s.at[ch, i], p_r.at[ch, i], xp
                    )
                    for i in range(2)
                )
            )
    small_copy.wait_recv()
    sx_r[2] = sx_r[1] + sy_r[0]
    second = []
    for b in range(nbits):
        sends.append(
            remote(sx_r.at[2 + b], sy_r.at[1 + b], s_s.at[3 + b], s_r.at[3 + b], flips[b])
        )
        if b == 0:
            for ch in range(NCH):
                h = ch // 2
                for copy in first[ch]:
                    copy.wait_recv()
                if ch % 2 == 0:
                    dv[ch, y] = add(dv[ch, y], r1a[h])
                    second.append(
                        remote(
                            dv.at[ch, y, :, 1 - x], r3.at[ch], q_s.at[ch], q_r.at[ch], xp
                        )
                    )
                else:
                    for i in range(2):
                        dv[ch, i, :, x] = add(dv[ch, i, :, x], r2a[h, i])
                    second.append(
                        remote(
                            dv.at[ch, 1 - y, :, x], r3.at[ch], q_s.at[ch], q_r.at[ch], yp
                        )
                    )
        sends[-1].wait_recv()
        sx_r[3 + b] = sx_r[2 + b] + sy_r[1 + b]
    last = []
    for ch in range(NCH):
        second[ch].wait_recv()
        dv[ch, y, :, x] = add(dv[ch, y, :, x], r3[ch])
        for d, peer in enumerate(zs):
            last.append(
                remote(
                    dv.at[ch, y, lax.rem(z + d + 1, nz), x],
                    rz.at[ch, d],
                    z_s.at[ch, d],
                    z_r.at[ch, d],
                    peer,
                )
            )
    for ch in range(NCH):
        for d in range(nz - 1):
            last[ch * (nz - 1) + d].wait_recv()
        value = dv[ch, y, z, x].astype(F32)
        for d in range(nz - 1):
            value = value + rz[ch, d].astype(F32)
        fin[ch] = value
    tot[...] = sx_r[2 + nbits]
    for copy in back:
        copy.wait_recv()
    for copy in core + back + sends + second + last:
        copy.wait_send()
    for group in first:
        for copy in group:
            copy.wait_send()
    for copy in outs:
        copy.wait()


def back_call(nt, nz, y_in, g_in, dw, small):
    rows, deep = y_in.shape[1], dw.shape[4]
    nbits = (2 * nz - 1).bit_length()
    sem = pltpu.SemaphoreType.DMA
    return pl.pallas_call(
        functools.partial(send_back, nt, nz, nbits),
        name="send_back",
        out_shape=(
            jax.ShapeDtypeStruct((nt, rows, LANES), BF16),
            jax.ShapeDtypeStruct((nt, rows, LANES), BF16),
            jax.ShapeDtypeStruct((NCH, deep, CW), F32),
            jax.ShapeDtypeStruct(small.shape[1:], F32),
        ),
        in_specs=[ANY] * 4,
        out_specs=(ANY, ANY, VM, VM),
        scratch_shapes=[
            pltpu.VMEM((rows, LANES), BF16),
            pltpu.VMEM((rows, LANES), BF16),
            pltpu.VMEM((NCH, 2, nz, 2, deep, CW), BF16),
            pltpu.VMEM((NCH, 2, nz, 2, deep, CW), BF16),
            pltpu.VMEM((NCH // 2, nz, 2, deep, CW), BF16),
            pltpu.VMEM((NCH // 2, 2, nz, deep, CW), BF16),
            pltpu.VMEM((NCH, nz, deep, CW), BF16),
            pltpu.VMEM((NCH, nz - 1, deep, CW), BF16),
            pltpu.VMEM(small.shape, F32),
            pltpu.VMEM((2,) + small.shape[1:], F32),
            pltpu.VMEM((1 + nbits,) + small.shape[1:], F32),
            pltpu.VMEM((3 + nbits,) + small.shape[1:], F32),
            sem((4,)),
            sem((2, nt - 1)),
            sem((2, nt - 1)),
            sem((NCH, 2)),
            sem((NCH, 2)),
            sem((NCH, 2)),
            sem((NCH, 2)),
            sem((NCH,)),
            sem((NCH,)),
            sem((NCH, nz - 1)),
            sem((NCH, nz - 1)),
            sem((3 + nbits,)),
            sem((3 + nbits,)),
        ],
        compiler_params=pltpu.CompilerParams(collective_id=1, has_side_effects=True),
    )(y_in, g_in, dw, small)


def per_device(
    nt, na, tokens, gain_one, shift_one, w_query, w_key, w_value, b_query, b_value, w_out, b_out,
    gain_two, shift_two, w_hidden, b_hidden, w_down, b_down, bias_table, rel_index, region,
    win_count, cotangent,
):
    nz = na // 2
    heads = bias_table.shape[1]
    slots = region.shape[0] // nt
    real = slots * WT
    deep = w_query.shape[0]
    t = lax.axis_index("ta")
    tok = tokens.reshape(nt, real, LANES)
    cot = cotangent.reshape(nt, real, LANES)
    wp = jnp.stack(
        [
            jnp.concatenate([w_query, w_out.T], axis=1),
            jnp.concatenate([w_key, w_value], axis=1),
            w_hidden[:, :CW],
            w_hidden[:, CW:],
            w_down[:CW].T,
            w_down[CW:].T,
        ]
    )
    onehot = rel_index.T.reshape(-1)[:, None] == jnp.arange(TPAD, dtype=jnp.int32)[None, :]
    onehot = onehot.astype(F32)
    table = jnp.pad(bias_table, ((0, TPAD - TABLE), (0, 0)))
    flat = lax.dot_general(
        table, onehot, (((0,), (1,)), ((), ())), precision=lax.Precision.HIGHEST,
        preferred_element_type=F32,
    )
    edge = PAD - WT
    rb = jnp.pad(flat.reshape(heads, WT, WT), ((0, 0), (0, edge), (0, edge)))
    rb = rb.transpose(1, 0, 2).reshape(PAD, heads * PAD)
    vec = [gain_one, shift_one, b_query, b_value, b_out, gain_two, shift_two, b_down, b_hidden]
    vec = jnp.pad(jnp.concatenate(vec).reshape(-1, LANES), ((0, SROWS - 12), (0, 0)))
    mine = lax.dynamic_slice_in_dim(region, t * slots, slots, 0)
    mine = jnp.pad(mine, ((0, 0), (0, edge)))
    mask = jnp.where(mine[:, :, None] == mine[:, None, :], 0.0, -100.0).astype(F32)
    keep = jnp.arange(PAD, dtype=jnp.int32)[None, :, None] < WT
    mask = jnp.where(keep, mask, -1e30)
    mask = jnp.tile(mask, (1, 1, heads))
    live = win_count - t * slots
    xg, cg, gw, vg, rg = bring_call(nt, nz, tok, cot, wp, vec, rb)
    gw = gw.reshape(NCH, nt, C, CW)
    y_loc, g_loc, dw, small, pairs = work_call(nt, slots, live, xg, cg, gw, vg, rg, mask)
    pairs = pairs.reshape(nt, PAD, heads, PAD)[:, :WT, :, :WT].transpose(0, 2, 1, 3)
    part = jnp.dot(
        pairs.reshape(nt * heads, WT * WT), onehot, precision=lax.Precision.HIGHEST,
        preferred_element_type=F32,
    )
    part = part.reshape(nt, heads * TPAD // LANES, LANES)
    small = jnp.concatenate([small[:, :12], part, small[:, 20:]], axis=1)
    y_all, g_all, fin, tot = back_call(
        nt, nz, y_loc, g_loc, dw.reshape(NCH, nt, nz, 2, deep, CW), small
    )
    rows = tokens.shape[0]
    y_out = y_all.reshape(rows, LANES).astype(F32)
    grad_tokens = g_all.reshape(rows, LANES).astype(F32)
    return (
        y_out,
        grad_tokens,
        tot[0],
        tot[1],
        fin[0, :, :LANES],
        fin[1, :, :LANES],
        fin[1, :, LANES:],
        tot[2],
        tot[3],
        fin[0, :, LANES:].T,
        tot[4],
        tot[5],
        tot[6],
        jnp.concatenate([fin[2], fin[3]], axis=1),
        tot[8:12].reshape(-1),
        jnp.concatenate([fin[4].T, fin[5].T], axis=0),
        tot[7],
        tot[12:20].reshape(heads, TPAD)[:, :TABLE].T,
    )


def solution(mesh):
    return jax.shard_map(
        functools.partial(per_device, mesh.shape["ta"], mesh.shape["wa"]),
        mesh=mesh,
        in_specs=(
            P("wa", "ta"),
            P("ta"),
            P("ta"),
            P("wa", "ta"),
            P("wa", "ta"),
            P("wa", "ta"),
            P("ta"),
            P("ta"),
            P("ta", "wa"),
            P("ta"),
            P("ta"),
            P("ta"),
            P("wa", "ta"),
            P("ta"),
            P("ta", "wa"),
            P("ta"),
            P(None, "ta"),
            P(),
            P("wa", None),
            P("wa"),
            P("wa", "ta"),
        ),
        out_specs=(
            P("wa", "ta"),
            P("wa", "ta"),
            P("ta"),
            P("ta"),
            P("wa", "ta"),
            P("wa", "ta"),
            P("wa", "ta"),
            P("ta"),
            P("ta"),
            P("ta", "wa"),
            P("ta"),
            P("ta"),
            P("ta"),
            P("wa", "ta"),
            P("ta"),
            P("ta", "wa"),
            P("ta"),
            P(None, "ta"),
        ),
        check_vma=False,
    )
```

time: 717 us -> 190 us (0.26)
  waiting for transfers between devices: 346 us -> 0 us
  blocking collectives: 209 us -> 0 us
  Pallas kernels: 0 us -> 156 us
  matrix products: 60.3 us -> 2.79 us
  other arithmetic: 33 us -> 5.96 us
  local copies, waits for them, and re-layouts: 49 us -> 22.6 us
  between operations: 15.6 us -> 1.45 us
    reduce_scatter x8 -> x0, waiting for transfers between devices: 325 us -> none  [the longest x4 133 us: share(): return lax.psum_scatter(value, 'ta', scatter_dimension=1, tiled=True)]
    pallas_call x0 -> x3, Pallas kernels: none -> 156 us  [the longest x1 55 us: back_call(): pl.pallas_call(functools.partial(send_back, nt, nz, nbits), name='send_ba...]
    all_gather x4 -> x0, blocking collectives: 127 us -> none  [the longest x2 64.3 us: gather_outputs(): return lax.all_gather(weight, 'wa', axis=1, tiled=True)]
    psum x5 -> x0, blocking collectives: 81.9 us -> none  [the longest x4 44.6 us: row_sums(): return lax.psum((jnp.sum(first, axis=1), jnp.sum(second, axis=1)), 'ta')]
    dot_general x21 -> x2, matrix products: 60.3 us -> 2.79 us  [the longest x1 1.89 us: per_device(): lax.dot_general(table, onehot, (((0,), (1,)), ((), ())), precision=lax.Pr...]
    all_gather x4 -> x0, waiting for transfers between devices: 20.1 us -> none  [full_rows(): return lax.all_gather(value, 'ta', axis=1, tiled=True)]
    reshape x9 -> x7, local copies, waits for them, and re-layouts: 23.6 us -> 3.51 us  [the longest x1 1.25 us: per_device(): tot[8:12].reshape(-1)]
    convert_element_type x8 -> x0, local copies, waits for them, and re-layouts: 18.8 us -> none  [the longest x2 6.42 us: per_device(): grad_q = jnp.einsum('whij,wjhd->wihd', grad_scores_low, key_view, preferr...]
  transfers between devices with their start and end apart: 12 -> 0, of which waited for: 9 -> 0; matrix products, arithmetic and copies ran while one was open for 6% -> 0% of each run, Pallas kernels for 0% -> 0%
where the time goes in v1:
time: 190 us; the launch traced here: 189 us
  Pallas kernels  156 us (82%)
  local copies, waits for them, and re-layouts  22.6 us (12%)
  other arithmetic  5.96 us (3%)
  matrix products  2.79 us (1%)
    pallas_call x1, Pallas kernels, back_call(): pl.pallas_call(functools.partial(send_back, nt, nz, nbits), name='send_ba...  55 us
    pallas_call x1, Pallas kernels, work_call(): pl.pallas_call(functools.partial(work, nt, slots), name='work', out_shape...  52.2 us
    pallas_call x1, Pallas kernels, bring_call(): pl.pallas_call(functools.partial(bring, nt, nz), name='bring', out_shape=...  48.6 us
    unnamed x16, local copies, waits for them, and re-layouts  7.65 us

profile of v1, /device:TPU:0, one launch (start us, length us, event | category | flops | bytes accessed | tf_op | source)
XLA Modules:
  0.0 188.6 jit_solution(10554153982104282520)
XLA Ops:
  0.7 0.0 copy-start
  1.3 0.0 copy-done
  1.4 0.7 constant_dynamic-update-slice_fusion
  2.1 0.7 constant_dynamic-update-slice_fusion.8
  2.7 0.7 constant_dynamic-update-slice_fusion.7
  3.4 0.7 constant_dynamic-update-slice_fusion.6
  4.0 0.7 constant_dynamic-update-slice_fusion.5
  4.7 0.7 constant_dynamic-update-slice_fusion.4
  5.4 0.7 constant_dynamic-update-slice_fusion.3
  6.0 0.7 constant_dynamic-update-slice_fusion.2
  6.7 0.7 constant_dynamic-update-slice_fusion.1
  7.4 0.6 pad.16.vec
  8.0 0.8 copy.40
  8.8 0.1 eq.32
  8.9 1.9 %fusion.1 = f32[4,2401]{1,0:T(4,128)S(1)} fusion(s32[2401]{0:T(1024)S(1)} %eq.32, f32[169,4]{0,1:T(4,128)} %param.37), kind=kOutput, calls=%fused_computation.2 | convolution fusion | flops 30118144 | bytes 50724 | tf_op jit(solution)/shard_map/dot_general | solution.py:649
  10.8 0.1 reshape.95
  11.0 0.1 copy.41
  11.1 0.8 reshape.96.rb
  11.8 0.7 fusion.4
  12.6 0.7 fusion.5
  13.3 0.8 bitcast_dynamic-update-slice_fusion.3
  14.1 0.8 bitcast_dynamic-update-slice_fusion.2
  14.9 0.8 bitcast_dynamic-update-slice_fusion.1
  15.6 0.8 bitcast_dynamic-update-slice_fusion.wp
  16.4 0.0 copy-start.1
  16.4 0.1 select_select_fusion
  16.5 0.2 tile.4
  16.7 1.4 tile.10.mask
  18.1 0.0 copy-done.1
  18.1 48.6 %bring.1 = (bf16[4,392,128]{2,1,0:T(8,128)(2,1)}, bf16[4,392,128]{2,1,0:T(8,128)(2,1)}, bf16[6,4,4,2,64,256]{5,4,3,2,1,0:T(8,128)(2,1)}, f32[4,24,128]{2,1,0:T(8,128)}, f32[4,64,256]{2,1,0:T(8,128)}) custom-call(bf16[4,392,128]{2,1,0:T(8,128)(2,1)} %bitcast.85, bf16[4,392,128]{2,1,0:T(8,128)(2,1)} %bitcast.86, bf16[6,64,256]{2,1,0:T(8,128)(2,1)} %copy-done.1, ...), custom_call_target="tpu_custom_call" | custom-call | tf_op jit(solution)/shard_map/bring/pallas_call | solution.py:136
  66.7 52.2 %work.1 = (bf16[4,392,128]{2,1,0:T(8,128)(2,1)}, bf16[4,392,128]{2,1,0:T(8,128)(2,1)}, bf16[6,4,512,256]{3,2,1,0:T(8,128)(2,1)}, f32[4,24,128]{2,1,0:T(8,128)}, f32[4,64,256]{2,1,0:T(8,128)}) custom-call(s32[1]{0:T(128)S(6)} %sub.7.live, bf16[4,392,128]{2,1,0:T(8,128)(2,1)} %get-tuple-element.32.x_in, bf16[4,392,128]{2,1,0:T(8,128)(2,1)} %get-tuple-element.33.c_in, ...), custom_call_target="tpu_custom_call" | custom-call | tf_op jit(solution)/shard_map/work/pallas_call | solution.py:403
  118.9 0.7 slice.84
  119.6 0.8 slice.82
  120.4 1.2 reshape.99
  121.6 0.2 reshape.100
  121.8 0.9 fusion
  122.7 0.6 pad_maximum_fusion.2.small
  123.4 55.0 %send_back.1 = (bf16[4,392,128]{2,1,0:T(8,128)(2,1)}, bf16[4,392,128]{2,1,0:T(8,128)(2,1)}, f32[6,64,256]{2,1,0:T(8,128)}, f32[24,128]{1,0:T(8,128)}) custom-call(bf16[4,392,128]{2,1,0:T(8,128)(2,1)} %get-tuple-element.37.y_in, bf16[4,392,128]{2,1,0:T(8,128)(2,1)} %get-tuple-element.38.g_in, bf16[6,4,4,2,64,256]{5,4,3,2,1,0:T(8,128)(2,1)} %bitcast.82, ...), custom_call_target="tpu_custom_call" | custom-call | tf_op jit(solution)/shard_map/send_back/pallas_call | solution.py:581
  178.4 1.2 slice_bitcast_fusion.9
  179.7 0.7 slice.102
  180.4 1.5 slice_bitcast_fusion.10
  181.9 0.6 slice_bitcast_fusion.8
  182.5 1.5 slice_bitcast_fusion.4
  183.9 1.0 slice_bitcast_fusion.1
  184.9 0.7 pad_maximum_fusion.1
  185.5 0.7 pad_maximum_fusion
  186.2 2.4 %bitcast_convert_fusion = (f32[1568,128]{1,0:T(8,128)}, f32[1568,128]{1,0:T(8,128)}) fusion(bf16[4,392,128]{2,1,0:T(8,128)(2,1)} %get-tuple-element.43, bf16[4,392,128]{2,1,0:T(8,128)(2,1)} %get-tuple-element.42), kind=kLoop, calls=%fused_computation.6 | loop fusion | flops 401408 | bytes 2408448 | tf_op jit(solution)/shard_map/convert_element_type | solution.py:680
  (9 shorter events, 0.1 us)
Async XLA Ops:
  0.7 0.7 copy-start
  16.4 1.8 copy-start.1

commit v2 on v0

v2 whole, which is shorter than its diff:
```python
import functools

import jax
import jax.numpy as jnp
from jax import lax
from jax.experimental import pallas as pl
from jax.experimental.pallas import tpu as pltpu
from jax.sharding import PartitionSpec as P

C = 512
HDIM = 32
WT = 49
PAD = 64
TABLE = 169
TPAD = 256
NCH = 6
CW = 256
LANES = 128
SROWS = 24
SCALE = HDIM ** (-0.5)
EPS = 1e-05
F32 = jnp.float32
BF16 = jnp.bfloat16
MESH = pl.DeviceIdType.MESH
ANY = pl.BlockSpec(memory_space=pl.ANY)
VM = pl.BlockSpec(memory_space=pltpu.VMEM)
SM = pl.BlockSpec(memory_space=pltpu.SMEM)
DMA = pltpu.SemaphoreType.DMA


def flip(bit, by):
    return bit + by - 2 * bit * by


def add(left, right):
    return (left.astype(F32) + right.astype(F32)).astype(BF16)


def nn(left, right):
    return jnp.dot(left, right, preferred_element_type=F32)


def nt_dot(left, right):
    return lax.dot_general(left, right, (((1,), (1,)), ((), ())), preferred_element_type=F32)


def tn_dot(left, right):
    return lax.dot_general(left, right, (((0,), (0,)), ((), ())), preferred_element_type=F32)


def norm(value):
    mean = jnp.mean(value, axis=1, keepdims=True)
    spread = jnp.mean(value * value, axis=1, keepdims=True) - mean * mean
    rstd = lax.rsqrt(spread + EPS)
    return (value - mean) * rstd, rstd


def norm_back(scaled, normed, rstd):
    first = jnp.mean(scaled, axis=1, keepdims=True)
    second = jnp.mean(scaled * normed, axis=1, keepdims=True)
    return rstd * (scaled - first - normed * second)


def gelu_pair(u):
    cdf = 0.5 + 0.5 * lax.erf(u * (0.5**0.5))
    pdf = jnp.exp(-0.5 * u * u) * ((2.0 * jnp.pi) ** -0.5)
    return u * cdf, cdf + u * pdf


def rowsum(value):
    return jnp.sum(value, axis=0, keepdims=True)


def block(nt, nz, slots, nbits, *refs):
    (
        live, tok, cot, wq, wk, wv, wo, wh, wd, g1, s1, bq, bv, bo, g2, s2, bd, bh, tab, rel, reg,
        y_all, g_all, fin, tot,
        xg, cg, gw, vg, rg, dv, rc, ry, rx, r3, rz, scr, syr, sx, small, yb, gb, square, mask, inv,
        xs, xp, gy, h1, h1t, h2t, gyt, qs, kvs, probs, att, acc, acc2, n1, r1, n2, r2, low, gkv, gq,
        pairs,
        loc, tok_s, tok_r, out_s, out_r, az_s, az_r, ax_s, ax_r, ay_s, ay_r, ac_s, ac_r,
        bx_s, bx_r, k_s, k_r, p_s, p_r, q_s, q_r, rz_s, rz_r, sm_s, sm_r,
    ) = refs
    heads = LANES // HDIM
    rows = slots * PAD
    half = 2 * PAD
    nhalf = rows // half
    a, t = lax.axis_index("wa"), lax.axis_index("ta")
    x, z, c, y = lax.rem(a, 2), lax.div(a, 2), lax.rem(t, 2), lax.div(t, 2)

    def group(m):
        return 2 * flip(y, m // 2 if isinstance(m, int) else lax.div(m, 2)) + flip(
            c, m % 2 if isinstance(m, int) else lax.rem(m, 2)
        )

    t1, t2, t3 = group(1), group(2), group(3)
    xpeer, ypeer, cpeer = (z * 2 + (1 - x), t), (a, t2), (a, t1)
    zs = [(lax.rem(z + d, nz) * 2 + x, t) for d in range(1, nz)]
    ts = [(a, tt) for tt in (t1, t2, t3)]
    flips = []
    for b in range(nbits):
        bit = 2**b
        flips.append((a + bit - 2 * bit * lax.rem(lax.div(a, bit), 2), t))
    peers = zs + ts + [xpeer]
    barrier = pltpu.get_barrier_semaphore()
    for peer in peers:
        pl.semaphore_signal(barrier, inc=1, device_id=peer, device_id_type=MESH)

    def far(src, dst, send, recv, peer):
        return pltpu.make_async_remote_copy(
            src_ref=src, dst_ref=dst, send_sem=send, recv_sem=recv, device_id=peer,
            device_id_type=MESH,
        )

    def tok_copy(i, d):
        src, dst = ((tok, xg), (cot, cg), (vg, vg), (rg, rg))[i]
        peer = ts[d]
        src = src.at[peer[1]] if i < 2 else src.at[t]
        return far(src, dst.at[t], tok_s.at[i, d], tok_r.at[i, d], peer)

    def out_copy(i, d):
        src, dst = ((yb, y_all), (gb, g_all))[i]
        peer = ts[d]
        return far(src.at[peer[1]], dst.at[t], out_s.at[i, d], out_r.at[i, d], peer)

    def az(ch, d):
        ref = gw.at[ch, t, z, x]
        return far(ref, ref, az_s.at[ch, d], az_r.at[ch, d], zs[d])

    def ax(ch, d):
        ref = gw.at[ch, t, lax.rem(z + nz - d, nz), x]
        return far(ref, ref, ax_s.at[ch, d], ax_r.at[ch, d], xpeer)

    def ay(ch, d):
        ref = gw.at[ch, t, lax.rem(z + nz - d, nz)]
        return far(ref, ref, ay_s.at[ch, d], ay_r.at[ch, d], ypeer)

    def by(ch):
        ref = gw.at[ch, t, :, x]
        return far(ref, ref, ay_s.at[ch, 0], ay_r.at[ch, 0], ypeer)

    def bx(ch, j):
        ref = gw.at[ch, t2 if j else t, :, x]
        return far(ref, ref, bx_s.at[ch, j], bx_r.at[ch, j], xpeer)

    def ac(ch, j):
        ref = gw.at[ch, t2 if j else t]
        return far(ref, ref, ac_s.at[ch, j], ac_r.at[ch, j], cpeer)

    def kc(ch, j):
        return far(dv.at[ch, t1 if j else t3], rc.at[ch, j], k_s.at[ch, j], k_r.at[ch, j], cpeer)

    def ya(ch):
        return far(dv.at[ch, t2], ry.at[ch], p_s.at[ch, 0], p_r.at[ch, 0], ypeer)

    def xa(ch):
        return far(dv.at[ch, t, :, 1 - x], r3.at[ch], q_s.at[ch], q_r.at[ch], xpeer)

    def xb(ch, j):
        src = dv.at[ch, t if j else t2, :, 1 - x]
        return far(src, rx.at[ch - 4, j], p_s.at[ch, j], p_r.at[ch, j], xpeer)

    def yb2(ch):
        return far(dv.at[ch, t2, :, x], r3.at[ch], q_s.at[ch], q_r.at[ch], ypeer)

    def zr(ch, d):
        src = dv.at[ch, t, lax.rem(z + d + 1, nz), x]
        return far(src, rz.at[ch, d], rz_s.at[ch, d], rz_r.at[ch, d], zs[d])

    def core_first(ch):
        kc(ch, 0).wait_recv()
        dv[ch, t2] = add(dv[ch, t2], rc[ch, 0])

    def core_second(ch):
        kc(ch, 1).wait_recv()
        dv[ch, t] = add(dv[ch, t], rc[ch, 1])

    def second_a(ch):
        ya(ch).wait_recv()
        dv[ch, t] = add(dv[ch, t], ry[ch])
        xa(ch).start()

    def second_b(ch):
        for j, tt in enumerate((t2, t)):
            xb(ch, j).wait_recv()
            dv[ch, tt, :, x] = add(dv[ch, tt, :, x], rx[ch - 4, j])
        yb2(ch).start()

    def third(ch):
        (xa(ch) if ch < 4 else yb2(ch)).wait_recv()
        dv[ch, t, :, x] = add(dv[ch, t, :, x], r3[ch])
        for d in range(nz - 1):
            zr(ch, d).start()

    def fourth(ch):
        value = dv[ch, t, z, x].astype(F32)
        for d in range(nz - 1):
            zr(ch, d).wait_recv()
            value = value + rz[ch, d].astype(F32)
        fin[ch] = value

    def small_core(j):
        return far(small.at[t1 if j else t3], scr.at[j], sm_s.at[j], sm_r.at[j], cpeer)

    def small_y():
        return far(sx.at[0], syr.at[0], sm_s.at[2], sm_r.at[2], ypeer)

    def small_flip(b):
        return far(sx.at[2 + b], syr.at[1 + b], sm_s.at[3 + b], sm_r.at[3 + b], flips[b])

    def flat(value):
        return value.astype(F32).T.astype(BF16)

    gw[0, t, z, x, :, :LANES] = wq[...]
    gw[0, t, z, x, :, LANES:] = flat(wo[...])
    gw[1, t, z, x, :, :LANES] = wk[...]
    gw[1, t, z, x, :, LANES:] = wv[...]
    for i, ref in enumerate((g1, s1, bq, bv, bo, g2, s2, bd)):
        vg[t, i : i + 1, :] = ref[...]
    vg[t, 8:12, :] = bh[...]
    vg[t, 12:, :] = jnp.zeros((SROWS - 12, LANES), F32)
    pl.semaphore_wait(barrier, len(peers))
    own_tok = pltpu.make_async_copy(tok.at[t], xg.at[t], loc.at[0])
    own_cot = pltpu.make_async_copy(cot.at[t], cg.at[t], loc.at[1])
    own_tok.start()
    own_cot.start()
    for ch in range(2):
        for d in range(nz - 1):
            az(ch, d).start()
        ax(ch, 0).start()
    for d in range(3):
        tok_copy(0, d).start()
    for d in range(3):
        tok_copy(2, d).start()
    square[...] = jnp.zeros_like(square)
    square[:TABLE, :heads] = tab[...]
    table = square[...].T
    square[...] = jnp.zeros_like(square)
    square[:WT, :WT] = rel[...].astype(F32)
    rel_t = square[:LANES, :].T[:PAD, :PAD]
    pick_at = jnp.concatenate([rel_t, rel_t], axis=1).astype(jnp.int32)
    lane = lax.broadcasted_iota(jnp.int32, (PAD, LANES), 1)
    low_at, high_at = jnp.minimum(pick_at, LANES - 1), jnp.maximum(pick_at - LANES, 0)

    def take(value, at):
        return jnp.take_along_axis(value, at, axis=1, mode="promise_in_bounds")

    def entry(h):
        first = jnp.broadcast_to(table[h : h + 1, :LANES], (PAD, LANES))
        second = jnp.broadcast_to(table[h : h + 1, LANES:], (PAD, LANES))
        return jnp.where(pick_at < LANES, take(first, low_at), take(second, high_at))

    for q in range(heads // 2):
        rg[t, :, q * LANES : (q + 1) * LANES] = jnp.where(
            lane < PAD, entry(2 * q), entry(2 * q + 1)
        )
    for d in range(3):
        tok_copy(3, d).start()
    number = lax.broadcasted_iota(jnp.int32, (PAD, TPAD), 1).astype(F32)
    found = jnp.full((PAD, TPAD), -1.0, F32)
    for i in range(WT):
        found = jnp.where(rel_t[:, i : i + 1] == number, float(i), found)
    inv[...] = found.astype(jnp.int32)
    square[...] = jnp.zeros_like(square)
    mine = reg[pl.ds(pl.multiple_of(t * slots, slots), slots), :]
    square[:slots, :WT] = mine.astype(F32)
    reg_row = square[:slots, :PAD]
    reg_row = jnp.concatenate([reg_row] * heads, axis=1)
    reg_col = square[:LANES, :].T[:PAD, :slots]
    real = lax.broadcasted_iota(jnp.int32, (PAD, heads * PAD), 0) < WT
    for w in range(slots):
        same = reg_col[:, w : w + 1] == reg_row[w : w + 1, :]
        mask[w] = jnp.where(real, jnp.where(same, 0.0, -100.0), -1e30)
    for s in range(2):
        gw[2 + s, t, z, x] = wh[:, s * CW : (s + 1) * CW]
        gw[4 + s, t, z, x] = flat(wd[s * CW : (s + 1) * CW, :])
    for ch in range(2):
        for d in range(nz - 1):
            az(ch, d).wait_recv()
            ax(ch, d + 1).start()
    for ch in (2, 4, 3, 5):
        for d in range(nz - 1):
            az(ch, d).start()

    def wide(i):
        return jnp.concatenate([vg[tt, i : i + 1, :] for tt in range(nt)], axis=1)

    def put_small(i, value):
        for tt in range(nt):
            small[tt, i : i + 1, :] = value[:, tt * LANES : (tt + 1) * LANES]

    def spread(source, target):
        for tt in range(nt):
            xs[:, tt * LANES : (tt + 1) * LANES] = source[tt].astype(F32)
        zero = jnp.zeros((PAD - WT, C), F32)
        for w in range(slots):
            target[w * PAD : w * PAD + WT, :] = xs[w * WT : (w + 1) * WT, :]
            target[w * PAD + WT : (w + 1) * PAD, :] = zero

    def gather(source, target):
        for w in range(slots):
            xs[w * WT : (w + 1) * WT, :] = source[w * PAD : w * PAD + WT, :]
        for tt in range(nt):
            target[tt] = xs[:, tt * LANES : (tt + 1) * LANES].astype(BF16)

    def each(body, init=0):
        def step(i, carry):
            return body(i, pl.ds(pl.multiple_of(i * half, half), half), carry)

        return lax.fori_loop(0, nhalf, step, init)

    def weight(ch, tt, start=0, size=CW):
        return gw[ch, tt, :, :, :, start : start + size].reshape(C, size)

    def put_grad(ch, tt, value):
        dv[ch, tt] = value.astype(BF16).reshape(dv.shape[2:])

    n_live = live[0] - t * slots
    small[...] = jnp.zeros_like(small)
    own_tok.wait()
    for i in (0, 2):
        for d in range(3):
            tok_copy(i, d).wait_recv()
    spread(xg, xp)
    gain1, shift1 = wide(0), wide(1)

    def start(i, at, carry):
        normed, rstd = norm(xp[at, :])
        n1[at, :] = normed
        r1[at, :] = rstd
        h = normed * gain1 + shift1
        h1[at, :] = h.astype(BF16)
        h1t[:, at] = h.T.astype(BF16)
        return carry

    each(start)
    for ch in range(2):
        for d in range(nz):
            ax(ch, d).wait_recv()
            ay(ch, d).start()
        ac(ch, 0).start()
    for d in range(3):
        tok_copy(3, d).wait_recv()
    for d in range(3):
        tok_copy(1, d).start()
    lane_head = lax.broadcasted_iota(jnp.int32, (PAD, LANES), 1) // HDIM
    ones = [(lane_head == h).astype(F32).astype(BF16) for h in range(heads)]

    def stack(value):
        return jnp.concatenate([value * ones[h] for h in range(heads)], axis=0)

    def pick(value):
        out = value[0:PAD]
        for h in range(1, heads):
            out = jnp.where(lane_head == h, value[h * PAD : (h + 1) * PAD], out)
        return out

    acc[...] = jnp.zeros_like(acc)

    def attend(i, carry):
        tt = group(i)

        @pl.when(i == 1)
        def _():
            for ch in range(2):
                ac(ch, 0).wait_recv()

        @pl.when(i == 2)
        def _():
            for ch in range(2):
                for d in range(nz):
                    ay(ch, d).wait_recv()
                ac(ch, 1).start()

        @pl.when(i == 3)
        def _():
            for ch in range(2):
                ac(ch, 1).wait_recv()

        q = (nn(h1[...], weight(0, tt, 0, LANES)) + vg[tt, 2:3, :]) * SCALE
        qs[tt] = q.astype(BF16)
        kv = nn(h1[...], weight(1, tt))
        kvs[tt, :, :LANES] = kv[:, :LANES].astype(BF16)
        kvs[tt, :, LANES:] = (kv[:, LANES:] + vg[tt, 3:4, :]).astype(BF16)

        def window(w, carry):
            at = pl.ds(pl.multiple_of(w * PAD, PAD), PAD)
            s = nt_dot(kvs[tt, at, :LANES], stack(qs[tt, at, :])) + rg[tt] + mask[w]
            e = jnp.exp(s - jnp.max(s, axis=0, keepdims=True))
            p = e / rowsum(e)
            probs[tt, w] = p
            att[tt, at, :] = pick(tn_dot(p.astype(BF16), kvs[tt, at, LANES:])).astype(BF16)
            return carry

        lax.fori_loop(0, slots, window, 0, unroll=2)
        acc[...] += nt_dot(att[tt], weight(0, tt, LANES, LANES))

        def feed(chs):
            for ch in chs:
                for d in range(nz - 1):
                    az(ch, d).wait_recv()
                by(ch).start()

        def feed_x(chs):
            for ch in chs:
                by(ch).wait_recv()
                for j in range(2):
                    bx(ch, j).start()

        @pl.when(i == 0)
        def _():
            feed((2, 4))

        @pl.when(i == 1)
        def _():
            feed((3, 5))

        @pl.when(i == 2)
        def _():
            feed_x((2, 4))

        @pl.when(i == 3)
        def _():
            feed_x((3, 5))

        return carry

    lax.fori_loop(0, nt, attend, 0)

    def feed_core(chs):
        for ch in chs:
            for j in range(2):
                bx(ch, j).wait_recv()
            for j in range(2):
                ac(ch, j).start()

    own_cot.wait()
    for d in range(3):
        tok_copy(1, d).wait_recv()
    spread(cg, gy)
    feed_core((2, 4))
    b_out, gain2, shift2 = wide(4), wide(5), wide(6)

    def live_rows(i):
        slot = lax.div(i * half + lax.broadcasted_iota(jnp.int32, (half, 1), 0), PAD)
        return slot < n_live

    def middle(i, at, carry):
        x1 = xp[at, :] + acc[at, :] + b_out
        xp[at, :] = x1
        normed, rstd = norm(x1)
        n2[at, :] = normed
        r2[at, :] = rstd
        h = normed * gain2 + shift2
        low[at, :] = h.astype(BF16)
        h2t[:, at] = h.T.astype(BF16)
        g = jnp.where(live_rows(i), gy[at, :], 0.0)
        gy[at, :] = g
        gkv[at, :] = g.astype(BF16)
        gyt[:, at] = g.T.astype(BF16)
        return carry

    each(middle)
    acc[...] = jnp.zeros_like(acc)
    acc2[...] = jnp.zeros_like(acc2)
    for ch in (2, 4):
        for j in range(2):
            ac(ch, j).wait_recv()

    def mlp(k, carry):
        s, i = lax.div(k, nt), lax.rem(k, nt)
        tt = group(3 - i)
        up, down = 2 + s, 4 + s

        @pl.when(k == 2)
        def _():
            feed_core((3, 5))

        @pl.when(k == 4)
        def _():
            for ch in (3, 5):
                for j in range(2):
                    ac(ch, j).wait_recv()

        bias = vg[tt, pl.ds(8 + 2 * s, 2), :]
        bias = jnp.concatenate([bias[0:1], bias[1:2]], axis=1)
        hidden = nn(low[...], weight(up, tt)) + bias
        act, slope = gelu_pair(hidden)
        act_low = act.astype(BF16)
        acc[...] += nt_dot(act_low, weight(down, tt))
        put_grad(down, tt, nn(gyt[...], act_low))
        grad = nn(gkv[...], weight(down, tt)) * slope
        total = rowsum(grad)
        small[tt, pl.ds(8 + 2 * s, 1), :] = total[:, :LANES]
        small[tt, pl.ds(9 + 2 * s, 1), :] = total[:, LANES:]
        grad_low = grad.astype(BF16)
        put_grad(up, tt, nn(h2t[...], grad_low))
        acc2[...] += nt_dot(grad_low, weight(up, tt))

        @pl.when(i == 0)
        def _():
            kc(down, 0).start()
            kc(up, 0).start()

        @pl.when(i == 1)
        def _():
            core_first(up)
            ya(up).start()
            core_first(down)

        @pl.when(i == 2)
        def _():
            kc(down, 1).start()
            kc(up, 1).start()

        @pl.when(i == 3)
        def _():
            core_second(down)
            for j in range(2):
                xb(down, j).start()
            core_second(up)

        return carry

    lax.fori_loop(0, 2 * nt, mlp, 0)
    second_a(2)
    second_b(4)
    b_down = wide(7)
    zero_row = jnp.zeros((1, C), F32)

    def turn(i, at, carry):
        xp[at, :] = jnp.where(live_rows(i), xp[at, :] + acc[at, :] + b_down, 0.0)
        e, normed, g = acc2[at, :], n2[at, :], gy[at, :]
        gx = norm_back(e * gain2, normed, r2[at, :]) + g
        gy[at, :] = gx
        low[at, :] = gx.astype(BF16)
        h2t[:, at] = gx.T.astype(BF16)
        sums = (rowsum(e * normed), rowsum(e), rowsum(gx), rowsum(g))
        return tuple(p + q for p, q in zip(carry, sums))

    sums = each(turn, (zero_row,) * 4)
    put_small(5, sums[0])
    put_small(6, sums[1])
    put_small(4, sums[2])
    put_small(7, sums[3])
    gather(xp, yb)
    own_y = pltpu.make_async_copy(yb.at[t], y_all.at[t], loc.at[2])
    own_y.start()
    for d in range(3):
        out_copy(0, d).start()
    acc[...] = jnp.zeros_like(acc)

    def back(i, carry):
        tt = group(3 - i)
        gatt = gq
        gatt[...] = nn(low[...], weight(0, tt, LANES, LANES)).astype(BF16)
        pairs[...] = jnp.zeros_like(pairs)

        def window(w, carry):
            at = pl.ds(pl.multiple_of(w * PAD, PAD), PAD)
            q4, g4 = stack(qs[tt, at, :]), stack(gatt[at, :])
            p = probs[tt, w]
            dp = nt_dot(kvs[tt, at, LANES:], g4)
            ds = p * (dp - rowsum(p * dp))
            ds_low = ds.astype(BF16)
            pairs[...] += ds_low.astype(F32)
            gkv[at, :LANES] = nn(ds_low, q4).astype(BF16)
            gkv[at, LANES:CW] = nn(p.astype(BF16), g4).astype(BF16)
            gatt[at, :] = pick(tn_dot(ds_low, kvs[tt, at, :LANES])).astype(BF16)
            return carry

        lax.fori_loop(0, slots, window, 0, unroll=2)
        gk_gv = gkv[:, :CW]
        put_grad(1, tt, nn(h1t[...], gk_gv))
        left = nn(h1t[...], gatt[...]) * SCALE
        put_grad(0, tt, jnp.concatenate([left, nn(h2t[...], att[tt])], axis=1))

        @pl.when(i == 0)
        def _():
            kc(1, 0).start()
            kc(0, 0).start()

        @pl.when(i == 2)
        def _():
            kc(1, 1).start()
            kc(0, 1).start()

        small[tt, 2:3, :] = rowsum(gatt[...].astype(F32)) * SCALE
        small[tt, 3:4, :] = rowsum(gkv[:, LANES:CW].astype(F32))
        grad_q = nt_dot(gatt[...], weight(0, tt, 0, LANES)) * SCALE
        acc[...] += grad_q + nt_dot(gk_gv, weight(1, tt))
        for h in range(heads):
            lanes = h // 2 * LANES
            source = pairs[:, lanes : lanes + LANES]
            for q in range(TPAD // LANES):
                where = inv[:, q * LANES : (q + 1) * LANES]
                value = take(source, jnp.maximum(where, 0) + h % 2 * PAD)
                value = jnp.where(where >= 0, value, 0.0)
                small[tt, pl.ds(12 + 2 * h + q, 1), :] = rowsum(value)

        @pl.when(i == 0)
        def _():
            third(2)
            third(4)

        @pl.when(i == 1)
        def _():
            for ch in range(2):
                core_first(ch)
                ya(ch).start()
            second_a(3)
            second_b(5)

        @pl.when(i == 2)
        def _():
            third(3)
            third(5)
            fourth(2)
            fourth(4)

        @pl.when(i == 3)
        def _():
            for ch in range(2):
                core_second(ch)

        return carry

    lax.fori_loop(0, nt, back, 0)

    def finish(i, at, carry):
        e, normed = acc[at, :], n1[at, :]
        xp[at, :] = norm_back(e * gain1, normed, r1[at, :]) + gy[at, :]
        sums = (rowsum(e * normed), rowsum(e))
        return tuple(p + q for p, q in zip(carry, sums))

    sums = each(finish, (zero_row,) * 2)
    put_small(0, sums[0])
    put_small(1, sums[1])
    for j in range(2):
        small_core(j).start()
    second_a(0)
    gather(xp, gb)
    own_g = pltpu.make_async_copy(gb.at[t], g_all.at[t], loc.at[3])
    own_g.start()
    for d in range(3):
        out_copy(1, d).start()
    for j in range(2):
        small_core(j).wait_recv()
    sx[0] = small[t2] + scr[0]
    sx[1] = small[t] + scr[1]
    small_y().start()
    second_a(1)
    small_y().wait_recv()
    sx[2] = sx[1] + syr[0]
    small_flip(0).start()
    fourth(3)
    third(0)
    third(1)
    fourth(5)
    for b in range(nbits):
        small_flip(b).wait_recv()
        sx[3 + b] = sx[2 + b] + syr[1 + b]
        if b + 1 < nbits:
            small_flip(b + 1).start()
    fourth(0)
    fourth(1)
    tot[...] = sx[2 + nbits]
    for i in range(2):
        for d in range(3):
            out_copy(i, d).wait_recv()
    sent = [tok_copy(i, d) for i in range(4) for d in range(3)]
    sent += [out_copy(i, d) for i in range(2) for d in range(3)]
    for ch in range(NCH):
        sent += [az(ch, d) for d in range(nz - 1)] + [zr(ch, d) for d in range(nz - 1)]
        sent += [ac(ch, j) for j in range(2)] + [kc(ch, j) for j in range(2)]
        if ch < 2:
            sent += [ax(ch, d) for d in range(nz)] + [ay(ch, d) for d in range(nz)]
        else:
            sent += [by(ch), bx(ch, 0), bx(ch, 1)]
        sent += [ya(ch), xa(ch)] if ch < 4 else [xb(ch, 0), xb(ch, 1), yb2(ch)]
    sent += [small_core(0), small_core(1), small_y()] + [small_flip(b) for b in range(nbits)]
    for copy in sent:
        copy.wait_send()
    own_y.wait()
    own_g.wait()


def block_call(nt, nz, slots, *args):
    tok, deep, heads = args[1], args[3].shape[0], args[18].shape[1]
    real = tok.shape[1]
    rows, wide = slots * PAD, heads * PAD
    nbits = (2 * nz - 1).bit_length()
    piece = (nz, 2, deep, CW)
    row = (nt, real, LANES)

    def vm(shape, kind=BF16):
        return pltpu.VMEM(shape, kind)

    def pair(*shape):
        return [DMA(shape), DMA(shape)]

    small = (SROWS, LANES)
    return pl.pallas_call(
        functools.partial(block, nt, nz, slots, nbits),
        name="block",
        out_shape=(
            jax.ShapeDtypeStruct(row, BF16),
            jax.ShapeDtypeStruct(row, BF16),
            jax.ShapeDtypeStruct((NCH, deep, CW), F32),
            jax.ShapeDtypeStruct(small, F32),
        ),
        in_specs=[SM, ANY, ANY] + [VM] * 18,
        out_specs=(ANY, ANY, VM, VM),
        scratch_shapes=[
            vm(row),
            vm(row),
            vm((NCH, nt) + piece),
            vm((nt,) + small, F32),
            vm((nt, PAD, wide), F32),
            vm((NCH, nt) + piece),
            vm((NCH, 2) + piece),
            vm((4,) + piece),
            vm((2, 2, nz, deep, CW)),
            vm((NCH, nz, deep, CW)),
            vm((NCH, nz - 1, deep, CW)),
            vm((2,) + small, F32),
            vm((1 + nbits,) + small, F32),
            vm((3 + nbits,) + small, F32),
            vm((nt,) + small, F32),
            vm(row),
            vm(row),
            vm((TPAD, LANES), F32),
            vm((slots, PAD, wide), F32),
            vm((PAD, TPAD), jnp.int32),
            vm((real, C), F32),
            vm((rows, C), F32),
            vm((rows, C), F32),
            vm((rows, C)),
            vm((C, rows)),
            vm((C, rows)),
            vm((C, rows)),
            vm((nt, rows, LANES)),
            vm((nt, rows, CW)),
            vm((nt, slots, PAD, wide), F32),
            vm((nt, rows, LANES)),
            vm((rows, C), F32),
            vm((rows, C), F32),
            vm((rows, C), F32),
            vm((rows, 1), F32),
            vm((rows, C), F32),
            vm((rows, 1), F32),
            vm((rows, C)),
            vm((rows, C)),
            vm((rows, LANES)),
            vm((PAD, wide), F32),
            DMA((4,)),
        ]
        + pair(4, 3)
        + pair(2, 3)
        + pair(NCH, nz - 1)
        + pair(2, nz)
        + pair(NCH, nz)
        + pair(NCH, 2)
        + pair(NCH, 2)
        + pair(NCH, 2)
        + pair(NCH, 2)
        + pair(NCH)
        + pair(NCH, nz - 1)
        + pair(3 + nbits),
        compiler_params=pltpu.CompilerParams(
            collective_id=0, has_side_effects=True, vmem_limit_bytes=60 * 2**20
        ),
    )(*args)


def spell(y_all, g_all, fin, tot, *outs):
    (
        y_out, g_out, d_g1, d_s1, d_wq, d_wk, d_wv, d_bq, d_bv, d_wo, d_bo, d_g2, d_s2, d_wh, d_bh,
        d_wd, d_bd, d_tab,
    ) = outs
    y_out[...] = y_all[...].astype(F32)
    g_out[...] = g_all[...].astype(F32)
    d_wq[...] = fin[0, :, :LANES]
    d_wk[...] = fin[1, :, :LANES]
    d_wv[...] = fin[1, :, LANES:]
    d_wo[...] = fin[0, :, LANES:].T
    for s in range(2):
        d_wh[:, s * CW : (s + 1) * CW] = fin[2 + s]
        d_wd[s * CW : (s + 1) * CW, :] = fin[4 + s].T
    for i, ref in enumerate((d_g1, d_s1, d_bq, d_bv, d_bo, d_g2, d_s2, d_bd)):
        ref[...] = tot[i : i + 1, :]
    d_bh[...] = tot[8:12, :]
    heads = d_tab.shape[1]
    table = [
        jnp.concatenate([tot[12 + 2 * h : 13 + 2 * h], tot[13 + 2 * h : 14 + 2 * h]], axis=1)
        for h in range(heads)
    ]
    table = jnp.concatenate(table + [jnp.zeros((8 - heads, TPAD), F32)], axis=0).T
    d_tab[...] = table[:TABLE, :heads]


def spell_call(outs, *args):
    return pl.pallas_call(
        spell,
        name="spell",
        out_shape=outs,
        in_specs=[VM] * 4,
        out_specs=(VM,) * len(outs),
        compiler_params=pltpu.CompilerParams(vmem_limit_bytes=24 * 2**20),
    )(*args)


def per_device(
    nt, na, tokens, gain_one, shift_one, w_query, w_key, w_value, b_query, b_value, w_out, b_out,
    gain_two, shift_two, w_hidden, b_hidden, w_down, b_down, bias_table, rel_index, region,
    win_count, cotangent,
):
    slots = region.shape[0] // nt
    cut = (nt, slots * WT, LANES)
    vectors = [gain_one, shift_one, b_query, b_value, b_out, gain_two, shift_two, b_down]
    parts = block_call(
        nt, na // 2, slots,
        win_count, tokens.reshape(cut), cotangent.reshape(cut),
        w_query, w_key, w_value, w_out, w_hidden, w_down,
        *[v.reshape(1, LANES) for v in vectors],
        b_hidden.reshape(-1, LANES), bias_table, rel_index, region,
    )

    def out(like, shape=None):
        return jax.ShapeDtypeStruct(shape or like.shape, F32)

    one = (1, LANES)
    shapes = (
        out(tokens, cut), out(tokens, cut), out(gain_one, one), out(gain_one, one), out(w_query),
        out(w_key), out(w_value), out(b_query, one), out(b_value, one), out(w_out),
        out(b_out, one), out(gain_two, one), out(shift_two, one), out(w_hidden),
        out(b_hidden, (b_hidden.shape[0] // LANES, LANES)), out(w_down), out(b_down, one),
        out(bias_table),
    )
    likes = (
        tokens, tokens, gain_one, gain_one, w_query, w_key, w_value, b_query, b_value, w_out,
        b_out, gain_two, shift_two, w_hidden, b_hidden, w_down, b_down, bias_table,
    )
    values = spell_call(shapes, *parts)
    return tuple(v.reshape(like.shape) for v, like in zip(values, likes))


def solution(mesh):
    return jax.shard_map(
        functools.partial(per_device, mesh.shape["ta"], mesh.shape["wa"]),
        mesh=mesh,
        in_specs=(
            P("wa", "ta"),
            P("ta"),
            P("ta"),
            P("wa", "ta"),
            P("wa", "ta"),
            P("wa", "ta"),
            P("ta"),
            P("ta"),
            P("ta", "wa"),
            P("ta"),
            P("ta"),
            P("ta"),
            P("wa", "ta"),
            P("ta"),
            P("ta", "wa"),
            P("ta"),
            P(None, "ta"),
            P(),
            P("wa", None),
            P("wa"),
            P("wa", "ta"),
        ),
        out_specs=(
            P("wa", "ta"),
            P("wa", "ta"),
            P("ta"),
            P("ta"),
            P("wa", "ta"),
            P("wa", "ta"),
            P("wa", "ta"),
            P("ta"),
            P("ta"),
            P("ta", "wa"),
            P("ta"),
            P("ta"),
            P("ta"),
            P("wa", "ta"),
            P("ta"),
            P("ta", "wa"),
            P("ta"),
            P(None, "ta"),
        ),
        check_vma=False,
    )
```

time: 717 us -> 133 us (0.19)
  waiting for transfers between devices: 346 us -> 0 us
  blocking collectives: 209 us -> 0 us
  Pallas kernels: 0 us -> 124 us
  matrix products: 60.3 us -> 0 us
  local copies, waits for them, and re-layouts: 49 us -> 8.12 us
  other arithmetic: 33 us -> 0 us
  between operations: 15.6 us -> 1.36 us
    reduce_scatter x8 -> x0, waiting for transfers between devices: 325 us -> none  [the longest x4 133 us: share(): return lax.psum_scatter(value, 'ta', scatter_dimension=1, tiled=True)]
    all_gather x4 -> x0, blocking collectives: 127 us -> none  [the longest x2 64.3 us: gather_outputs(): return lax.all_gather(weight, 'wa', axis=1, tiled=True)]
    pallas_call x0 -> x2, Pallas kernels: none -> 124 us  [the longest x1 122 us: block_call(): pl.pallas_call(functools.partial(block, nt, nz, slots, nbits), name='bloc...]
    psum x5 -> x0, blocking collectives: 81.9 us -> none  [the longest x4 44.6 us: row_sums(): return lax.psum((jnp.sum(first, axis=1), jnp.sum(second, axis=1)), 'ta')]
    dot_general x21 -> x0, matrix products: 60.3 us -> none  [the longest x5 21.5 us: against(): lax.dot_general(left, right, (((1,), (1,)), ((), ())), preferred_element_...]
    reshape x9 -> x0, local copies, waits for them, and re-layouts: 23.6 us -> none  [the longest x2 7.31 us: per_device(): value_view = values.reshape(slots, WT, heads, HDIM)]
    all_gather x4 -> x0, waiting for transfers between devices: 20.1 us -> none  [full_rows(): return lax.all_gather(value, 'ta', axis=1, tiled=True)]
    convert_element_type x8 -> x0, local copies, waits for them, and re-layouts: 18.8 us -> none  [the longest x2 6.42 us: per_device(): grad_q = jnp.einsum('whij,wjhd->wihd', grad_scores_low, key_view, preferr...]
  transfers between devices with their start and end apart: 12 -> 0, of which waited for: 9 -> 0; matrix products, arithmetic and copies ran while one was open for 6% -> 0% of each run, Pallas kernels for 0% -> 0%
where the time goes in v2:
time: 133 us
  Pallas kernels  124 us (93%)
  local copies, waits for them, and re-layouts  8.12 us (6%)
  between operations  1.36 us (1%)
    pallas_call x1, Pallas kernels, block_call(): pl.pallas_call(functools.partial(block, nt, nz, slots, nbits), name='bloc...  122 us
    unnamed x20, local copies, waits for them, and re-layouts  8.12 us

profile of v2, /device:TPU:0, one launch (start us, length us, event | category | flops | bytes accessed | tf_op | source)
XLA Modules:
  0.0 133.1 jit_solution(4677232328013449654)
XLA Ops:
  0.7 0.0 copy-start.5
  1.3 0.0 copy-start.6
  1.3 0.0 copy-done.5
  1.4 0.0 copy-start.4
  1.4 0.7 copy.39.refs_6_
  2.1 0.0 copy-done.6
  2.1 0.8 copy.41.refs_18_
  2.9 0.0 copy-done.4
  2.9 0.8 copy.40.refs_8_
  3.6 122.2 %block.1 = (bf16[4,392,128]{2,1,0:T(8,128)(2,1)}, bf16[4,392,128]{2,1,0:T(8,128)(2,1)}, f32[6,64,256]{2,1,0:T(8,128)}, f32[24,128]{1,0:T(8,128)}) custom-call(s32[1]{0:T(128)S(6)} %copy.45.refs_0_, bf16[4,392,128]{2,1,0:T(8,128)(2,1)} %bitcast.22, bf16[4,392,128]{2,1,0:T(8,128)(2,1)} %bitcast.23, bf16[64,128]{1,0:T(8,128)(2,1)} %refs_3_.1, ...), custom_call_target="tpu_custom_call" | custom-call | tf_op jit(solution)/shard_map/block/pallas_call | solution.py:703
  125.9 0.0 copy-start
  125.9 1.0 copy-done
  126.9 0.0 copy-start.1
  126.9 1.0 copy-done.1
  127.9 0.0 copy-start.2
  127.9 1.0 copy-done.2
  128.9 0.0 copy-start.3
  128.9 0.7 copy-done.3
  129.6 1.4 %spell.1 = (f32[4,392,128]{2,1,0:T(8,128)}, f32[4,392,128]{2,1,0:T(8,128)}, f32[1,128]{1,0:T(1,128)}, f32[1,128]{1,0:T(1,128)}, f32[64,128]{1,0:T(8,128)}, /*ind...) custom-call(bf16[4,392,128]{2,1,0:T(8,128)(2,1)S(1)} %copy-done, ...), custom_call_target="tpu_custom_call" | custom-call | tf_op jit(solution)/shard_map/spell/pallas_call | solution.py:803
  131.0 0.7 copy.44
  131.6 0.7 copy.42
  132.3 0.8 copy.43
Async XLA Ops:
  0.7 0.7 copy-start.5
  1.3 0.8 copy-start.6
  1.4 1.5 %copy-start.4 = (bf16[512,64]{0,1:T(8,128)(2,1)S(1)}, bf16[512,64]{0,1:T(8,128)(2,1)}, u32[]{:S(2)}) copy-start(bf16[512,64]{0,1:T(8,128)(2,1)} %param.35) | copy-start | bytes 196612
  125.9 1.0 copy-start
  126.9 1.0 copy-start.1
  127.9 1.0 copy-start.2
  128.9 0.7 copy-start.3

commit v3 on v2

--- a/solution.py
+++ b/solution.py
@@ -71,15 +71,15 @@
     return jnp.sum(value, axis=0, keepdims=True)
 
 
-def block(nt, nz, slots, nbits, *refs):
+def block(nt, nz, slots, *refs):
     (
         live, tok, cot, wq, wk, wv, wo, wh, wd, g1, s1, bq, bv, bo, g2, s2, bd, bh, tab, rel, reg,
         y_all, g_all, fin, tot,
-        xg, cg, gw, vg, rg, dv, rc, ry, rx, r3, rz, scr, syr, sx, small, yb, gb, square, mask, inv,
+        xg, cg, gw, vg, rg, dv, rc, ry, rx, r3, rz, scr, syr, sx, zb, small, yb, gb, square, mask, inv,
         xs, xp, gy, h1, h1t, h2t, gyt, qs, kvs, probs, att, acc, acc2, n1, r1, n2, r2, low, gkv, gq,
         pairs,
         loc, tok_s, tok_r, out_s, out_r, az_s, az_r, ax_s, ax_r, ay_s, ay_r, ac_s, ac_r,
-        bx_s, bx_r, k_s, k_r, p_s, p_r, q_s, q_r, rz_s, rz_r, sm_s, sm_r,
+        bx_s, bx_r, by_s, by_r, cz_s, cz_r, k_s, k_r, p_s, p_r, q_s, q_r, rz_s, rz_r, sm_s, sm_r,
     ) = refs
     heads = LANES // HDIM
     rows = slots * PAD
@@ -97,10 +97,6 @@
     xpeer, ypeer, cpeer = (z * 2 + (1 - x), t), (a, t2), (a, t1)
     zs = [(lax.rem(z + d, nz) * 2 + x, t) for d in range(1, nz)]
     ts = [(a, tt) for tt in (t1, t2, t3)]
-    flips = []
-    for b in range(nbits):
-        bit = 2**b
-        flips.append((a + bit - 2 * bit * lax.rem(lax.div(a, bit), 2), t))
     peers = zs + ts + [xpeer]
     barrier = pltpu.get_barrier_semaphore()
     for peer in peers:
@@ -123,26 +119,41 @@
         peer = ts[d]
         return far(src.at[peer[1]], dst.at[t], out_s.at[i, d], out_r.at[i, d], peer)
 
+    def far_z(d):
+        return lax.rem(z + nz - d, nz)
+
     def az(ch, d):
         ref = gw.at[ch, t, z, x]
         return far(ref, ref, az_s.at[ch, d], az_r.at[ch, d], zs[d])
 
     def ax(ch, d):
-        ref = gw.at[ch, t, lax.rem(z + nz - d, nz), x]
+        ref = gw.at[ch, t, far_z(d), x]
         return far(ref, ref, ax_s.at[ch, d], ax_r.at[ch, d], xpeer)
 
     def ay(ch, d):
-        ref = gw.at[ch, t, lax.rem(z + nz - d, nz)]
+        ref = gw.at[ch, t, far_z(d)] if ch == 0 else gw.at[ch, t, far_z(d), x]
         return far(ref, ref, ay_s.at[ch, d], ay_r.at[ch, d], ypeer)
-
-    def by(ch):
-        ref = gw.at[ch, t, :, x]
-        return far(ref, ref, ay_s.at[ch, 0], ay_r.at[ch, 0], ypeer)
 
     def bx(ch, j):
         ref = gw.at[ch, t2 if j else t, :, x]
         return far(ref, ref, bx_s.at[ch, j], bx_r.at[ch, j], xpeer)
 
+    def by(ch):
+        ref = gw.at[ch, t, :, x]
+        return far(ref, ref, by_s.at[ch], by_r.at[ch], ypeer)
+
+    def cy():
+        ref = gw.at[5, t, z, x]
+        return far(ref, ref, by_s.at[5], by_r.at[5], ypeer)
+
+    def cx(j):
+        ref = gw.at[5, t2 if j else t, z, x]
+        return far(ref, ref, bx_s.at[5, j], bx_r.at[5, j], xpeer)
+
+    def cz(d, j):
+        ref = gw.at[5, t2 if j else t, z]
+        return far(ref, ref, cz_s.at[d, j], cz_r.at[d, j], zs[d])
+
     def ac(ch, j):
         ref = gw.at[ch, t2 if j else t]
         return far(ref, ref, ac_s.at[ch, j], ac_r.at[ch, j], cpeer)
@@ -151,14 +162,17 @@
         return far(dv.at[ch, t1 if j else t3], rc.at[ch, j], k_s.at[ch, j], k_r.at[ch, j], cpeer)
 
     def ya(ch):
-        return far(dv.at[ch, t2], ry.at[ch], p_s.at[ch, 0], p_r.at[ch, 0], ypeer)
+        return far(dv.at[ch, t2], ry.at[ch - 2], p_s.at[ch, 0], p_r.at[ch, 0], ypeer)
 
     def xa(ch):
         return far(dv.at[ch, t, :, 1 - x], r3.at[ch], q_s.at[ch], q_r.at[ch], xpeer)
 
+    def slot_b(ch):
+        return ch if isinstance(ch, int) and ch < 2 else ch - 2
+
     def xb(ch, j):
         src = dv.at[ch, t if j else t2, :, 1 - x]
-        return far(src, rx.at[ch - 4, j], p_s.at[ch, j], p_r.at[ch, j], xpeer)
+        return far(src, rx.at[slot_b(ch), j], p_s.at[ch, j], p_r.at[ch, j], xpeer)
 
     def yb2(ch):
         return far(dv.at[ch, t2, :, x], r3.at[ch], q_s.at[ch], q_r.at[ch], ypeer)
@@ -177,17 +191,24 @@
 
     def second_a(ch):
         ya(ch).wait_recv()
-        dv[ch, t] = add(dv[ch, t], ry[ch])
+        dv[ch, t] = add(dv[ch, t], ry[ch - 2])
         xa(ch).start()
 
+    def first_half(ch):
+        xb(ch, 0).wait_recv()
+        dv[ch, t2, :, x] = add(dv[ch, t2, :, x], rx[slot_b(ch), 0])
+        yb2(ch).start()
+
+    def second_half(ch):
+        xb(ch, 1).wait_recv()
+        dv[ch, t, :, x] = add(dv[ch, t, :, x], rx[slot_b(ch), 1])
+
     def second_b(ch):
-        for j, tt in enumerate((t2, t)):
-            xb(ch, j).wait_recv()
-            dv[ch, tt, :, x] = add(dv[ch, tt, :, x], rx[ch - 4, j])
-        yb2(ch).start()
+        first_half(ch)
+        second_half(ch)
 
     def third(ch):
-        (xa(ch) if ch < 4 else yb2(ch)).wait_recv()
+        (xa(ch) if ch in (2, 3) else yb2(ch)).wait_recv()
         dv[ch, t, :, x] = add(dv[ch, t, :, x], r3[ch])
         for d in range(nz - 1):
             zr(ch, d).start()
@@ -205,39 +226,47 @@
     def small_y():
         return far(sx.at[0], syr.at[0], sm_s.at[2], sm_r.at[2], ypeer)
 
-    def small_flip(b):
-        return far(sx.at[2 + b], syr.at[1 + b], sm_s.at[3 + b], sm_r.at[3 + b], flips[b])
-
-    def flat(value):
-        return value.astype(F32).T.astype(BF16)
+    def small_z(d):
+        return far(zb.at[z], zb.at[z], sm_s.at[3 + d], sm_r.at[3 + d], zs[d])
+
+    def small_x():
+        return far(sx.at[2], syr.at[1], sm_s.at[2 + nz], sm_r.at[2 + nz], xpeer)
 
     gw[0, t, z, x, :, :LANES] = wq[...]
-    gw[0, t, z, x, :, LANES:] = flat(wo[...])
+    gw[0, t, z, x, :, LANES:] = wo[...]
     gw[1, t, z, x, :, :LANES] = wk[...]
     gw[1, t, z, x, :, LANES:] = wv[...]
     for i, ref in enumerate((g1, s1, bq, bv, bo, g2, s2, bd)):
         vg[t, i : i + 1, :] = ref[...]
     vg[t, 8:12, :] = bh[...]
     vg[t, 12:, :] = jnp.zeros((SROWS - 12, LANES), F32)
+    for s in range(2):
+        gw[2 + s, t, z, x] = wh[:, s * CW : (s + 1) * CW]
+        gw[4 + s, t, z, x] = wd[:, s * CW : (s + 1) * CW]
     pl.semaphore_wait(barrier, len(peers))
     own_tok = pltpu.make_async_copy(tok.at[t], xg.at[t], loc.at[0])
     own_cot = pltpu.make_async_copy(cot.at[t], cg.at[t], loc.at[1])
     own_tok.start()
     own_cot.start()
-    for ch in range(2):
+    for d in range(nz - 1):
+        az(0, d).start()
+    for d in range(3):
+        tok_copy(0, d).start()
+    ax(0, 0).start()
+    for d in range(nz - 1):
+        az(1, d).start()
+    for d in range(3):
+        tok_copy(2, d).start()
+    ax(1, 0).start()
+    cy().start()
+    ay(1, 0).start()
+    for ch in (2, 4, 3):
         for d in range(nz - 1):
             az(ch, d).start()
-        ax(ch, 0).start()
-    for d in range(3):
-        tok_copy(0, d).start()
-    for d in range(3):
-        tok_copy(2, d).start()
     square[...] = jnp.zeros_like(square)
-    square[:TABLE, :heads] = tab[...]
-    table = square[...].T
-    square[...] = jnp.zeros_like(square)
+    table = tab[...]
     square[:WT, :WT] = rel[...].astype(F32)
-    rel_t = square[:LANES, :].T[:PAD, :PAD]
+    rel_t = square[...].T[:PAD, :PAD]
     pick_at = jnp.concatenate([rel_t, rel_t], axis=1).astype(jnp.int32)
     lane = lax.broadcasted_iota(jnp.int32, (PAD, LANES), 1)
     low_at, high_at = jnp.minimum(pick_at, LANES - 1), jnp.maximum(pick_at - LANES, 0)
@@ -247,7 +276,10 @@
 
     def entry(h):
         first = jnp.broadcast_to(table[h : h + 1, :LANES], (PAD, LANES))
-        second = jnp.broadcast_to(table[h : h + 1, LANES:], (PAD, LANES))
+        second = jnp.concatenate(
+            [table[h : h + 1, LANES:], jnp.zeros((1, TPAD - TABLE), F32)], axis=1
+        )
+        second = jnp.broadcast_to(second, (PAD, LANES))
         return jnp.where(pick_at < LANES, take(first, low_at), take(second, high_at))
 
     for q in range(heads // 2):
@@ -266,21 +298,17 @@
     square[:slots, :WT] = mine.astype(F32)
     reg_row = square[:slots, :PAD]
     reg_row = jnp.concatenate([reg_row] * heads, axis=1)
-    reg_col = square[:LANES, :].T[:PAD, :slots]
+    reg_col = square[...].T[:PAD, :slots]
     real = lax.broadcasted_iota(jnp.int32, (PAD, heads * PAD), 0) < WT
     for w in range(slots):
         same = reg_col[:, w : w + 1] == reg_row[w : w + 1, :]
         mask[w] = jnp.where(real, jnp.where(same, 0.0, -100.0), -1e30)
-    for s in range(2):
-        gw[2 + s, t, z, x] = wh[:, s * CW : (s + 1) * CW]
-        gw[4 + s, t, z, x] = flat(wd[s * CW : (s + 1) * CW, :])
-    for ch in range(2):
-        for d in range(nz - 1):
-            az(ch, d).wait_recv()
-            ax(ch, d + 1).start()
-    for ch in (2, 4, 3, 5):
-        for d in range(nz - 1):
-            az(ch, d).start()
+    for d in range(nz - 1):
+        az(0, d).wait_recv()
+        ax(0, d + 1).start()
+    cy().wait_recv()
+    for j in range(2):
+        cx(j).start()
 
     def wide(i):
         return jnp.concatenate([vg[tt, i : i + 1, :] for tt in range(nt)], axis=1)
@@ -334,15 +362,19 @@
         return carry
 
     each(start)
-    for ch in range(2):
-        for d in range(nz):
-            ax(ch, d).wait_recv()
-            ay(ch, d).start()
-        ac(ch, 0).start()
+    for d in range(nz - 1):
+        az(1, d).wait_recv()
+        ax(1, d + 1).start()
+        ay(1, d + 1).start()
+    for d in range(nz):
+        ax(0, d).wait_recv()
+        ay(0, d).start()
+    ac(0, 0).start()
     for d in range(3):
         tok_copy(3, d).wait_recv()
-    for d in range(3):
-        tok_copy(1, d).start()
+    for d in range(nz):
+        ax(1, d).wait_recv()
+    ac(1, 0).start()
     lane_head = lax.broadcasted_iota(jnp.int32, (PAD, LANES), 1) // HDIM
     ones = [(lane_head == h).astype(F32).astype(BF16) for h in range(heads)]
 
@@ -357,6 +389,69 @@
 
     acc[...] = jnp.zeros_like(acc)
 
+    def events(i, table):
+        for when, todo in table.items():
+
+            @pl.when(i == when)
+            def _(todo=todo):
+                for act in todo:
+                    act()
+
+    def z_to_xy(ch):
+        for d in range(nz - 1):
+            az(ch, d).wait_recv()
+        bx(ch, 0).start()
+        by(ch).start()
+
+    def y_to_x(ch):
+        by(ch).wait_recv()
+        bx(ch, 1).start()
+
+    def x_to_core(ch, j):
+        bx(ch, j).wait_recv()
+        ac(ch, j).start()
+
+    def ay_to_bx():
+        for d in range(nz):
+            ay(1, d).wait_recv()
+        bx(1, 1).start()
+
+    def start_cz():
+        for j in range(2):
+            cx(j).wait_recv()
+        for d in range(nz - 1):
+            for j in range(2):
+                cz(d, j).start()
+
+    def groups_in():
+        for d in range(nz):
+            ay(0, d).wait_recv()
+        ac(0, 1).start()
+        x_to_core(1, 1)
+
+    def start_cot():
+        for d in range(3):
+            tok_copy(1, d).start()
+
+    def end_cz():
+        for d in range(nz - 1):
+            for j in range(2):
+                cz(d, j).wait_recv()
+        for j in range(2):
+            ac(5, j).start()
+
+    in_first = {
+        0: [ay_to_bx, lambda: z_to_xy(2)],
+        2: [lambda: y_to_x(2), lambda: z_to_xy(3)],
+        3: [lambda: x_to_core(4, 0), lambda: x_to_core(2, 1)],
+    }
+    in_second = {
+        0: [lambda: z_to_xy(4), start_cz],
+        1: [groups_in, start_cot],
+        2: [lambda: y_to_x(4), lambda: x_to_core(2, 0)],
+        3: [lambda: x_to_core(4, 1)],
+    }
+
     def attend(i, carry):
         tt = group(i)
 
@@ -364,13 +459,6 @@
         def _():
             for ch in range(2):
                 ac(ch, 0).wait_recv()
-
-        @pl.when(i == 2)
-        def _():
-            for ch in range(2):
-                for d in range(nz):
-                    ay(ch, d).wait_recv()
-                ac(ch, 1).start()
 
         @pl.when(i == 3)
         def _():
@@ -392,53 +480,18 @@
             att[tt, at, :] = pick(tn_dot(p.astype(BF16), kvs[tt, at, LANES:])).astype(BF16)
             return carry
 
-        lax.fori_loop(0, slots, window, 0, unroll=2)
+        lax.fori_loop(0, slots // 2, window, 0, unroll=2)
+        events(i, in_first)
+        lax.fori_loop(slots // 2, slots, window, 0, unroll=2)
         acc[...] += nt_dot(att[tt], weight(0, tt, LANES, LANES))
-
-        def feed(chs):
-            for ch in chs:
-                for d in range(nz - 1):
-                    az(ch, d).wait_recv()
-                by(ch).start()
-
-        def feed_x(chs):
-            for ch in chs:
-                by(ch).wait_recv()
-                for j in range(2):
-                    bx(ch, j).start()
-
-        @pl.when(i == 0)
-        def _():
-            feed((2, 4))
-
-        @pl.when(i == 1)
-        def _():
-            feed((3, 5))
-
-        @pl.when(i == 2)
-        def _():
-            feed_x((2, 4))
-
-        @pl.when(i == 3)
-        def _():
-            feed_x((3, 5))
-
+        events(i, in_second)
         return carry
 
     lax.fori_loop(0, nt, attend, 0)
-
-    def feed_core(chs):
-        for ch in chs:
-            for j in range(2):
-                bx(ch, j).wait_recv()
-            for j in range(2):
-                ac(ch, j).start()
-
     own_cot.wait()
     for d in range(3):
         tok_copy(1, d).wait_recv()
     spread(cg, gy)
-    feed_core((2, 4))
     b_out, gain2, shift2 = wide(4), wide(5), wide(6)
 
     def live_rows(i):
@@ -467,14 +520,15 @@
         for j in range(2):
             ac(ch, j).wait_recv()
 
+    mlp_events = {
+        0: [lambda: y_to_x(3), lambda: x_to_core(3, 0)],
+        2: [lambda: x_to_core(3, 1), end_cz],
+    }
+
     def mlp(k, carry):
         s, i = lax.div(k, nt), lax.rem(k, nt)
         tt = group(3 - i)
         up, down = 2 + s, 4 + s
-
-        @pl.when(k == 2)
-        def _():
-            feed_core((3, 5))
 
         @pl.when(k == 4)
         def _():
@@ -497,6 +551,8 @@
         put_grad(up, tt, nn(h2t[...], grad_low))
         acc2[...] += nt_dot(grad_low, weight(up, tt))
 
+        events(k, mlp_events)
+
         @pl.when(i == 0)
         def _():
             kc(down, 0).start()
@@ -524,7 +580,6 @@
 
     lax.fori_loop(0, 2 * nt, mlp, 0)
     second_a(2)
-    second_b(4)
     b_down = wide(7)
     zero_row = jnp.zeros((1, C), F32)
 
@@ -546,9 +601,34 @@
     gather(xp, yb)
     own_y = pltpu.make_async_copy(yb.at[t], y_all.at[t], loc.at[2])
     own_y.start()
-    for d in range(3):
-        out_copy(0, d).start()
+    second_b(4)
     acc[...] = jnp.zeros_like(acc)
+
+    def start_y():
+        for d in range(3):
+            out_copy(0, d).start()
+
+    def core_zero():
+        for ch in range(2):
+            core_first(ch)
+            xb(ch, 0).start()
+
+    def core_one():
+        for ch in range(2):
+            core_second(ch)
+            xb(ch, 1).start()
+
+    out_first = {
+        1: [lambda: third(4)],
+        2: [lambda: third(3)],
+        3: [lambda: first_half(0), lambda: first_half(1)],
+    }
+    out_second = {
+        0: [lambda: second_a(3)],
+        1: [lambda: third(2), core_zero, lambda: second_b(5), start_y],
+        2: [lambda: third(5), lambda: fourth(2), lambda: fourth(4)],
+        3: [core_one],
+    }
 
     def back(i, carry):
         tt = group(3 - i)
@@ -569,7 +649,9 @@
             gatt[at, :] = pick(tn_dot(ds_low, kvs[tt, at, :LANES])).astype(BF16)
             return carry
 
-        lax.fori_loop(0, slots, window, 0, unroll=2)
+        lax.fori_loop(0, slots // 2, window, 0, unroll=2)
+        events(i, out_first)
+        lax.fori_loop(slots // 2, slots, window, 0, unroll=2)
         gk_gv = gkv[:, :CW]
         put_grad(1, tt, nn(h1t[...], gk_gv))
         left = nn(h1t[...], gatt[...]) * SCALE
@@ -598,31 +680,7 @@
                 value = jnp.where(where >= 0, value, 0.0)
                 small[tt, pl.ds(12 + 2 * h + q, 1), :] = rowsum(value)
 
-        @pl.when(i == 0)
-        def _():
-            third(2)
-            third(4)
-
-        @pl.when(i == 1)
-        def _():
-            for ch in range(2):
-                core_first(ch)
-                ya(ch).start()
-            second_a(3)
-            second_b(5)
-
-        @pl.when(i == 2)
-        def _():
-            third(3)
-            third(5)
-            fourth(2)
-            fourth(4)
-
-        @pl.when(i == 3)
-        def _():
-            for ch in range(2):
-                core_second(ch)
-
+        events(i, out_second)
         return carry
 
     lax.fori_loop(0, nt, back, 0)
@@ -638,47 +696,55 @@
     put_small(1, sums[1])
     for j in range(2):
         small_core(j).start()
-    second_a(0)
     gather(xp, gb)
     own_g = pltpu.make_async_copy(gb.at[t], g_all.at[t], loc.at[3])
     own_g.start()
-    for d in range(3):
-        out_copy(1, d).start()
     for j in range(2):
         small_core(j).wait_recv()
     sx[0] = small[t2] + scr[0]
     sx[1] = small[t] + scr[1]
     small_y().start()
-    second_a(1)
+    for d in range(3):
+        out_copy(1, d).start()
+    fourth(3)
+    fourth(5)
     small_y().wait_recv()
-    sx[2] = sx[1] + syr[0]
-    small_flip(0).start()
-    fourth(3)
+    zb[z] = sx[1] + syr[0]
+    for d in range(nz - 1):
+        small_z(d).start()
+    second_half(0)
     third(0)
+    for d in range(nz - 1):
+        small_z(d).wait_recv()
+    value = zb[0]
+    for zz in range(1, nz):
+        value = value + zb[zz]
+    sx[2] = value
+    small_x().start()
+    second_half(1)
     third(1)
-    fourth(5)
-    for b in range(nbits):
-        small_flip(b).wait_recv()
-        sx[3 + b] = sx[2 + b] + syr[1 + b]
-        if b + 1 < nbits:
-            small_flip(b + 1).start()
+    small_x().wait_recv()
+    tot[...] = sx[2] + syr[1]
     fourth(0)
     fourth(1)
-    tot[...] = sx[2 + nbits]
     for i in range(2):
         for d in range(3):
             out_copy(i, d).wait_recv()
     sent = [tok_copy(i, d) for i in range(4) for d in range(3)]
     sent += [out_copy(i, d) for i in range(2) for d in range(3)]
     for ch in range(NCH):
-        sent += [az(ch, d) for d in range(nz - 1)] + [zr(ch, d) for d in range(nz - 1)]
+        sent += [zr(ch, d) for d in range(nz - 1)]
         sent += [ac(ch, j) for j in range(2)] + [kc(ch, j) for j in range(2)]
+        sent += [az(ch, d) for d in range(nz - 1)] if ch < 5 else [cy(), cx(0), cx(1)]
         if ch < 2:
             sent += [ax(ch, d) for d in range(nz)] + [ay(ch, d) for d in range(nz)]
-        else:
+            sent += [bx(1, 1)] if ch == 1 else []
+        elif ch < 5:
             sent += [by(ch), bx(ch, 0), bx(ch, 1)]
-        sent += [ya(ch), xa(ch)] if ch < 4 else [xb(ch, 0), xb(ch, 1), yb2(ch)]
-    sent += [small_core(0), small_core(1), small_y()] + [small_flip(b) for b in range(nbits)]
+        sent += [ya(ch), xa(ch)] if ch in (2, 3) else [xb(ch, 0), xb(ch, 1), yb2(ch)]
+    sent += [cz(d, j) for d in range(nz - 1) for j in range(2)]
+    sent += [small_core(0), small_core(1), small_y(), small_x()]
+    sent += [small_z(d) for d in range(nz - 1)]
     for copy in sent:
         copy.wait_send()
     own_y.wait()
@@ -686,10 +752,9 @@
 
 
 def block_call(nt, nz, slots, *args):
-    tok, deep, heads = args[1], args[3].shape[0], args[18].shape[1]
+    tok, deep, heads = args[1], args[3].shape[0], args[18].shape[0]
     real = tok.shape[1]
     rows, wide = slots * PAD, heads * PAD
-    nbits = (2 * nz - 1).bit_length()
     piece = (nz, 2, deep, CW)
     row = (nt, real, LANES)
 
@@ -701,7 +766,7 @@
 
     small = (SROWS, LANES)
     return pl.pallas_call(
-        functools.partial(block, nt, nz, slots, nbits),
+        functools.partial(block, nt, nz, slots),
         name="block",
         out_shape=(
             jax.ShapeDtypeStruct(row, BF16),
@@ -719,17 +784,18 @@
             vm((nt, PAD, wide), F32),
             vm((NCH, nt) + piece),
             vm((NCH, 2) + piece),
-            vm((4,) + piece),
-            vm((2, 2, nz, deep, CW)),
+            vm((2,) + piece),
+            vm((4, 2, nz, deep, CW)),
             vm((NCH, nz, deep, CW)),
             vm((NCH, nz - 1, deep, CW)),
             vm((2,) + small, F32),
-            vm((1 + nbits,) + small, F32),
-            vm((3 + nbits,) + small, F32),
+            vm((2,) + small, F32),
+            vm((3,) + small, F32),
+            vm((nz,) + small, F32),
             vm((nt,) + small, F32),
             vm(row),
             vm(row),
-            vm((TPAD, LANES), F32),
+            vm((LANES, LANES), F32),
             vm((slots, PAD, wide), F32),
             vm((PAD, TPAD), jnp.int32),
             vm((real, C), F32),
@@ -759,14 +825,16 @@
         + pair(2, 3)
         + pair(NCH, nz - 1)
         + pair(2, nz)
-        + pair(NCH, nz)
+        + pair(2, nz)
         + pair(NCH, 2)
         + pair(NCH, 2)
+        + pair(NCH)
+        + pair(nz - 1, 2)
         + pair(NCH, 2)
         + pair(NCH, 2)
         + pair(NCH)
         + pair(NCH, nz - 1)
-        + pair(3 + nbits),
+        + pair(3 + nz),
         compiler_params=pltpu.CompilerParams(
             collective_id=0, has_side_effects=True, vmem_limit_bytes=60 * 2**20
         ),
@@ -783,20 +851,16 @@
     d_wq[...] = fin[0, :, :LANES]
     d_wk[...] = fin[1, :, :LANES]
     d_wv[...] = fin[1, :, LANES:]
-    d_wo[...] = fin[0, :, LANES:].T
+    d_wo[...] = fin[0, :, LANES:]
     for s in range(2):
         d_wh[:, s * CW : (s + 1) * CW] = fin[2 + s]
-        d_wd[s * CW : (s + 1) * CW, :] = fin[4 + s].T
+        d_wd[:, s * CW : (s + 1) * CW] = fin[4 + s]
     for i, ref in enumerate((d_g1, d_s1, d_bq, d_bv, d_bo, d_g2, d_s2, d_bd)):
         ref[...] = tot[i : i + 1, :]
     d_bh[...] = tot[8:12, :]
-    heads = d_tab.shape[1]
-    table = [
-        jnp.concatenate([tot[12 + 2 * h : 13 + 2 * h], tot[13 + 2 * h : 14 + 2 * h]], axis=1)
-        for h in range(heads)
-    ]
-    table = jnp.concatenate(table + [jnp.zeros((8 - heads, TPAD), F32)], axis=0).T
-    d_tab[...] = table[:TABLE, :heads]
+    for h in range(d_tab.shape[0]):
+        d_tab[h : h + 1, :LANES] = tot[12 + 2 * h : 13 + 2 * h]
+        d_tab[h : h + 1, LANES:] = tot[13 + 2 * h : 14 + 2 * h, : TABLE - LANES]
 
 
 def spell_call(outs, *args):
@@ -806,7 +870,7 @@
         out_shape=outs,
         in_specs=[VM] * 4,
         out_specs=(VM,) * len(outs),
-        compiler_params=pltpu.CompilerParams(vmem_limit_bytes=24 * 2**20),
+        compiler_params=pltpu.CompilerParams(vmem_limit_bytes=60 * 2**20),
     )(*args)
 
 
@@ -821,9 +885,9 @@
     parts = block_call(
         nt, na // 2, slots,
         win_count, tokens.reshape(cut), cotangent.reshape(cut),
-        w_query, w_key, w_value, w_out, w_hidden, w_down,
+        w_query, w_key, w_value, w_out.T, w_hidden, w_down.T,
         *[v.reshape(1, LANES) for v in vectors],
-        b_hidden.reshape(-1, LANES), bias_table, rel_index, region,
+        b_hidden.reshape(-1, LANES), bias_table.T, rel_index, region,
     )
 
     def out(like, shape=None):
@@ -832,17 +896,21 @@
     one = (1, LANES)
     shapes = (
         out(tokens, cut), out(tokens, cut), out(gain_one, one), out(gain_one, one), out(w_query),
-        out(w_key), out(w_value), out(b_query, one), out(b_value, one), out(w_out),
+        out(w_key), out(w_value), out(b_query, one), out(b_value, one), out(w_out, w_out.shape[::-1]),
         out(b_out, one), out(gain_two, one), out(shift_two, one), out(w_hidden),
-        out(b_hidden, (b_hidden.shape[0] // LANES, LANES)), out(w_down), out(b_down, one),
-        out(bias_table),
+        out(b_hidden, (b_hidden.shape[0] // LANES, LANES)), out(w_down, w_down.shape[::-1]),
+        out(b_down, one), out(bias_table, bias_table.shape[::-1]),
     )
     likes = (
         tokens, tokens, gain_one, gain_one, w_query, w_key, w_value, b_query, b_value, w_out,
         b_out, gain_two, shift_two, w_hidden, b_hidden, w_down, b_down, bias_table,
     )
     values = spell_call(shapes, *parts)
-    return tuple(v.reshape(like.shape) for v, like in zip(values, likes))
+    turned = (9, 15, 17)
+    return tuple(
+        v.T if i in turned else v.reshape(like.shape)
+        for i, (v, like) in enumerate(zip(values, likes))
+    )
 
 
 def solution(mesh):

time: 133 us -> 99 us (0.74)
  Pallas kernels: 124 us -> 97.5 us
  local copies, waits for them, and re-layouts: 8.12 us -> 0 us
    pallas_call x1, Pallas kernels: 122 us -> 94.9 us  [block_call(): pl.pallas_call(functools.partial(block, nt, nz, slots), name='block', out...]
    unnamed x20 -> x0, local copies, waits for them, and re-layouts: 8.12 us -> none
where the time goes in v3:
time: 99 us; the launch traced here: 98.8 us
  Pallas kernels  97.5 us (98%)
  between operations  1.32 us (1%)
    pallas_call x1, Pallas kernels, block_call(): pl.pallas_call(functools.partial(block, nt, nz, slots), name='block', out...  94.9 us
    pallas_call x1, Pallas kernels, spell_call(): pl.pallas_call(spell, name='spell', out_shape=outs, in_specs=[VM] * 4, ou...  2.63 us

profile of v3, /device:TPU:0, one launch (start us, length us, event | category | flops | bytes accessed | tf_op | source)
XLA Modules:
  0.0 98.8 jit_solution(11417199536938518397)
XLA Ops:
  1.3 94.9 %block.1 = (bf16[4,392,128]{2,1,0:T(8,128)(2,1)}, bf16[4,392,128]{2,1,0:T(8,128)(2,1)}, f32[6,64,256]{2,1,0:T(8,128)}, f32[24,128]{1,0:T(8,128)}) custom-call(s32[1]{0:T(128)S(6)} %copy.39.refs_0_, bf16[4,392,128]{2,1,0:T(8,128)(2,1)} %bitcast.28, bf16[4,392,128]{2,1,0:T(8,128)(2,1)} %bitcast.29, bf16[64,128]{1,0:T(8,128)(2,1)} %refs_3_.1, ...), custom_call_target="tpu_custom_call" | custom-call | tf_op jit(solution)/shard_map/block/pallas_call | solution.py:768
  96.2 2.6 %spell.1 = (f32[4,392,128]{2,1,0:T(8,128)}, f32[4,392,128]{2,1,0:T(8,128)}, f32[1,128]{1,0:T(1,128)}, f32[1,128]{1,0:T(1,128)}, f32[64,128]{1,0:T(8,128)}, /*ind...) custom-call(bf16[4,392,128]{2,1,0:T(8,128)(2,1)} %get-tuple-element., ...), custom_call_target="tpu_custom_call" | custom-call | tf_op jit(solution)/shard_map/spell/pallas_call | solution.py:867

commit v4 on v3

--- a/solution.py
+++ b/solution.py
@@ -75,11 +75,12 @@
     (
         live, tok, cot, wq, wk, wv, wo, wh, wd, g1, s1, bq, bv, bo, g2, s2, bd, bh, tab, rel, reg,
         y_all, g_all, fin, tot,
-        xg, cg, gw, vg, rg, dv, rc, ry, rx, r3, rz, scr, syr, sx, zb, small, yb, gb, square, mask, inv,
+        xg, cg, gw, vg, rg, dv, rc, ry, rx, r3, rz, rzc, rxc, scr, syr, sx, zb, small, yb, gb, square, mask, inv,
         xs, xp, gy, h1, h1t, h2t, gyt, qs, kvs, probs, att, acc, acc2, n1, r1, n2, r2, low, gkv, gq,
         pairs,
-        loc, tok_s, tok_r, out_s, out_r, az_s, az_r, ax_s, ax_r, ay_s, ay_r, ac_s, ac_r,
-        bx_s, bx_r, by_s, by_r, cz_s, cz_r, k_s, k_r, p_s, p_r, q_s, q_r, rz_s, rz_r, sm_s, sm_r,
+        loc, tok_s, tok_r, out_s, out_r, ln_s, ln_r, az_s, az_r, ax_s, ax_r, ay_s, ay_r, ac_s, ac_r,
+        bx_s, bx_r, by_s, by_r, cz_s, cz_r, px_s, px_r, zc_s, zc_r, xc_s,
+        xc_r, k_s, k_r, p_s, p_r, q_s, q_r, rz_s, rz_r, sm_s, sm_r,
     ) = refs
     heads = LANES // HDIM
     rows = slots * PAD
@@ -109,7 +110,7 @@
         )
 
     def tok_copy(i, d):
-        src, dst = ((tok, xg), (cot, cg), (vg, vg), (rg, rg))[i]
+        src, dst = ((tok, xg), (cot, cg), (vg, vg))[i]
         peer = ts[d]
         src = src.at[peer[1]] if i < 2 else src.at[t]
         return far(src, dst.at[t], tok_s.at[i, d], tok_r.at[i, d], peer)
@@ -119,20 +120,71 @@
         peer = ts[d]
         return far(src.at[peer[1]], dst.at[t], out_s.at[i, d], out_r.at[i, d], peer)
 
-    def far_z(d):
-        return lax.rem(z + nz - d, nz)
-
     def az(ch, d):
         ref = gw.at[ch, t, z, x]
         return far(ref, ref, az_s.at[ch, d], az_r.at[ch, d], zs[d])
 
-    def ax(ch, d):
-        ref = gw.at[ch, t, far_z(d), x]
-        return far(ref, ref, ax_s.at[ch, d], ax_r.at[ch, d], xpeer)
-
-    def ay(ch, d):
-        ref = gw.at[ch, t, far_z(d)] if ch == 0 else gw.at[ch, t, far_z(d), x]
-        return far(ref, ref, ay_s.at[ch, d], ay_r.at[ch, d], ypeer)
+    def far_first(k):
+        rising = k + jnp.where(z > k, 0, 1)
+        falling = nz - 1 - k - jnp.where(z < nz - 1 - k, 0, 1)
+        zz = jnp.where(2 * z < nz, falling, rising)
+        return zz, lax.rem(zz - z + nz, nz) - 1
+
+    def line(ch, zz, up):
+        ref = gw.at[ch, t, zz, x]
+        there = (lax.rem(z + nz + (1 if up else -1), nz) * 2 + x, t)
+        return far(ref, ref, ln_s.at[ch, up, zz], ln_r.at[ch, zz], there)
+
+    def pass_on(ch, zz):
+        @pl.when((zz <= z) & (z < nz - 1))
+        def _():
+            line(ch, zz, 1).start()
+
+        @pl.when((zz >= z) & (z > 0))
+        def _():
+            line(ch, zz, 0).start()
+
+        ax(ch, zz).start()
+        if ch == 1:
+            ay(ch, zz).start()
+
+    def line_step(ch, step):
+        for zz, there in ((z - step, z >= step), (z + step, z + step < nz)):
+
+            @pl.when(there)
+            def _(zz=zz):
+                line(ch, zz, 0).wait_recv()
+                pass_on(ch, zz)
+
+    def line_sent(ch):
+        for zz in range(nz):
+
+            @pl.when((zz <= z) & (z < nz - 1))
+            def _(zz=zz):
+                line(ch, zz, 1).wait_send()
+
+            @pl.when((zz >= z) & (z > 0))
+            def _(zz=zz):
+                line(ch, zz, 0).wait_send()
+
+    def az_start(ch):
+        ref = gw.at[ch, t, z, x]
+        for k in range(nz - 1):
+            zz, d = far_first(k)
+            far(ref, ref, az_s.at[ch, d], az_r.at[ch, d], (zz * 2 + x, t)).start()
+
+    def zr_start(ch, k):
+        zz, d = far_first(k)
+        src = dv.at[ch, t, zz, x]
+        far(src, rz.at[ch, d], rz_s.at[ch, d], rz_r.at[ch, d], (zz * 2 + x, t)).start()
+
+    def ax(ch, zz):
+        ref = gw.at[ch, t, zz, x]
+        return far(ref, ref, ax_s.at[ch, zz], ax_r.at[ch, zz], xpeer)
+
+    def ay(ch, zz):
+        ref = gw.at[ch, t, zz] if ch == 0 else gw.at[ch, t, zz, x]
+        return far(ref, ref, ay_s.at[ch, zz], ay_r.at[ch, zz], ypeer)
 
     def bx(ch, j):
         ref = gw.at[ch, t2 if j else t, :, x]
@@ -167,8 +219,53 @@
     def xa(ch):
         return far(dv.at[ch, t, :, 1 - x], r3.at[ch], q_s.at[ch], q_r.at[ch], xpeer)
 
+    def zc(d, j):
+        src = dv.at[5, t if j else t2, lax.rem(z + d + 1, nz)]
+        return far(src, rzc.at[d, j], zc_s.at[d, j], zc_r.at[d, j], zs[d])
+
+    def xc(j):
+        src = dv.at[5, t if j else t2, z, 1 - x]
+        return far(src, rxc.at[j], xc_s.at[j], xc_r.at[j], xpeer)
+
+    def yc():
+        return far(dv.at[5, t2, z, x], rxc.at[2], xc_s.at[2], xc_r.at[2], ypeer)
+
+    def c_start():
+        for k in range(nz - 1):
+            zz, d = far_first(k)
+            for j in range(2):
+                src = dv.at[5, t if j else t2, zz]
+                far(src, rzc.at[d, j], zc_s.at[d, j], zc_r.at[d, j], (zz * 2 + x, t)).start()
+
+    def c_sum():
+        for j, tt in enumerate((t2, t)):
+            value = dv[5, tt, z].astype(F32)
+            for d in range(nz - 1):
+                zc(d, j).wait_recv()
+                value = value + rzc[d, j].astype(F32)
+            dv[5, tt, z] = value.astype(BF16)
+            xc(j).start()
+
+    def c_x():
+        for j, tt in enumerate((t2, t)):
+            xc(j).wait_recv()
+            dv[5, tt, z, x] = add(dv[5, tt, z, x], rxc[j])
+        yc().start()
+
+    def c_end():
+        yc().wait_recv()
+        fin[5] = dv[5, t, z, x].astype(F32) + rxc[2].astype(F32)
+
     def slot_b(ch):
         return ch if isinstance(ch, int) and ch < 2 else ch - 2
+
+    def piece_of(d):
+        return far_first(d)[0] if d < nz - 1 else z
+
+    def xp1(ch, d):
+        zz = piece_of(d)
+        src, dst = dv.at[ch, t, zz, 1 - x], rx.at[slot_b(ch), 1, zz]
+        return far(src, dst, px_s.at[ch, d], px_r.at[ch, d], xpeer)
 
     def xb(ch, j):
         src = dv.at[ch, t if j else t2, :, 1 - x]
@@ -210,8 +307,23 @@
     def third(ch):
         (xa(ch) if ch in (2, 3) else yb2(ch)).wait_recv()
         dv[ch, t, :, x] = add(dv[ch, t, :, x], r3[ch])
-        for d in range(nz - 1):
-            zr(ch, d).start()
+        for k in range(nz - 1):
+            zr_start(ch, k)
+
+    def last_out(ch):
+        core_second(ch)
+        for d in range(nz):
+            xp1(ch, d).start()
+
+    def last_third(ch):
+        yb2(ch).wait_recv()
+        for d in range(nz):
+            zz = piece_of(d)
+            xp1(ch, d).wait_recv()
+            value = dv[ch, t, zz, x].astype(F32) + rx[slot_b(ch), 1, zz].astype(F32)
+            dv[ch, t, zz, x] = (value + r3[ch, zz].astype(F32)).astype(BF16)
+            if d < nz - 1:
+                zr_start(ch, d)
 
     def fourth(ch):
         value = dv[ch, t, z, x].astype(F32)
@@ -220,17 +332,14 @@
             value = value + rz[ch, d].astype(F32)
         fin[ch] = value
 
-    def small_core(j):
-        return far(small.at[t1 if j else t3], scr.at[j], sm_s.at[j], sm_r.at[j], cpeer)
-
-    def small_y():
-        return far(sx.at[0], syr.at[0], sm_s.at[2], sm_r.at[2], ypeer)
+    def small_t(d):
+        return far(small.at[ts[d][1]], scr.at[d], sm_s.at[d], sm_r.at[d], ts[d])
 
     def small_z(d):
         return far(zb.at[z], zb.at[z], sm_s.at[3 + d], sm_r.at[3 + d], zs[d])
 
     def small_x():
-        return far(sx.at[2], syr.at[1], sm_s.at[2 + nz], sm_r.at[2 + nz], xpeer)
+        return far(sx, syr, sm_s.at[2 + nz], sm_r.at[2 + nz], xpeer)
 
     gw[0, t, z, x, :, :LANES] = wq[...]
     gw[0, t, z, x, :, LANES:] = wo[...]
@@ -239,7 +348,11 @@
     for i, ref in enumerate((g1, s1, bq, bv, bo, g2, s2, bd)):
         vg[t, i : i + 1, :] = ref[...]
     vg[t, 8:12, :] = bh[...]
-    vg[t, 12:, :] = jnp.zeros((SROWS - 12, LANES), F32)
+    for h in range(heads):
+        vg[t, 12 + 2 * h : 13 + 2 * h, :] = tab[h : h + 1, :LANES]
+        vg[t, 13 + 2 * h : 14 + 2 * h, : TABLE - LANES] = tab[h : h + 1, LANES:]
+        vg[t, 13 + 2 * h : 14 + 2 * h, TABLE - LANES :] = jnp.zeros((1, TPAD - TABLE), F32)
+    vg[t, 12 + 2 * heads :, :] = jnp.zeros((SROWS - 12 - 2 * heads, LANES), F32)
     for s in range(2):
         gw[2 + s, t, z, x] = wh[:, s * CW : (s + 1) * CW]
         gw[4 + s, t, z, x] = wd[:, s * CW : (s + 1) * CW]
@@ -248,23 +361,14 @@
     own_cot = pltpu.make_async_copy(cot.at[t], cg.at[t], loc.at[1])
     own_tok.start()
     own_cot.start()
-    for d in range(nz - 1):
-        az(0, d).start()
+    for d in range(3):
+        tok_copy(2, d).start()
+    pass_on(1, z)
+    pass_on(0, z)
     for d in range(3):
         tok_copy(0, d).start()
-    ax(0, 0).start()
-    for d in range(nz - 1):
-        az(1, d).start()
-    for d in range(3):
-        tok_copy(2, d).start()
-    ax(1, 0).start()
     cy().start()
-    ay(1, 0).start()
-    for ch in (2, 4, 3):
-        for d in range(nz - 1):
-            az(ch, d).start()
     square[...] = jnp.zeros_like(square)
-    table = tab[...]
     square[:WT, :WT] = rel[...].astype(F32)
     rel_t = square[...].T[:PAD, :PAD]
     pick_at = jnp.concatenate([rel_t, rel_t], axis=1).astype(jnp.int32)
@@ -274,20 +378,17 @@
     def take(value, at):
         return jnp.take_along_axis(value, at, axis=1, mode="promise_in_bounds")
 
-    def entry(h):
-        first = jnp.broadcast_to(table[h : h + 1, :LANES], (PAD, LANES))
-        second = jnp.concatenate(
-            [table[h : h + 1, LANES:], jnp.zeros((1, TPAD - TABLE), F32)], axis=1
-        )
-        second = jnp.broadcast_to(second, (PAD, LANES))
+    def entry(tt, h):
+        first = jnp.broadcast_to(vg[tt, 12 + 2 * h : 13 + 2 * h, :], (PAD, LANES))
+        second = jnp.broadcast_to(vg[tt, 13 + 2 * h : 14 + 2 * h, :], (PAD, LANES))
         return jnp.where(pick_at < LANES, take(first, low_at), take(second, high_at))
 
-    for q in range(heads // 2):
-        rg[t, :, q * LANES : (q + 1) * LANES] = jnp.where(
-            lane < PAD, entry(2 * q), entry(2 * q + 1)
-        )
-    for d in range(3):
-        tok_copy(3, d).start()
+    def bias_of(tt):
+        for q in range(heads // 2):
+            rg[tt, :, q * LANES : (q + 1) * LANES] = jnp.where(
+                lane < PAD, entry(tt, 2 * q), entry(tt, 2 * q + 1)
+            )
+
     number = lax.broadcasted_iota(jnp.int32, (PAD, TPAD), 1).astype(F32)
     found = jnp.full((PAD, TPAD), -1.0, F32)
     for i in range(WT):
@@ -303,9 +404,11 @@
     for w in range(slots):
         same = reg_col[:, w : w + 1] == reg_row[w : w + 1, :]
         mask[w] = jnp.where(real, jnp.where(same, 0.0, -100.0), -1e30)
-    for d in range(nz - 1):
-        az(0, d).wait_recv()
-        ax(0, d + 1).start()
+    for step in range(1, nz):
+        line_step(1, step)
+        line_step(0, step)
+    az_start(2)
+    az_start(4)
     cy().wait_recv()
     for j in range(2):
         cx(j).start()
@@ -343,10 +446,61 @@
     def put_grad(ch, tt, value):
         dv[ch, tt] = value.astype(BF16).reshape(dv.shape[2:])
 
+    def events(i, table):
+        for when, todo in table.items():
+
+            @pl.when(i == when)
+            def _(todo=todo):
+                for act in todo:
+                    act()
+
+    def z_to_xy(ch):
+        for d in range(nz - 1):
+            az(ch, d).wait_recv()
+        bx(ch, 0).start()
+        by(ch).start()
+
+    def y_to_x(ch):
+        by(ch).wait_recv()
+        bx(ch, 1).start()
+
+    def x_to_core(ch, j):
+        bx(ch, j).wait_recv()
+        ac(ch, j).start()
+
+    def ay_to_bx():
+        for d in range(nz):
+            ay(1, d).wait_recv()
+        bx(1, 1).start()
+
+    def start_cz():
+        for j in range(2):
+            cx(j).wait_recv()
+        for d in range(nz - 1):
+            for j in range(2):
+                cz(d, j).start()
+
+    def groups_in():
+        for d in range(nz):
+            ay(0, d).wait_recv()
+        ac(0, 1).start()
+        x_to_core(1, 1)
+
+    def start_cot():
+        for d in range(3):
+            tok_copy(1, d).start()
+
+    def end_cz():
+        for d in range(nz - 1):
+            for j in range(2):
+                cz(d, j).wait_recv()
+        for j in range(2):
+            ac(5, j).start()
+
     n_live = live[0] - t * slots
     small[...] = jnp.zeros_like(small)
     own_tok.wait()
-    for i in (0, 2):
+    for i in (2, 0):
         for d in range(3):
             tok_copy(i, d).wait_recv()
     spread(xg, xp)
@@ -362,19 +516,16 @@
         return carry
 
     each(start)
-    for d in range(nz - 1):
-        az(1, d).wait_recv()
-        ax(1, d + 1).start()
-        ay(1, d + 1).start()
+    for tt in range(nt):
+        bias_of(tt)
+    for d in range(nz):
+        ax(1, d).wait_recv()
+    ac(1, 0).start()
     for d in range(nz):
         ax(0, d).wait_recv()
         ay(0, d).start()
     ac(0, 0).start()
-    for d in range(3):
-        tok_copy(3, d).wait_recv()
-    for d in range(nz):
-        ax(1, d).wait_recv()
-    ac(1, 0).start()
+    z_to_xy(2)
     lane_head = lax.broadcasted_iota(jnp.int32, (PAD, LANES), 1) // HDIM
     ones = [(lane_head == h).astype(F32).astype(BF16) for h in range(heads)]
 
@@ -389,67 +540,17 @@
 
     acc[...] = jnp.zeros_like(acc)
 
-    def events(i, table):
-        for when, todo in table.items():
-
-            @pl.when(i == when)
-            def _(todo=todo):
-                for act in todo:
-                    act()
-
-    def z_to_xy(ch):
-        for d in range(nz - 1):
-            az(ch, d).wait_recv()
-        bx(ch, 0).start()
-        by(ch).start()
-
-    def y_to_x(ch):
-        by(ch).wait_recv()
-        bx(ch, 1).start()
-
-    def x_to_core(ch, j):
-        bx(ch, j).wait_recv()
-        ac(ch, j).start()
-
-    def ay_to_bx():
-        for d in range(nz):
-            ay(1, d).wait_recv()
-        bx(1, 1).start()
-
-    def start_cz():
-        for j in range(2):
-            cx(j).wait_recv()
-        for d in range(nz - 1):
-            for j in range(2):
-                cz(d, j).start()
-
-    def groups_in():
-        for d in range(nz):
-            ay(0, d).wait_recv()
-        ac(0, 1).start()
-        x_to_core(1, 1)
-
-    def start_cot():
-        for d in range(3):
-            tok_copy(1, d).start()
-
-    def end_cz():
-        for d in range(nz - 1):
-            for j in range(2):
-                cz(d, j).wait_recv()
-        for j in range(2):
-            ac(5, j).start()
-
     in_first = {
-        0: [ay_to_bx, lambda: z_to_xy(2)],
-        2: [lambda: y_to_x(2), lambda: z_to_xy(3)],
-        3: [lambda: x_to_core(4, 0), lambda: x_to_core(2, 1)],
+        0: [ay_to_bx, lambda: az_start(3)],
+        1: [start_cz],
+        2: [lambda: y_to_x(2)],
+        3: [lambda: y_to_x(4), lambda: z_to_xy(3)],
     }
     in_second = {
-        0: [lambda: z_to_xy(4), start_cz],
+        0: [lambda: z_to_xy(4)],
         1: [groups_in, start_cot],
-        2: [lambda: y_to_x(4), lambda: x_to_core(2, 0)],
-        3: [lambda: x_to_core(4, 1)],
+        2: [lambda: x_to_core(2, 0), lambda: x_to_core(4, 0)],
+        3: [lambda: x_to_core(2, 1)],
     }
 
     def attend(i, carry):
@@ -480,9 +581,9 @@
             att[tt, at, :] = pick(tn_dot(p.astype(BF16), kvs[tt, at, LANES:])).astype(BF16)
             return carry
 
-        lax.fori_loop(0, slots // 2, window, 0, unroll=2)
+        lax.fori_loop(0, slots // 2, window, 0, unroll=4)
         events(i, in_first)
-        lax.fori_loop(slots // 2, slots, window, 0, unroll=2)
+        lax.fori_loop(slots // 2, slots, window, 0, unroll=4)
         acc[...] += nt_dot(att[tt], weight(0, tt, LANES, LANES))
         events(i, in_second)
         return carry
@@ -516,25 +617,36 @@
     each(middle)
     acc[...] = jnp.zeros_like(acc)
     acc2[...] = jnp.zeros_like(acc2)
-    for ch in (2, 4):
+    def from_core(chs, j):
+        for ch in chs:
+            ac(ch, j).wait_recv()
+
+    def sums_out():
+        core_first(2)
+        ya(2).start()
+        core_first(4)
         for j in range(2):
-            ac(ch, j).wait_recv()
-
-    mlp_events = {
-        0: [lambda: y_to_x(3), lambda: x_to_core(3, 0)],
-        2: [lambda: x_to_core(3, 1), end_cz],
+            xb(4, j).start()
+
+    mlp_before = {
+        1: [lambda: from_core((2, 4), 0)],
+        3: [lambda: from_core((2, 4), 1)],
+        5: [lambda: from_core((3, 5), 0)],
+        7: [lambda: from_core((3, 5), 1)],
+    }
+    mlp_after = {
+        0: [lambda: x_to_core(4, 1)],
+        1: [lambda: y_to_x(3), lambda: x_to_core(3, 0)],
+        2: [end_cz],
+        4: [lambda: core_second(2), lambda: core_second(4)],
+        5: [sums_out, lambda: x_to_core(3, 1)],
     }
 
     def mlp(k, carry):
         s, i = lax.div(k, nt), lax.rem(k, nt)
-        tt = group(3 - i)
+        tt = group(i)
         up, down = 2 + s, 4 + s
-
-        @pl.when(k == 4)
-        def _():
-            for ch in (3, 5):
-                for j in range(2):
-                    ac(ch, j).wait_recv()
+        events(k, mlp_before)
 
         bias = vg[tt, pl.ds(8 + 2 * s, 2), :]
         bias = jnp.concatenate([bias[0:1], bias[1:2]], axis=1)
@@ -551,35 +663,17 @@
         put_grad(up, tt, nn(h2t[...], grad_low))
         acc2[...] += nt_dot(grad_low, weight(up, tt))
 
-        events(k, mlp_events)
-
-        @pl.when(i == 0)
-        def _():
-            kc(down, 0).start()
-            kc(up, 0).start()
-
-        @pl.when(i == 1)
-        def _():
-            core_first(up)
-            ya(up).start()
-            core_first(down)
-
-        @pl.when(i == 2)
-        def _():
-            kc(down, 1).start()
-            kc(up, 1).start()
-
-        @pl.when(i == 3)
-        def _():
-            core_second(down)
-            for j in range(2):
-                xb(down, j).start()
-            core_second(up)
-
+        for when, j in ((1, 1), (3, 0)):
+
+            @pl.when(i == when)
+            def _(j=j):
+                kc(down, j).start()
+                kc(up, j).start()
+
+        events(k, mlp_after)
         return carry
 
     lax.fori_loop(0, 2 * nt, mlp, 0)
-    second_a(2)
     b_down = wide(7)
     zero_row = jnp.zeros((1, C), F32)
 
@@ -601,33 +695,28 @@
     gather(xp, yb)
     own_y = pltpu.make_async_copy(yb.at[t], y_all.at[t], loc.at[2])
     own_y.start()
-    second_b(4)
+    core_second(5)
+    core_first(5)
+    c_start()
+    core_second(3)
+    core_first(3)
+    ya(3).start()
     acc[...] = jnp.zeros_like(acc)
 
     def start_y():
         for d in range(3):
             out_copy(0, d).start()
 
-    def core_zero():
-        for ch in range(2):
-            core_first(ch)
-            xb(ch, 0).start()
-
-    def core_one():
-        for ch in range(2):
-            core_second(ch)
-            xb(ch, 1).start()
-
     out_first = {
-        1: [lambda: third(4)],
-        2: [lambda: third(3)],
-        3: [lambda: first_half(0), lambda: first_half(1)],
+        0: [lambda: second_a(2)],
+        1: [lambda: second_a(3)],
+        2: [c_sum, lambda: third(2)],
+        3: [lambda: first_half(1), lambda: first_half(0), c_x],
     }
     out_second = {
-        0: [lambda: second_a(3)],
-        1: [lambda: third(2), core_zero, lambda: second_b(5), start_y],
-        2: [lambda: third(5), lambda: fourth(2), lambda: fourth(4)],
-        3: [core_one],
+        0: [lambda: second_b(4), start_y],
+        2: [lambda: third(4), lambda: third(3)],
+        3: [lambda: fourth(2), lambda: fourth(4)],
     }
 
     def back(i, carry):
@@ -649,11 +738,21 @@
             gatt[at, :] = pick(tn_dot(ds_low, kvs[tt, at, :LANES])).astype(BF16)
             return carry
 
-        lax.fori_loop(0, slots // 2, window, 0, unroll=2)
+        lax.fori_loop(0, slots // 2, window, 0, unroll=4)
         events(i, out_first)
-        lax.fori_loop(slots // 2, slots, window, 0, unroll=2)
+        lax.fori_loop(slots // 2, slots, window, 0, unroll=4)
         gk_gv = gkv[:, :CW]
         put_grad(1, tt, nn(h1t[...], gk_gv))
+
+        @pl.when(i == 1)
+        def _():
+            core_first(1)
+            xb(1, 0).start()
+
+        @pl.when(i == 3)
+        def _():
+            last_out(1)
+
         left = nn(h1t[...], gatt[...]) * SCALE
         put_grad(0, tt, jnp.concatenate([left, nn(h2t[...], att[tt])], axis=1))
 
@@ -666,6 +765,15 @@
         def _():
             kc(1, 1).start()
             kc(0, 1).start()
+
+        @pl.when(i == 1)
+        def _():
+            core_first(0)
+            xb(0, 0).start()
+
+        @pl.when(i == 3)
+        def _():
+            last_out(0)
 
         small[tt, 2:3, :] = rowsum(gatt[...].astype(F32)) * SCALE
         small[tt, 3:4, :] = rowsum(gkv[:, LANES:CW].astype(F32))
@@ -694,59 +802,58 @@
     sums = each(finish, (zero_row,) * 2)
     put_small(0, sums[0])
     put_small(1, sums[1])
-    for j in range(2):
-        small_core(j).start()
+    for d in range(3):
+        small_t(d).start()
     gather(xp, gb)
     own_g = pltpu.make_async_copy(gb.at[t], g_all.at[t], loc.at[3])
     own_g.start()
-    for j in range(2):
-        small_core(j).wait_recv()
-    sx[0] = small[t2] + scr[0]
-    sx[1] = small[t] + scr[1]
-    small_y().start()
     for d in range(3):
         out_copy(1, d).start()
-    fourth(3)
-    fourth(5)
-    small_y().wait_recv()
-    zb[z] = sx[1] + syr[0]
+    last_third(1)
+    for d in range(3):
+        small_t(d).wait_recv()
+    zb[z] = small[t] + scr[0] + (scr[1] + scr[2])
     for d in range(nz - 1):
         small_z(d).start()
-    second_half(0)
-    third(0)
+    fourth(3)
+    c_end()
+    last_third(0)
     for d in range(nz - 1):
         small_z(d).wait_recv()
     value = zb[0]
     for zz in range(1, nz):
         value = value + zb[zz]
-    sx[2] = value
+    sx[...] = value
     small_x().start()
-    second_half(1)
-    third(1)
+    fourth(1)
+    fourth(0)
     small_x().wait_recv()
-    tot[...] = sx[2] + syr[1]
-    fourth(0)
-    fourth(1)
+    tot[...] = sx[...] + syr[...]
     for i in range(2):
         for d in range(3):
             out_copy(i, d).wait_recv()
-    sent = [tok_copy(i, d) for i in range(4) for d in range(3)]
+    sent = [tok_copy(i, d) for i in range(3) for d in range(3)]
     sent += [out_copy(i, d) for i in range(2) for d in range(3)]
     for ch in range(NCH):
-        sent += [zr(ch, d) for d in range(nz - 1)]
         sent += [ac(ch, j) for j in range(2)] + [kc(ch, j) for j in range(2)]
-        sent += [az(ch, d) for d in range(nz - 1)] if ch < 5 else [cy(), cx(0), cx(1)]
+        if ch < 5:
+            sent += [az(ch, d) for d in range(nz - 1) if ch > 1]
+            sent += [zr(ch, d) for d in range(nz - 1)]
         if ch < 2:
             sent += [ax(ch, d) for d in range(nz)] + [ay(ch, d) for d in range(nz)]
-            sent += [bx(1, 1)] if ch == 1 else []
+            sent += [xp1(ch, d) for d in range(nz)] + [xb(ch, 0), yb2(ch)]
         elif ch < 5:
             sent += [by(ch), bx(ch, 0), bx(ch, 1)]
-        sent += [ya(ch), xa(ch)] if ch in (2, 3) else [xb(ch, 0), xb(ch, 1), yb2(ch)]
+    sent += [bx(1, 1), cy(), cx(0), cx(1)]
+    sent += [ya(2), xa(2), ya(3), xa(3), xb(4, 0), xb(4, 1), yb2(4), xc(0), xc(1), yc()]
+    sent += [zc(d, j) for d in range(nz - 1) for j in range(2)]
     sent += [cz(d, j) for d in range(nz - 1) for j in range(2)]
-    sent += [small_core(0), small_core(1), small_y(), small_x()]
+    sent += [small_t(d) for d in range(3)] + [small_x()]
     sent += [small_z(d) for d in range(nz - 1)]
     for copy in sent:
         copy.wait_send()
+    line_sent(0)
+    line_sent(1)
     own_y.wait()
     own_g.wait()
 
@@ -785,12 +892,14 @@
             vm((NCH, nt) + piece),
             vm((NCH, 2) + piece),
             vm((2,) + piece),
-            vm((4, 2, nz, deep, CW)),
+            vm((3, 2, nz, deep, CW)),
             vm((NCH, nz, deep, CW)),
             vm((NCH, nz - 1, deep, CW)),
-            vm((2,) + small, F32),
-            vm((2,) + small, F32),
+            vm((nz - 1, 2, 2, deep, CW)),
+            vm((3, deep, CW)),
             vm((3,) + small, F32),
+            vm(small, F32),
+            vm(small, F32),
             vm((nz,) + small, F32),
             vm((nt,) + small, F32),
             vm(row),
@@ -821,8 +930,9 @@
             vm((PAD, wide), F32),
             DMA((4,)),
         ]
-        + pair(4, 3)
+        + pair(3, 3)
         + pair(2, 3)
+        + [DMA((2, 2, nz)), DMA((2, nz))]
         + pair(NCH, nz - 1)
         + pair(2, nz)
         + pair(2, nz)
@@ -830,6 +940,9 @@
         + pair(NCH, 2)
         + pair(NCH)
         + pair(nz - 1, 2)
+        + pair(2, nz)
+        + pair(nz - 1, 2)
+        + pair(3)
         + pair(NCH, 2)
         + pair(NCH, 2)
         + pair(NCH)

time: 99 us -> 90.7 us (0.916)
  Pallas kernels: 97.5 us -> 89.2 us
    pallas_call x1, Pallas kernels: 94.9 us -> 86.6 us  [block_call(): pl.pallas_call(functools.partial(block, nt, nz, slots), name='block', out...]
where the time goes in v4:
time: 90.7 us; the launch traced here: 90.5 us
  Pallas kernels  89.2 us (98%)
  between operations  1.32 us (1%)
    pallas_call x1, Pallas kernels, block_call(): pl.pallas_call(functools.partial(block, nt, nz, slots), name='block', out...  86.6 us
    pallas_call x1, Pallas kernels, spell_call(): pl.pallas_call(spell, name='spell', out_shape=outs, in_specs=[VM] * 4, ou...  2.63 us

profile of v4, /device:TPU:0, one launch (start us, length us, event | category | flops | bytes accessed | tf_op | source)
XLA Modules:
  0.0 90.5 jit_solution(11391554203968814278)
XLA Ops:
  1.3 86.6 %block.1 = (bf16[4,392,128]{2,1,0:T(8,128)(2,1)}, bf16[4,392,128]{2,1,0:T(8,128)(2,1)}, f32[6,64,256]{2,1,0:T(8,128)}, f32[24,128]{1,0:T(8,128)}) custom-call(s32[1]{0:T(128)S(6)} %copy.39.refs_0_, bf16[4,392,128]{2,1,0:T(8,128)(2,1)} %bitcast.28, bf16[4,392,128]{2,1,0:T(8,128)(2,1)} %bitcast.29, bf16[64,128]{1,0:T(8,128)(2,1)} %refs_3_.1, ...), custom_call_target="tpu_custom_call" | custom-call | tf_op jit(solution)/shard_map/block/pallas_call | solution.py:875
  87.9 2.6 %spell.1 = (f32[4,392,128]{2,1,0:T(8,128)}, f32[4,392,128]{2,1,0:T(8,128)}, f32[1,128]{1,0:T(1,128)}, f32[1,128]{1,0:T(1,128)}, f32[64,128]{1,0:T(8,128)}, /*ind...) custom-call(bf16[4,392,128]{2,1,0:T(8,128)(2,1)} %get-tuple-element., ...), custom_call_target="tpu_custom_call" | custom-call | tf_op jit(solution)/shard_map/spell/pallas_call | solution.py:980

commit v5 on v4

--- a/solution.py
+++ b/solution.py
@@ -28,6 +28,60 @@
 DMA = pltpu.SemaphoreType.DMA
 
 
+WAY_IN = ("A", "B", "A", "B", "E", "C")
+WAY_OUT = ("B", "B", "B", "C", "A", "B")
+MLP_ORDER = (0, 1, 3, 2)
+PLAN = {
+    "h0": ("az2",),
+    "h1": ("az4", "yx1",),
+    "h2": ("zx2", "ay0",),
+    "h3": ("az3",),
+    "a0f": ("c11", "cot",),
+    "a1f": ("zt4", "az5", "xy2", "zx4",),
+    "a1s": ("c02", "zy3", "c10",),
+    "a3f": ("zx3",),
+    "a3s": ("c04",),
+    "mid": ("c12", "c14",),
+    "m1": ("yx3", "c03",),
+    "m2": ("c15",),
+    "m3": ("c05",),
+    "m4": ("o14", "c13", "ot2", "oo2",),
+    "m7": ("o22", "oo3", "oo5",),
+    "turn": ("ot3",),
+    "b0f": ("ot5", "yout",),
+    "b0d": ("o24",),
+    "b0s": ("o32",),
+    "b1d": ("ot1", "o25", "ot0",),
+    "b2d": ("o34",),
+    "b3f": ("o21",),
+    "b3d": ("oo1", "oo0",),
+    "b3s": ("o35",),
+    "t1": ("o20", "o23",),
+    "t2": ("g",),
+    "t3": ("o31", "o30",),
+    "t4": ("o33",),
+}
+
+
+def plan_order(sched):
+    out = list(sched.get("h0", ())) + list(sched.get("h1", ()))
+    out += list(sched.get("h2", ())) + ["use_a0"]
+    out += sched.get("h3", ())
+    for i in range(4):
+        out += ([f"use_a{i}"] if i else []) + list(sched.get(f"a{i}f", ()))
+        out += sched.get(f"a{i}s", ())
+    out += list(sched.get("mid", ()))
+    for k in range(8):
+        out += [f"use_m{k}"] + list(sched.get(f"m{k}", ()))
+    out += sched.get("turn", ())
+    for i in range(4):
+        for part in "fds":
+            out += sched.get(f"b{i}{part}", ())
+    for i in range(1, 6):
+        out += sched.get(f"t{i}", ())
+    return out + ["end"]
+
+
 def flip(bit, by):
     return bit + by - 2 * bit * by
 
@@ -72,14 +126,17 @@
 
 
 def block(nt, nz, slots, *refs):
+    live, tok, cot, wq, wk, wv, wo, wh, wd = refs[:9]
+    outside, refs = refs[9:21], refs[21:]
+    inside, refs = refs[4:16], refs[:4] + refs[16:]
+    g1, s1, bq, bv, bo, g2, s2, bd, bh, tab, rel, reg = inside
     (
-        live, tok, cot, wq, wk, wv, wo, wh, wd, g1, s1, bq, bv, bo, g2, s2, bd, bh, tab, rel, reg,
         y_all, g_all, fin, tot,
         xg, cg, gw, vg, rg, dv, rc, ry, rx, r3, rz, rzc, rxc, scr, syr, sx, zb, small, yb, gb, square, mask, inv,
-        xs, xp, gy, h1, h1t, h2t, gyt, qs, kvs, probs, att, acc, acc2, n1, r1, n2, r2, low, gkv, gq,
+        xs, xp, gy, h1, h1t, h2t, gyt, qs, kvs, probs, att, acc, acc2, n1, r1, n2, r2, low, gkv, gq, gatt,
         pairs,
-        loc, tok_s, tok_r, out_s, out_r, ln_s, ln_r, az_s, az_r, ax_s, ax_r, ay_s, ay_r, ac_s, ac_r,
-        bx_s, bx_r, by_s, by_r, cz_s, cz_r, px_s, px_r, zc_s, zc_r, xc_s,
+        loc, ld, tok_s, tok_r, out_s, out_r, az_s, az_r, ax_s, ax_r, ay_s, ay_r, ac_s, ac_r,
+        bx_s, bx_r, by_s, by_r, px_s, px_r, zc_s, zc_r, xc_s,
         xc_r, k_s, k_r, p_s, p_r, q_s, q_r, rz_s, rz_r, sm_s, sm_r,
     ) = refs
     heads = LANES // HDIM
@@ -120,9 +177,18 @@
         peer = ts[d]
         return far(src.at[peer[1]], dst.at[t], out_s.at[i, d], out_r.at[i, d], peer)
 
-    def az(ch, d):
-        ref = gw.at[ch, t, z, x]
-        return far(ref, ref, az_s.at[ch, d], az_r.at[ch, d], zs[d])
+    def az(ch, d, j=0):
+        far_t = t2 if j else t
+        ref = gw.at[ch, far_t, z] if WAY_IN[ch] == "C" else gw.at[ch, far_t, z, x]
+        return far(ref, ref, az_s.at[ch, d, j], az_r.at[ch, d, j], zs[d])
+
+    def az_all(ch):
+        both = 2 if WAY_IN[ch] in "CE" else 1
+        return [az(ch, d, j) for d in range(nz - 1) for j in range(both)]
+
+    def az_from(ch, zz):
+        ref, d = gw.at[ch, t, z, x], lax.rem(z - zz + nz, nz) - 1
+        return far(ref, ref, az_s.at[ch, d, 0], az_r.at[ch, d, 0], xpeer)
 
     def far_first(k):
         rising = k + jnp.where(z > k, 0, 1)
@@ -130,48 +196,14 @@
         zz = jnp.where(2 * z < nz, falling, rising)
         return zz, lax.rem(zz - z + nz, nz) - 1
 
-    def line(ch, zz, up):
-        ref = gw.at[ch, t, zz, x]
-        there = (lax.rem(z + nz + (1 if up else -1), nz) * 2 + x, t)
-        return far(ref, ref, ln_s.at[ch, up, zz], ln_r.at[ch, zz], there)
-
-    def pass_on(ch, zz):
-        @pl.when((zz <= z) & (z < nz - 1))
-        def _():
-            line(ch, zz, 1).start()
-
-        @pl.when((zz >= z) & (z > 0))
-        def _():
-            line(ch, zz, 0).start()
-
-        ax(ch, zz).start()
-        if ch == 1:
-            ay(ch, zz).start()
-
-    def line_step(ch, step):
-        for zz, there in ((z - step, z >= step), (z + step, z + step < nz)):
-
-            @pl.when(there)
-            def _(zz=zz):
-                line(ch, zz, 0).wait_recv()
-                pass_on(ch, zz)
-
-    def line_sent(ch):
-        for zz in range(nz):
-
-            @pl.when((zz <= z) & (z < nz - 1))
-            def _(zz=zz):
-                line(ch, zz, 1).wait_send()
-
-            @pl.when((zz >= z) & (z > 0))
-            def _(zz=zz):
-                line(ch, zz, 0).wait_send()
-
     def az_start(ch):
-        ref = gw.at[ch, t, z, x]
         for k in range(nz - 1):
             zz, d = far_first(k)
-            far(ref, ref, az_s.at[ch, d], az_r.at[ch, d], (zz * 2 + x, t)).start()
+            for j in range(2 if WAY_IN[ch] in "CE" else 1):
+                far_t = t2 if j else t
+                ref = gw.at[ch, far_t, z] if WAY_IN[ch] == "C" else gw.at[ch, far_t, z, x]
+                peer = (zz * 2 + x, t)
+                far(ref, ref, az_s.at[ch, d, j], az_r.at[ch, d, j], peer).start()
 
     def zr_start(ch, k):
         zz, d = far_first(k)
@@ -191,20 +223,16 @@
         return far(ref, ref, bx_s.at[ch, j], bx_r.at[ch, j], xpeer)
 
     def by(ch):
-        ref = gw.at[ch, t, :, x]
+        ref = gw.at[ch, t] if WAY_IN[ch] == "A" else gw.at[ch, t, :, x]
         return far(ref, ref, by_s.at[ch], by_r.at[ch], ypeer)
 
-    def cy():
-        ref = gw.at[5, t, z, x]
-        return far(ref, ref, by_s.at[5], by_r.at[5], ypeer)
-
-    def cx(j):
-        ref = gw.at[5, t2 if j else t, z, x]
-        return far(ref, ref, bx_s.at[5, j], bx_r.at[5, j], xpeer)
-
-    def cz(d, j):
-        ref = gw.at[5, t2 if j else t, z]
-        return far(ref, ref, cz_s.at[d, j], cz_r.at[d, j], zs[d])
+    def cy(ch):
+        ref = gw.at[ch, t, z, x]
+        return far(ref, ref, by_s.at[ch], by_r.at[ch], ypeer)
+
+    def cx(ch, j):
+        ref = gw.at[ch, t2 if j else t, z, x]
+        return far(ref, ref, bx_s.at[ch, j], bx_r.at[ch, j], xpeer)
 
     def ac(ch, j):
         ref = gw.at[ch, t2 if j else t]
@@ -213,63 +241,27 @@
     def kc(ch, j):
         return far(dv.at[ch, t1 if j else t3], rc.at[ch, j], k_s.at[ch, j], k_r.at[ch, j], cpeer)
 
+    a_slot = {ch: i for i, ch in enumerate(c for c in range(NCH) if WAY_OUT[c] == "A")}
+    b_slot = {ch: i for i, ch in enumerate(c for c in range(NCH) if WAY_OUT[c] == "B")}
+    c_slot = {ch: i for i, ch in enumerate(c for c in range(NCH) if WAY_OUT[c] == "C")}
+
     def ya(ch):
-        return far(dv.at[ch, t2], ry.at[ch - 2], p_s.at[ch, 0], p_r.at[ch, 0], ypeer)
+        return far(dv.at[ch, t2], ry.at[a_slot[ch]], p_s.at[ch, 0], p_r.at[ch, 0], ypeer)
 
     def xa(ch):
         return far(dv.at[ch, t, :, 1 - x], r3.at[ch], q_s.at[ch], q_r.at[ch], xpeer)
 
-    def zc(d, j):
-        src = dv.at[5, t if j else t2, lax.rem(z + d + 1, nz)]
-        return far(src, rzc.at[d, j], zc_s.at[d, j], zc_r.at[d, j], zs[d])
-
-    def xc(j):
-        src = dv.at[5, t if j else t2, z, 1 - x]
-        return far(src, rxc.at[j], xc_s.at[j], xc_r.at[j], xpeer)
-
-    def yc():
-        return far(dv.at[5, t2, z, x], rxc.at[2], xc_s.at[2], xc_r.at[2], ypeer)
-
-    def c_start():
-        for k in range(nz - 1):
-            zz, d = far_first(k)
-            for j in range(2):
-                src = dv.at[5, t if j else t2, zz]
-                far(src, rzc.at[d, j], zc_s.at[d, j], zc_r.at[d, j], (zz * 2 + x, t)).start()
-
-    def c_sum():
-        for j, tt in enumerate((t2, t)):
-            value = dv[5, tt, z].astype(F32)
-            for d in range(nz - 1):
-                zc(d, j).wait_recv()
-                value = value + rzc[d, j].astype(F32)
-            dv[5, tt, z] = value.astype(BF16)
-            xc(j).start()
-
-    def c_x():
-        for j, tt in enumerate((t2, t)):
-            xc(j).wait_recv()
-            dv[5, tt, z, x] = add(dv[5, tt, z, x], rxc[j])
-        yc().start()
-
-    def c_end():
-        yc().wait_recv()
-        fin[5] = dv[5, t, z, x].astype(F32) + rxc[2].astype(F32)
-
-    def slot_b(ch):
-        return ch if isinstance(ch, int) and ch < 2 else ch - 2
-
     def piece_of(d):
         return far_first(d)[0] if d < nz - 1 else z
 
     def xp1(ch, d):
         zz = piece_of(d)
-        src, dst = dv.at[ch, t, zz, 1 - x], rx.at[slot_b(ch), 1, zz]
+        src, dst = dv.at[ch, t, zz, 1 - x], rx.at[b_slot[ch], 1, zz]
         return far(src, dst, px_s.at[ch, d], px_r.at[ch, d], xpeer)
 
     def xb(ch, j):
         src = dv.at[ch, t if j else t2, :, 1 - x]
-        return far(src, rx.at[slot_b(ch), j], p_s.at[ch, j], p_r.at[ch, j], xpeer)
+        return far(src, rx.at[b_slot[ch], j], p_s.at[ch, j], p_r.at[ch, j], xpeer)
 
     def yb2(ch):
         return far(dv.at[ch, t2, :, x], r3.at[ch], q_s.at[ch], q_r.at[ch], ypeer)
@@ -278,59 +270,24 @@
         src = dv.at[ch, t, lax.rem(z + d + 1, nz), x]
         return far(src, rz.at[ch, d], rz_s.at[ch, d], rz_r.at[ch, d], zs[d])
 
-    def core_first(ch):
-        kc(ch, 0).wait_recv()
-        dv[ch, t2] = add(dv[ch, t2], rc[ch, 0])
-
-    def core_second(ch):
-        kc(ch, 1).wait_recv()
-        dv[ch, t] = add(dv[ch, t], rc[ch, 1])
-
-    def second_a(ch):
-        ya(ch).wait_recv()
-        dv[ch, t] = add(dv[ch, t], ry[ch - 2])
-        xa(ch).start()
-
-    def first_half(ch):
-        xb(ch, 0).wait_recv()
-        dv[ch, t2, :, x] = add(dv[ch, t2, :, x], rx[slot_b(ch), 0])
-        yb2(ch).start()
-
-    def second_half(ch):
-        xb(ch, 1).wait_recv()
-        dv[ch, t, :, x] = add(dv[ch, t, :, x], rx[slot_b(ch), 1])
-
-    def second_b(ch):
-        first_half(ch)
-        second_half(ch)
-
-    def third(ch):
-        (xa(ch) if ch in (2, 3) else yb2(ch)).wait_recv()
-        dv[ch, t, :, x] = add(dv[ch, t, :, x], r3[ch])
+    def zc(ch, d, j):
+        src, i = dv.at[ch, t if j else t2, lax.rem(z + d + 1, nz)], c_slot[ch]
+        return far(src, rzc.at[i, d, j], zc_s.at[i, d, j], zc_r.at[i, d, j], zs[d])
+
+    def zc_start(ch, j):
+        i = c_slot[ch]
         for k in range(nz - 1):
-            zr_start(ch, k)
-
-    def last_out(ch):
-        core_second(ch)
-        for d in range(nz):
-            xp1(ch, d).start()
-
-    def last_third(ch):
-        yb2(ch).wait_recv()
-        for d in range(nz):
-            zz = piece_of(d)
-            xp1(ch, d).wait_recv()
-            value = dv[ch, t, zz, x].astype(F32) + rx[slot_b(ch), 1, zz].astype(F32)
-            dv[ch, t, zz, x] = (value + r3[ch, zz].astype(F32)).astype(BF16)
-            if d < nz - 1:
-                zr_start(ch, d)
-
-    def fourth(ch):
-        value = dv[ch, t, z, x].astype(F32)
-        for d in range(nz - 1):
-            zr(ch, d).wait_recv()
-            value = value + rz[ch, d].astype(F32)
-        fin[ch] = value
+            zz, d = far_first(k)
+            src, peer = dv.at[ch, t if j else t2, zz], (zz * 2 + x, t)
+            far(src, rzc.at[i, d, j], zc_s.at[i, d, j], zc_r.at[i, d, j], peer).start()
+
+    def xc(ch, j):
+        src, i = dv.at[ch, t if j else t2, z, 1 - x], c_slot[ch]
+        return far(src, rxc.at[i, j], xc_s.at[i, j], xc_r.at[i, j], xpeer)
+
+    def yc(ch):
+        i = c_slot[ch]
+        return far(dv.at[ch, t2, z, x], rxc.at[i, 2], xc_s.at[i, 2], xc_r.at[i, 2], ypeer)
 
     def small_t(d):
         return far(small.at[ts[d][1]], scr.at[d], sm_s.at[d], sm_r.at[d], ts[d])
@@ -341,10 +298,20 @@
     def small_x():
         return far(sx, syr, sm_s.at[2 + nz], sm_r.at[2 + nz], xpeer)
 
-    gw[0, t, z, x, :, :LANES] = wq[...]
-    gw[0, t, z, x, :, LANES:] = wo[...]
-    gw[1, t, z, x, :, :LANES] = wk[...]
-    gw[1, t, z, x, :, LANES:] = wv[...]
+    def lanes(ch, i, size):
+        return gw.at[ch, t, z, x, :, pl.ds(i * size, size)]
+
+    loads = [(wq, lanes(0, 0, LANES)), (wo, lanes(0, 1, LANES))]
+    loads += [(wk, lanes(1, 0, LANES)), (wv, lanes(1, 1, LANES))]
+    for i in range(2):
+        loads += [(wh.at[:, pl.ds(i * CW, CW)], gw.at[2 + i, t, z, x])]
+        loads += [(wd.at[:, pl.ds(i * CW, CW)], gw.at[4 + i, t, z, x])]
+    loads += list(zip(outside, inside))
+    loads = [pltpu.make_async_copy(*pair, ld.at[i]) for i, pair in enumerate(loads)]
+    for copy in loads:
+        copy.start()
+    for copy in loads:
+        copy.wait()
     for i, ref in enumerate((g1, s1, bq, bv, bo, g2, s2, bd)):
         vg[t, i : i + 1, :] = ref[...]
     vg[t, 8:12, :] = bh[...]
@@ -353,21 +320,27 @@
         vg[t, 13 + 2 * h : 14 + 2 * h, : TABLE - LANES] = tab[h : h + 1, LANES:]
         vg[t, 13 + 2 * h : 14 + 2 * h, TABLE - LANES :] = jnp.zeros((1, TPAD - TABLE), F32)
     vg[t, 12 + 2 * heads :, :] = jnp.zeros((SROWS - 12 - 2 * heads, LANES), F32)
-    for s in range(2):
-        gw[2 + s, t, z, x] = wh[:, s * CW : (s + 1) * CW]
-        gw[4 + s, t, z, x] = wd[:, s * CW : (s + 1) * CW]
     pl.semaphore_wait(barrier, len(peers))
     own_tok = pltpu.make_async_copy(tok.at[t], xg.at[t], loc.at[0])
     own_cot = pltpu.make_async_copy(cot.at[t], cg.at[t], loc.at[1])
     own_tok.start()
     own_cot.start()
+    early = [ch for ch in range(2, NCH) if WAY_IN[ch] in "CE"]
+    first = [ch for ch in early if f"az{ch}" in PLAN.get("h0", ())]
+    for ch in first:
+        cy(ch).start()
     for d in range(3):
         tok_copy(2, d).start()
-    pass_on(1, z)
-    pass_on(0, z)
+    az_start(1)
+    ax(1, z).start()
+    ay(1, z).start()
+    az_start(0)
+    ax(0, z).start()
     for d in range(3):
         tok_copy(0, d).start()
-    cy().start()
+    for ch in early:
+        if ch not in first:
+            cy(ch).start()
     square[...] = jnp.zeros_like(square)
     square[:WT, :WT] = rel[...].astype(F32)
     rel_t = square[...].T[:PAD, :PAD]
@@ -404,14 +377,14 @@
     for w in range(slots):
         same = reg_col[:, w : w + 1] == reg_row[w : w + 1, :]
         mask[w] = jnp.where(real, jnp.where(same, 0.0, -100.0), -1e30)
-    for step in range(1, nz):
-        line_step(1, step)
-        line_step(0, step)
-    az_start(2)
-    az_start(4)
-    cy().wait_recv()
-    for j in range(2):
-        cx(j).start()
+    def cross(ch):
+        cy(ch).wait_recv()
+        if WAY_IN[ch] == "C":
+            for j in range(2):
+                cx(ch, j).start()
+
+    for ch in first:
+        cross(ch)
 
     def wide(i):
         return jnp.concatenate([vg[tt, i : i + 1, :] for tt in range(nt)], axis=1)
@@ -446,63 +419,216 @@
     def put_grad(ch, tt, value):
         dv[ch, tt] = value.astype(BF16).reshape(dv.shape[2:])
 
-    def events(i, table):
-        for when, todo in table.items():
-
-            @pl.when(i == when)
-            def _(todo=todo):
-                for act in todo:
-                    act()
-
-    def z_to_xy(ch):
+    def tok_all(i):
+        return [tok_copy(i, d) for d in range(3)]
+
+    def arrivals(name):
+        kind, ch = name[:-1], int(name[-1])
+        if kind == "x":
+            return [ax(ch, zz) for zz in range(nz)]
+        if kind == "ay":
+            return [ay(ch, zz) for zz in range(nz)]
+        if kind == "z":
+            return az_all(ch)
+        if kind in ("xo", "xt"):
+            return [bx(ch, int(kind == "xt"))]
+        if kind == "yo":
+            return [by(ch)]
+        if kind in ("k0", "k1"):
+            return [ac(ch, int(kind == "k1"))]
+        if kind in ("r0", "r1"):
+            return [kc(ch, int(kind == "r1"))]
+        if kind == "ya":
+            return [ya(ch)]
+        if kind == "xa":
+            return [xa(ch)]
+        if kind == "xbt":
+            return [xb(ch, 0)]
+        if kind == "xbo":
+            return [xb(ch, 1)]
+        if kind == "yb":
+            return [yb2(ch)]
+        if kind == "zc":
+            return [zc(ch, d, j) for d in range(nz - 1) for j in range(2)]
+        assert kind == "xc"
+        return [xc(ch, 0), xc(ch, 1)]
+
+    def own_of(ch):
+        return ("z%d" if WAY_IN[ch] == "C" else "xo%d") % ch
+
+    def other_y_of(ch):
+        return {"A": "yo%d", "B": "xt%d", "C": "z%d", "E": "xt%d"}[WAY_IN[ch]] % ch
+
+    def waits_of(entry):
+        fixed = {
+            "use_a0": ("x1", "x0"), "use_a1": ("k01", "k00"), "use_a2": ("xt1", "ay0"),
+            "use_a3": ("k11", "k10"), "yx1": ("ay1",), "c11": ("xt1",), "c10": ("ay0",),
+            "ay0": ("x0",), "end": (), "cot": (), "yout": (), "g": (),
+        }
+        if entry in fixed:
+            return fixed[entry]
+        if entry.startswith("use_m"):
+            k = int(entry[-1])
+            chs, m = ((2, 4) if k < nt else (3, 5)), MLP_ORDER[k % nt]
+            names = {0: own_of, 1: "k0{}".format, 2: other_y_of, 3: "k1{}".format}[m]
+            return tuple(names(ch) for ch in chs)
+        kind, ch = entry[:-1], int(entry[-1])
+        way = WAY_OUT[ch]
+        names = {
+            "az": (), "zx": ("z",), "zy": ("z",), "zt": ("z",), "yx": ("yo",), "xy": ("xo",),
+            "o1": ("r0",), "oo": ("r1",), "ot": ("r0",),
+            "o2": {"A": ("ya", "r1"), "B": ("xbt",), "C": ("zc",)}[way],
+            "o3": {"A": ("xa",), "B": ("yb",) if ch < 2 else ("xbo", "yb"), "C": ("xc",)}[way],
+        }
+        if kind == "c0":
+            return (own_of(ch),)
+        if kind == "c1":
+            return (other_y_of(ch),)
+        return tuple(f"{n}{ch}" for n in names[kind])
+
+    first_use = {}
+    for item in plan_order(PLAN):
+        for name in waits_of(item):
+            first_use.setdefault(name, item)
+
+    def arrive(entry):
+        for name in waits_of(entry):
+            if first_use[name] == entry:
+                for copy in arrivals(name):
+                    copy.wait_recv()
+
+    def act(entry):
+        arrive(entry)
+        if entry == "cot":
+            for copy in tok_all(1):
+                copy.start()
+            return
+        if entry in ("yout", "g"):
+            for d in range(3):
+                out_copy(int(entry == "g"), d).start()
+            return
+        kind, ch = entry[:-1], int(entry[-1])
+        way = WAY_OUT[ch]
+        if kind == "ay":
+            for zz in range(nz):
+                ay(ch, zz).start()
+        elif kind == "az":
+            for j in range(2 if WAY_IN[ch] == "C" else 0):
+                cx(ch, j).wait_recv()
+            az_start(ch)
+        elif kind == "zx":
+            bx(ch, 0).start()
+        elif kind in ("zt", "yx"):
+            bx(ch, 1).start()
+        elif kind in ("zy", "xy"):
+            by(ch).start()
+        elif kind in ("c0", "c1"):
+            ac(ch, int(kind == "c1")).start()
+        elif kind == "o1":
+            dv[ch, t2] = add(dv[ch, t2], rc[ch, 0])
+            ya(ch).start()
+        elif kind == "ot":
+            dv[ch, t2] = add(dv[ch, t2], rc[ch, 0])
+            if way == "B":
+                xb(ch, 0).start()
+            else:
+                zc_start(ch, 0)
+        elif kind == "oo":
+            dv[ch, t] = add(dv[ch, t], rc[ch, 1])
+            if way == "C":
+                zc_start(ch, 1)
+            elif ch < 2:
+                for d in range(nz):
+                    xp1(ch, d).start()
+            else:
+                xb(ch, 1).start()
+        elif kind == "o2" and way == "A":
+            value = dv[ch, t].astype(F32) + rc[ch, 1].astype(F32)
+            dv[ch, t] = (value + ry[a_slot[ch]].astype(F32)).astype(BF16)
+            xa(ch).start()
+        elif kind == "o2" and way == "B":
+            dv[ch, t2, :, x] = add(dv[ch, t2, :, x], rx[b_slot[ch], 0])
+            yb2(ch).start()
+        elif kind == "o2":
+            for j, tt in enumerate((t2, t)):
+                value = dv[ch, tt, z].astype(F32)
+                for d in range(nz - 1):
+                    value = value + rzc[c_slot[ch], d, j].astype(F32)
+                dv[ch, tt, z] = value.astype(BF16)
+                xc(ch, j).start()
+        elif kind == "o3" and way == "C":
+            for j, tt in enumerate((t2, t)):
+                dv[ch, tt, z, x] = add(dv[ch, tt, z, x], rxc[c_slot[ch], j])
+            yc(ch).start()
+        elif kind == "o3" and ch < 2:
+            for d in range(nz):
+                zz = piece_of(d)
+                xp1(ch, d).wait_recv()
+                value = dv[ch, t, zz, x].astype(F32) + rx[b_slot[ch], 1, zz].astype(F32)
+                dv[ch, t, zz, x] = (value + r3[ch, zz].astype(F32)).astype(BF16)
+                if d < nz - 1:
+                    zr_start(ch, d)
+        else:
+            assert kind == "o3"
+            value = dv[ch, t, :, x].astype(F32) + r3[ch].astype(F32)
+            if way == "B":
+                value = value + rx[b_slot[ch], 1].astype(F32)
+            dv[ch, t, :, x] = value.astype(BF16)
+            for k in range(nz - 1):
+                zr_start(ch, k)
+
+    def last(ch):
+        if WAY_OUT[ch] == "C":
+            yc(ch).wait_recv()
+            fin[ch] = dv[ch, t, z, x].astype(F32) + rxc[c_slot[ch], 2].astype(F32)
+            return
+        value = dv[ch, t, z, x].astype(F32)
         for d in range(nz - 1):
-            az(ch, d).wait_recv()
-        bx(ch, 0).start()
-        by(ch).start()
-
-    def y_to_x(ch):
-        by(ch).wait_recv()
-        bx(ch, 1).start()
-
-    def x_to_core(ch, j):
-        bx(ch, j).wait_recv()
-        ac(ch, j).start()
-
-    def ay_to_bx():
-        for d in range(nz):
-            ay(1, d).wait_recv()
-        bx(1, 1).start()
-
-    def start_cz():
-        for j in range(2):
-            cx(j).wait_recv()
-        for d in range(nz - 1):
-            for j in range(2):
-                cz(d, j).start()
-
-    def groups_in():
-        for d in range(nz):
-            ay(0, d).wait_recv()
-        ac(0, 1).start()
-        x_to_core(1, 1)
-
-    def start_cot():
-        for d in range(3):
-            tok_copy(1, d).start()
-
-    def end_cz():
-        for d in range(nz - 1):
-            for j in range(2):
-                cz(d, j).wait_recv()
-        for j in range(2):
-            ac(5, j).start()
+            zr(ch, d).wait_recv()
+            value = value + rz[ch, d].astype(F32)
+        fin[ch] = value
+
+    def run(slot):
+        for entry in PLAN.get(slot, ()):
+            act(entry)
+
+    def run_at(index, pattern, count):
+        for i in range(count):
+            if PLAN.get(pattern % i):
+
+                @pl.when(index == i)
+                def _(i=i):
+                    run(pattern % i)
+
+    def use_at(index, pattern, count, start=0):
+        for i in range(start, count):
+            if any(first_use[n] == pattern % i for n in waits_of(pattern % i)):
+
+                @pl.when(index == i)
+                def _(i=i):
+                    arrive(pattern % i)
 
     n_live = live[0] - t * slots
     small[...] = jnp.zeros_like(small)
     own_tok.wait()
-    for i in (2, 0):
-        for d in range(3):
-            tok_copy(i, d).wait_recv()
+    run("h0")
+    for ch in (1, 0):
+        for k in range(nz - 1):
+            zz, _ = far_first(nz - 2 - k)
+            az_from(ch, zz).wait_recv()
+            ax(ch, zz).start()
+            if ch == 1:
+                ay(ch, zz).start()
+    for ch in early:
+        if ch not in first:
+            cross(ch)
+    run("h1")
+    for copy in tok_all(2):
+        copy.wait_recv()
+    for tt in range(nt):
+        bias_of(tt)
+    for d in range(3):
+        tok_copy(0, d).wait_recv()
     spread(xg, xp)
     gain1, shift1 = wide(0), wide(1)
 
@@ -516,16 +642,11 @@
         return carry
 
     each(start)
-    for tt in range(nt):
-        bias_of(tt)
-    for d in range(nz):
-        ax(1, d).wait_recv()
+    run("h2")
+    arrive("use_a0")
     ac(1, 0).start()
-    for d in range(nz):
-        ax(0, d).wait_recv()
-        ay(0, d).start()
     ac(0, 0).start()
-    z_to_xy(2)
+    run("h3")
     lane_head = lax.broadcasted_iota(jnp.int32, (PAD, LANES), 1) // HDIM
     ones = [(lane_head == h).astype(F32).astype(BF16) for h in range(heads)]
 
@@ -540,52 +661,37 @@
 
     acc[...] = jnp.zeros_like(acc)
 
-    in_first = {
-        0: [ay_to_bx, lambda: az_start(3)],
-        1: [start_cz],
-        2: [lambda: y_to_x(2)],
-        3: [lambda: y_to_x(4), lambda: z_to_xy(3)],
-    }
-    in_second = {
-        0: [lambda: z_to_xy(4)],
-        1: [groups_in, start_cot],
-        2: [lambda: x_to_core(2, 0), lambda: x_to_core(4, 0)],
-        3: [lambda: x_to_core(2, 1)],
-    }
-
     def attend(i, carry):
         tt = group(i)
 
-        @pl.when(i == 1)
-        def _():
-            for ch in range(2):
-                ac(ch, 0).wait_recv()
-
-        @pl.when(i == 3)
-        def _():
-            for ch in range(2):
-                ac(ch, 1).wait_recv()
-
+        use_at(i, "use_a%d", nt, 1)
         q = (nn(h1[...], weight(0, tt, 0, LANES)) + vg[tt, 2:3, :]) * SCALE
         qs[tt] = q.astype(BF16)
         kv = nn(h1[...], weight(1, tt))
         kvs[tt, :, :LANES] = kv[:, :LANES].astype(BF16)
         kvs[tt, :, LANES:] = (kv[:, LANES:] + vg[tt, 3:4, :]).astype(BF16)
 
-        def window(w, carry):
+        def window(w):
             at = pl.ds(pl.multiple_of(w * PAD, PAD), PAD)
             s = nt_dot(kvs[tt, at, :LANES], stack(qs[tt, at, :])) + rg[tt] + mask[w]
             e = jnp.exp(s - jnp.max(s, axis=0, keepdims=True))
             p = e / rowsum(e)
             probs[tt, w] = p
             att[tt, at, :] = pick(tn_dot(p.astype(BF16), kvs[tt, at, LANES:])).astype(BF16)
+
+        def four(hh, carry):
+            for j in range(slots // 2):
+                window(hh * (slots // 2) + j)
+
+            @pl.when(hh == 0)
+            def _():
+                run_at(i, "a%df", nt)
+
             return carry
 
-        lax.fori_loop(0, slots // 2, window, 0, unroll=4)
-        events(i, in_first)
-        lax.fori_loop(slots // 2, slots, window, 0, unroll=4)
+        lax.fori_loop(0, 2, four, 0)
         acc[...] += nt_dot(att[tt], weight(0, tt, LANES, LANES))
-        events(i, in_second)
+        run_at(i, "a%ds", nt)
         return carry
 
     lax.fori_loop(0, nt, attend, 0)
@@ -615,38 +721,17 @@
         return carry
 
     each(middle)
+    run("mid")
     acc[...] = jnp.zeros_like(acc)
     acc2[...] = jnp.zeros_like(acc2)
-    def from_core(chs, j):
-        for ch in chs:
-            ac(ch, j).wait_recv()
-
-    def sums_out():
-        core_first(2)
-        ya(2).start()
-        core_first(4)
-        for j in range(2):
-            xb(4, j).start()
-
-    mlp_before = {
-        1: [lambda: from_core((2, 4), 0)],
-        3: [lambda: from_core((2, 4), 1)],
-        5: [lambda: from_core((3, 5), 0)],
-        7: [lambda: from_core((3, 5), 1)],
-    }
-    mlp_after = {
-        0: [lambda: x_to_core(4, 1)],
-        1: [lambda: y_to_x(3), lambda: x_to_core(3, 0)],
-        2: [end_cz],
-        4: [lambda: core_second(2), lambda: core_second(4)],
-        5: [sums_out, lambda: x_to_core(3, 1)],
-    }
-
     def mlp(k, carry):
         s, i = lax.div(k, nt), lax.rem(k, nt)
-        tt = group(i)
+        turn_at = MLP_ORDER[nt - 1]
+        for j in range(nt - 1):
+            turn_at = jnp.where(i == j, MLP_ORDER[j], turn_at)
+        tt = group(turn_at)
         up, down = 2 + s, 4 + s
-        events(k, mlp_before)
+        use_at(k, "use_m%d", 2 * nt)
 
         bias = vg[tt, pl.ds(8 + 2 * s, 2), :]
         bias = jnp.concatenate([bias[0:1], bias[1:2]], axis=1)
@@ -663,14 +748,14 @@
         put_grad(up, tt, nn(h2t[...], grad_low))
         acc2[...] += nt_dot(grad_low, weight(up, tt))
 
-        for when, j in ((1, 1), (3, 0)):
+        for when, j in ((MLP_ORDER.index(1), 1), (MLP_ORDER.index(3), 0)):
 
             @pl.when(i == when)
             def _(j=j):
+                kc(up, j).start()
                 kc(down, j).start()
-                kc(up, j).start()
-
-        events(k, mlp_after)
+
+        run_at(k, "m%d", 2 * nt)
         return carry
 
     lax.fori_loop(0, 2 * nt, mlp, 0)
@@ -695,65 +780,43 @@
     gather(xp, yb)
     own_y = pltpu.make_async_copy(yb.at[t], y_all.at[t], loc.at[2])
     own_y.start()
-    core_second(5)
-    core_first(5)
-    c_start()
-    core_second(3)
-    core_first(3)
-    ya(3).start()
+    run("turn")
     acc[...] = jnp.zeros_like(acc)
-
-    def start_y():
-        for d in range(3):
-            out_copy(0, d).start()
-
-    out_first = {
-        0: [lambda: second_a(2)],
-        1: [lambda: second_a(3)],
-        2: [c_sum, lambda: third(2)],
-        3: [lambda: first_half(1), lambda: first_half(0), c_x],
-    }
-    out_second = {
-        0: [lambda: second_b(4), start_y],
-        2: [lambda: third(4), lambda: third(3)],
-        3: [lambda: fourth(2), lambda: fourth(4)],
-    }
 
     def back(i, carry):
         tt = group(3 - i)
-        gatt = gq
         gatt[...] = nn(low[...], weight(0, tt, LANES, LANES)).astype(BF16)
         pairs[...] = jnp.zeros_like(pairs)
 
-        def window(w, carry):
+        def window(w):
             at = pl.ds(pl.multiple_of(w * PAD, PAD), PAD)
             q4, g4 = stack(qs[tt, at, :]), stack(gatt[at, :])
             p = probs[tt, w]
             dp = nt_dot(kvs[tt, at, LANES:], g4)
             ds = p * (dp - rowsum(p * dp))
             ds_low = ds.astype(BF16)
-            pairs[...] += ds_low.astype(F32)
             gkv[at, :LANES] = nn(ds_low, q4).astype(BF16)
             gkv[at, LANES:CW] = nn(p.astype(BF16), g4).astype(BF16)
-            gatt[at, :] = pick(tn_dot(ds_low, kvs[tt, at, :LANES])).astype(BF16)
+            gq[at, :] = pick(tn_dot(ds_low, kvs[tt, at, :LANES])).astype(BF16)
+            return ds_low.astype(F32)
+
+        def four(hh, carry):
+            total = window(hh * (slots // 2))
+            for j in range(1, slots // 2):
+                total = total + window(hh * (slots // 2) + j)
+            pairs[...] += total
+
+            @pl.when(hh == 0)
+            def _():
+                run_at(i, "b%df", nt)
+
             return carry
 
-        lax.fori_loop(0, slots // 2, window, 0, unroll=4)
-        events(i, out_first)
-        lax.fori_loop(slots // 2, slots, window, 0, unroll=4)
+        lax.fori_loop(0, 2, four, 0)
         gk_gv = gkv[:, :CW]
         put_grad(1, tt, nn(h1t[...], gk_gv))
 
-        @pl.when(i == 1)
-        def _():
-            core_first(1)
-            xb(1, 0).start()
-
-        @pl.when(i == 3)
-        def _():
-            last_out(1)
-
-        left = nn(h1t[...], gatt[...]) * SCALE
+        left = nn(h1t[...], gq[...]) * SCALE
         put_grad(0, tt, jnp.concatenate([left, nn(h2t[...], att[tt])], axis=1))
 
         @pl.when(i == 0)
@@ -766,18 +829,10 @@
             kc(1, 1).start()
             kc(0, 1).start()
 
-        @pl.when(i == 1)
-        def _():
-            core_first(0)
-            xb(0, 0).start()
-
-        @pl.when(i == 3)
-        def _():
-            last_out(0)
-
-        small[tt, 2:3, :] = rowsum(gatt[...].astype(F32)) * SCALE
+        run_at(i, "b%dd", nt)
+        small[tt, 2:3, :] = rowsum(gq[...].astype(F32)) * SCALE
         small[tt, 3:4, :] = rowsum(gkv[:, LANES:CW].astype(F32))
-        grad_q = nt_dot(gatt[...], weight(0, tt, 0, LANES)) * SCALE
+        grad_q = nt_dot(gq[...], weight(0, tt, 0, LANES)) * SCALE
         acc[...] += grad_q + nt_dot(gk_gv, weight(1, tt))
         for h in range(heads):
             lanes = h // 2 * LANES
@@ -788,7 +843,7 @@
                 value = jnp.where(where >= 0, value, 0.0)
                 small[tt, pl.ds(12 + 2 * h + q, 1), :] = rowsum(value)
 
-        events(i, out_second)
+        run_at(i, "b%ds", nt)
         return carry
 
     lax.fori_loop(0, nt, back, 0)
@@ -807,17 +862,14 @@
     gather(xp, gb)
     own_g = pltpu.make_async_copy(gb.at[t], g_all.at[t], loc.at[3])
     own_g.start()
-    for d in range(3):
-        out_copy(1, d).start()
-    last_third(1)
+    run("t1")
+    run("t2")
     for d in range(3):
         small_t(d).wait_recv()
     zb[z] = small[t] + scr[0] + (scr[1] + scr[2])
     for d in range(nz - 1):
         small_z(d).start()
-    fourth(3)
-    c_end()
-    last_third(0)
+    run("t3")
     for d in range(nz - 1):
         small_z(d).wait_recv()
     value = zb[0]
@@ -825,8 +877,10 @@
         value = value + zb[zz]
     sx[...] = value
     small_x().start()
-    fourth(1)
-    fourth(0)
+    run("t4")
+    run("t5")
+    for ch in (2, 4, 3, 5, 1, 0):
+        last(ch)
     small_x().wait_recv()
     tot[...] = sx[...] + syr[...]
     for i in range(2):
@@ -836,24 +890,30 @@
     sent += [out_copy(i, d) for i in range(2) for d in range(3)]
     for ch in range(NCH):
         sent += [ac(ch, j) for j in range(2)] + [kc(ch, j) for j in range(2)]
-        if ch < 5:
-            sent += [az(ch, d) for d in range(nz - 1) if ch > 1]
-            sent += [zr(ch, d) for d in range(nz - 1)]
         if ch < 2:
-            sent += [ax(ch, d) for d in range(nz)] + [ay(ch, d) for d in range(nz)]
-            sent += [xp1(ch, d) for d in range(nz)] + [xb(ch, 0), yb2(ch)]
-        elif ch < 5:
-            sent += [by(ch), bx(ch, 0), bx(ch, 1)]
-    sent += [bx(1, 1), cy(), cx(0), cx(1)]
-    sent += [ya(2), xa(2), ya(3), xa(3), xb(4, 0), xb(4, 1), yb2(4), xc(0), xc(1), yc()]
-    sent += [zc(d, j) for d in range(nz - 1) for j in range(2)]
-    sent += [cz(d, j) for d in range(nz - 1) for j in range(2)]
+            sent += [ax(ch, zz) for zz in range(nz)] + [ay(ch, zz) for zz in range(nz)]
+            sent += [az(ch, d) for d in range(nz - 1)] + ([bx(1, 1)] if ch else [])
+        else:
+            sent += az_all(ch)
+            sent += [cy(ch)] if WAY_IN[ch] in "CE" else [by(ch)]
+            if WAY_IN[ch] == "C":
+                sent += [cx(ch, 0), cx(ch, 1)]
+            else:
+                sent += [bx(ch, 0)] + ([] if WAY_IN[ch] == "A" else [bx(ch, 1)])
+        if WAY_OUT[ch] == "C":
+            sent += [zc(ch, d, j) for d in range(nz - 1) for j in range(2)]
+            sent += [xc(ch, 0), xc(ch, 1), yc(ch)]
+            continue
+        sent += [zr(ch, d) for d in range(nz - 1)]
+        if WAY_OUT[ch] == "A":
+            sent += [ya(ch), xa(ch)]
+        else:
+            sent += [xb(ch, 0), yb2(ch)]
+            sent += [xp1(ch, d) for d in range(nz)] if ch < 2 else [xb(ch, 1)]
     sent += [small_t(d) for d in range(3)] + [small_x()]
     sent += [small_z(d) for d in range(nz - 1)]
     for copy in sent:
         copy.wait_send()
-    line_sent(0)
-    line_sent(1)
     own_y.wait()
     own_g.wait()
 
@@ -872,6 +932,7 @@
         return [DMA(shape), DMA(shape)]
 
     small = (SROWS, LANES)
+    n_c = max(1, WAY_OUT.count("C"))
     return pl.pallas_call(
         functools.partial(block, nt, nz, slots),
         name="block",
@@ -881,9 +942,10 @@
             jax.ShapeDtypeStruct((NCH, deep, CW), F32),
             jax.ShapeDtypeStruct(small, F32),
         ),
-        in_specs=[SM, ANY, ANY] + [VM] * 18,
+        in_specs=[SM] + [ANY] * 20,
         out_specs=(ANY, ANY, VM, VM),
-        scratch_shapes=[
+        scratch_shapes=[vm(arg.shape, arg.dtype) for arg in args[9:]]
+        + [
             vm(row),
             vm(row),
             vm((NCH, nt) + piece),
@@ -891,12 +953,12 @@
             vm((nt, PAD, wide), F32),
             vm((NCH, nt) + piece),
             vm((NCH, 2) + piece),
-            vm((2,) + piece),
-            vm((3, 2, nz, deep, CW)),
+            vm((max(1, WAY_OUT.count("A")),) + piece),
+            vm((WAY_OUT.count("B"), 2, nz, deep, CW)),
             vm((NCH, nz, deep, CW)),
             vm((NCH, nz - 1, deep, CW)),
-            vm((nz - 1, 2, 2, deep, CW)),
-            vm((3, deep, CW)),
+            vm((n_c, nz - 1, 2, 2, deep, CW)),
+            vm((n_c, 3, deep, CW)),
             vm((3,) + small, F32),
             vm(small, F32),
             vm(small, F32),
@@ -927,22 +989,22 @@
             vm((rows, C)),
             vm((rows, C)),
             vm((rows, LANES)),
+            vm((rows, LANES)),
             vm((PAD, wide), F32),
             DMA((4,)),
+            DMA((20,)),
         ]
         + pair(3, 3)
         + pair(2, 3)
-        + [DMA((2, 2, nz)), DMA((2, nz))]
-        + pair(NCH, nz - 1)
+        + pair(NCH, nz - 1, 2)
         + pair(2, nz)
         + pair(2, nz)
         + pair(NCH, 2)
         + pair(NCH, 2)
         + pair(NCH)
-        + pair(nz - 1, 2)
         + pair(2, nz)
-        + pair(nz - 1, 2)
-        + pair(3)
+        + pair(n_c, nz - 1, 2)
+        + pair(n_c, 3)
         + pair(NCH, 2)
         + pair(NCH, 2)
         + pair(NCH)
@@ -954,13 +1016,42 @@
     )(*args)
 
 
-def spell(y_all, g_all, fin, tot, *outs):
+def spell(n, *refs):
+    ins, outs, refs = refs[:4], refs[4 : 4 + n], refs[4 + n :]
+    (y_in, g_in, fin, tot), refs = refs[:4], refs[4:]
+    held, (get, put) = refs[:n], refs[n:]
+    steps = ins[0].shape[0]
+    loads = [pltpu.make_async_copy(ins[2], fin, get.at[0])]
+    loads.append(pltpu.make_async_copy(ins[3], tot, get.at[1]))
+    for i in range(steps):
+        for j, ref in enumerate((y_in, g_in)):
+            loads.append(
+                pltpu.make_async_copy(ins[j].at[i], ref.at[i], get.at[2 + 2 * i + j])
+            )
+    for copy in loads:
+        copy.start()
+    loads[0].wait()
+    loads[1].wait()
+    spell_rest(fin, tot, *held[2:])
+    stores = [pltpu.make_async_copy(held[k], outs[k], put.at[k]) for k in range(2, n)]
+    for copy in stores:
+        copy.start()
+    for i in range(steps):
+        for j, ref in enumerate((y_in, g_in)):
+            loads[2 + 2 * i + j].wait()
+            held[j][i] = ref[i].astype(F32)
+            copy = pltpu.make_async_copy(held[j].at[i], outs[j].at[i], put.at[n + 2 * i + j])
+            copy.start()
+            stores.append(copy)
+    for copy in stores:
+        copy.wait()
+
+
+def spell_rest(fin, tot, *outs):
     (
-        y_out, g_out, d_g1, d_s1, d_wq, d_wk, d_wv, d_bq, d_bv, d_wo, d_bo, d_g2, d_s2, d_wh, d_bh,
+        d_g1, d_s1, d_wq, d_wk, d_wv, d_bq, d_bv, d_wo, d_bo, d_g2, d_s2, d_wh, d_bh,
         d_wd, d_bd, d_tab,
     ) = outs
-    y_out[...] = y_all[...].astype(F32)
-    g_out[...] = g_all[...].astype(F32)
     d_wq[...] = fin[0, :, :LANES]
     d_wk[...] = fin[1, :, :LANES]
     d_wv[...] = fin[1, :, LANES:]
@@ -977,12 +1068,15 @@
 
 
 def spell_call(outs, *args):
+    n, steps = len(outs), args[0].shape[0]
+    held = [pltpu.VMEM(v.shape, v.dtype) for v in args + outs]
     return pl.pallas_call(
-        spell,
+        functools.partial(spell, n),
         name="spell",
         out_shape=outs,
-        in_specs=[VM] * 4,
-        out_specs=(VM,) * len(outs),
+        in_specs=[ANY] * 4,
+        out_specs=(ANY,) * n,
+        scratch_shapes=held + [DMA((2 + 2 * steps,)), DMA((n + 2 * steps,))],
         compiler_params=pltpu.CompilerParams(vmem_limit_bytes=60 * 2**20),
     )(*args)
 

time: 90.7 us -> 84.8 us (0.935)
  Pallas kernels: 89.2 us -> 83.2 us
    pallas_call x1, Pallas kernels: 86.6 us -> 80.5 us  [block_call(): pl.pallas_call(functools.partial(block, nt, nz, slots), name='block', out...]
where the time goes in v5:
time: 84.8 us; the launch traced here: 84.5 us
  Pallas kernels  83.2 us (98%)
  between operations  1.32 us (2%)
    pallas_call x1, Pallas kernels, block_call(): pl.pallas_call(functools.partial(block, nt, nz, slots), name='block', out...  80.5 us
    pallas_call x1, Pallas kernels, spell_call(): pl.pallas_call(functools.partial(spell, n), name='spell', out_shape=outs,...  2.64 us

profile of v5, /device:TPU:0, one launch (start us, length us, event | category | flops | bytes accessed | tf_op | source)
XLA Modules:
  0.0 84.5 jit_solution(13987412413224466792)
XLA Ops:
  1.3 80.5 %block.1 = (bf16[4,392,128]{2,1,0:T(8,128)(2,1)}, bf16[4,392,128]{2,1,0:T(8,128)(2,1)}, f32[6,64,256]{2,1,0:T(8,128)}, f32[24,128]{1,0:T(8,128)}) custom-call(s32[1]{0:T(128)S(6)} %copy.39.refs_0_, bf16[4,392,128]{2,1,0:T(8,128)(2,1)} %bitcast.28, bf16[4,392,128]{2,1,0:T(8,128)(2,1)} %bitcast.29, bf16[64,128]{1,0:T(8,128)(2,1)} %refs_3_.1, ...), custom_call_target="tpu_custom_call" | custom-call | tf_op jit(solution)/shard_map/block/pallas_call | solution.py:936
  81.9 2.6 %spell.1 = (f32[4,392,128]{2,1,0:T(8,128)}, f32[4,392,128]{2,1,0:T(8,128)}, f32[1,128]{1,0:T(1,128)}, f32[1,128]{1,0:T(1,128)}, f32[64,128]{1,0:T(8,128)}, /*ind...) custom-call(bf16[4,392,128]{2,1,0:T(8,128)(2,1)} %get-tuple-element., ...), custom_call_target="tpu_custom_call" | custom-call | tf_op jit(solution)/shard_map/spell/pallas_call | solution.py:1073

commit v6 on v5

--- a/solution.py
+++ b/solution.py
@@ -41,7 +41,6 @@
     "a1s": ("c02", "zy3", "c10",),
     "a3f": ("zx3",),
     "a3s": ("c04",),
-    "mid": ("c12", "c14",),
     "m1": ("yx3", "c03",),
     "m2": ("c15",),
     "m3": ("c05",),
@@ -60,6 +59,7 @@
     "t2": ("g",),
     "t3": ("o31", "o30",),
     "t4": ("o33",),
+    "m0": ("c12", "c14",),
 }
 
 
@@ -125,6 +125,75 @@
     return jnp.sum(value, axis=0, keepdims=True)
 
 
+def arrival_table(nz):
+    keys = [("kc", ch, j) for ch in range(NCH) for j in range(2)]
+    keys += [("ac", ch, j) for ch in range(NCH) for j in range(2)]
+    keys += [("az", ch, d) for ch in range(2) for d in range(nz - 1)]
+    keys += [("tok", i) for i in range(3)] + [("out", i) for i in range(2)]
+    keys += [(kind, ch) for kind in ("ax", "ay") for ch in range(2)]
+    keys += [("bx", 1, 1), ("st",), ("sz",), ("sx",)]
+    for ch in range(2, NCH):
+        keys += [("az", ch), ("by", ch)]
+        if WAY_IN[ch] == "C":
+            keys.append(("cx", ch))
+        else:
+            keys += [("bx", ch, j) for j in range(1 if WAY_IN[ch] == "A" else 2)]
+    for ch in range(NCH):
+        if WAY_OUT[ch] == "C":
+            keys += [("zc", ch), ("xc", ch), ("yc", ch)]
+            continue
+        keys += [("zr", ch), ("q", ch), ("p", ch, 0)]
+        if WAY_OUT[ch] == "B":
+            keys += [("px", ch, d) for d in range(nz)] if ch < 2 else [("p", ch, 1)]
+    return {key: i for i, key in enumerate(keys)}
+
+
+def send_table(nt, nz):
+    whole = {("kc", ch, j): 2 * nz for ch in range(NCH) for j in range(2)}
+    whole.update({("ac", ch, j): 2 * nz for ch in range(NCH) for j in range(2)})
+    sends = {}
+    for ch in range(2):
+        sends.update({("az", ch, d, 0): 1 for d in range(nz - 1)})
+        sends.update({("ax", ch, i): 1 for i in range(nz)})
+        sends.update({("ay", ch, i): 2 - ch for i in range(nz)})
+        sends.update({("px", ch, d): 1 for d in range(nz)})
+    sends["bx", 1, 1] = nz
+    for ch in range(2, NCH):
+        way = WAY_IN[ch]
+        both = 2 if way in "CE" else 1
+        size = 2 if way == "C" else 1
+        sends.update({("az", ch, d, j): size for d in range(nz - 1) for j in range(both)})
+        sends["by", ch] = {"A": 2 * nz, "B": nz, "C": 1, "E": 1}[way]
+        sends.update({("bx", ch, j): 1 if way == "C" else nz for j in range(1 + (way != "A"))})
+    for ch in range(NCH):
+        way = WAY_OUT[ch]
+        if way == "C":
+            sends.update({("zc", ch, d, j): 2 for d in range(nz - 1) for j in range(2)})
+            sends.update({("xc", ch, j): 1 for j in range(3)})
+            continue
+        sends.update({("zr", ch, d): 1 for d in range(nz - 1)})
+        sends["q", ch] = nz
+        sends["p", ch, 0] = 2 * nz if way == "A" else nz
+        if way == "B" and ch > 1:
+            sends["p", ch, 1] = nz
+    order = sorted(sends, key=lambda key: -sends[key])
+    left = sum(sends.values())
+    groups, totals = {key: 0 for key in whole}, [sum(whole.values())]
+    for unit, most in ((2 * nz * nt, NCH), (2 * nz, nt), (2, nz), (1, 1)):
+        goal = unit * min(most, left // unit)
+        if goal:
+            total = 0
+            while total < goal:
+                key = order.pop(0)
+                total += sends[key]
+                groups[key] = len(totals)
+            assert total == goal
+            totals.append(total)
+            left -= total
+    assert not order
+    return groups, totals
+
+
 def block(nt, nz, slots, *refs):
     live, tok, cot, wq, wk, wv, wo, wh, wd = refs[:9]
     outside, refs = refs[9:21], refs[21:]
@@ -135,9 +204,7 @@
         xg, cg, gw, vg, rg, dv, rc, ry, rx, r3, rz, rzc, rxc, scr, syr, sx, zb, small, yb, gb, square, mask, inv,
         xs, xp, gy, h1, h1t, h2t, gyt, qs, kvs, probs, att, acc, acc2, n1, r1, n2, r2, low, gkv, gq, gatt,
         pairs,
-        loc, ld, tok_s, tok_r, out_s, out_r, az_s, az_r, ax_s, ax_r, ay_s, ay_r, ac_s, ac_r,
-        bx_s, bx_r, by_s, by_r, px_s, px_r, zc_s, zc_r, xc_s,
-        xc_r, k_s, k_r, p_s, p_r, q_s, q_r, rz_s, rz_r, sm_s, sm_r,
+        loc, ld, rs, ss,
     ) = refs
     heads = LANES // HDIM
     rows = slots * PAD
@@ -160,6 +227,24 @@
     for peer in peers:
         pl.semaphore_signal(barrier, inc=1, device_id=peer, device_id_type=MESH)
 
+    arrival, (group_of, totals) = arrival_table(nz), send_table(nt, nz)
+
+    def coming(*key):
+        return rs.at[arrival[key]]
+
+    def going(*key):
+        return ss.at[group_of[key]]
+
+    def blocks(n):
+        for unit, ref in ((2 * nz * nt, gw), (2 * nz, gw.at[0]), (2, gw.at[0, 0])):
+            if n % unit == 0:
+                return ref.at[pl.ds(0, n // unit)]
+        assert n == 1
+        return gw.at[0, 0, 0, 0]
+
+    def await_bytes(ref, sem):
+        pltpu.make_async_copy(ref, ref, sem).wait()
+
     def far(src, dst, send, recv, peer):
         return pltpu.make_async_remote_copy(
             src_ref=src, dst_ref=dst, send_sem=send, recv_sem=recv, device_id=peer,
@@ -170,25 +255,22 @@
         src, dst = ((tok, xg), (cot, cg), (vg, vg))[i]
         peer = ts[d]
         src = src.at[peer[1]] if i < 2 else src.at[t]
-        return far(src, dst.at[t], tok_s.at[i, d], tok_r.at[i, d], peer)
+        return far(src, dst.at[t], ss.at[len(totals) + i], coming("tok", i), peer)
 
     def out_copy(i, d):
         src, dst = ((yb, y_all), (gb, g_all))[i]
         peer = ts[d]
-        return far(src.at[peer[1]], dst.at[t], out_s.at[i, d], out_r.at[i, d], peer)
-
-    def az(ch, d, j=0):
-        far_t = t2 if j else t
-        ref = gw.at[ch, far_t, z] if WAY_IN[ch] == "C" else gw.at[ch, far_t, z, x]
-        return far(ref, ref, az_s.at[ch, d, j], az_r.at[ch, d, j], zs[d])
-
-    def az_all(ch):
-        both = 2 if WAY_IN[ch] in "CE" else 1
-        return [az(ch, d, j) for d in range(nz - 1) for j in range(both)]
+        return far(src.at[peer[1]], dst.at[t], ss.at[len(totals) + 3 + i], coming("out", i), peer)
+
+    def az_await(ch):
+        n = (nz - 1) * {"A": 1, "B": 1, "C": 4, "E": 2}[WAY_IN[ch]]
+        size = n // (nz - 1)
+        ref = rz.at[0] if size == 1 else rzc.at[0, :, :, 0] if size == 2 else rzc.at[0]
+        await_bytes(ref, coming("az", ch))
 
     def az_from(ch, zz):
-        ref, d = gw.at[ch, t, z, x], lax.rem(z - zz + nz, nz) - 1
-        return far(ref, ref, az_s.at[ch, d, 0], az_r.at[ch, d, 0], xpeer)
+        d = lax.rem(z - zz + nz, nz) - 1
+        await_bytes(gw.at[ch, t, z, x], rs.at[arrival["az", ch, 0] + d])
 
     def far_first(k):
         rising = k + jnp.where(z > k, 0, 1)
@@ -202,54 +284,54 @@
             for j in range(2 if WAY_IN[ch] in "CE" else 1):
                 far_t = t2 if j else t
                 ref = gw.at[ch, far_t, z] if WAY_IN[ch] == "C" else gw.at[ch, far_t, z, x]
-                peer = (zz * 2 + x, t)
-                far(ref, ref, az_s.at[ch, d, j], az_r.at[ch, d, j], peer).start()
+                there = rs.at[arrival["az", ch, 0] + d] if ch < 2 else coming("az", ch)
+                far(ref, ref, going("az", ch, k, j), there, (zz * 2 + x, t)).start()
 
     def zr_start(ch, k):
         zz, d = far_first(k)
         src = dv.at[ch, t, zz, x]
-        far(src, rz.at[ch, d], rz_s.at[ch, d], rz_r.at[ch, d], (zz * 2 + x, t)).start()
-
-    def ax(ch, zz):
+        far(src, rz.at[ch, d], going("zr", ch, k), coming("zr", ch), (zz * 2 + x, t)).start()
+
+    def ax(ch, zz, i):
         ref = gw.at[ch, t, zz, x]
-        return far(ref, ref, ax_s.at[ch, zz], ax_r.at[ch, zz], xpeer)
-
-    def ay(ch, zz):
+        return far(ref, ref, going("ax", ch, i), coming("ax", ch), xpeer)
+
+    def ay(ch, zz, i):
         ref = gw.at[ch, t, zz] if ch == 0 else gw.at[ch, t, zz, x]
-        return far(ref, ref, ay_s.at[ch, zz], ay_r.at[ch, zz], ypeer)
+        return far(ref, ref, going("ay", ch, i), coming("ay", ch), ypeer)
 
     def bx(ch, j):
         ref = gw.at[ch, t2 if j else t, :, x]
-        return far(ref, ref, bx_s.at[ch, j], bx_r.at[ch, j], xpeer)
+        return far(ref, ref, going("bx", ch, j), coming("bx", ch, j), xpeer)
 
     def by(ch):
         ref = gw.at[ch, t] if WAY_IN[ch] == "A" else gw.at[ch, t, :, x]
-        return far(ref, ref, by_s.at[ch], by_r.at[ch], ypeer)
+        return far(ref, ref, going("by", ch), coming("by", ch), ypeer)
 
     def cy(ch):
         ref = gw.at[ch, t, z, x]
-        return far(ref, ref, by_s.at[ch], by_r.at[ch], ypeer)
+        return far(ref, ref, going("by", ch), coming("by", ch), ypeer)
 
     def cx(ch, j):
         ref = gw.at[ch, t2 if j else t, z, x]
-        return far(ref, ref, bx_s.at[ch, j], bx_r.at[ch, j], xpeer)
+        return far(ref, ref, going("bx", ch, j), coming("cx", ch), xpeer)
 
     def ac(ch, j):
         ref = gw.at[ch, t2 if j else t]
-        return far(ref, ref, ac_s.at[ch, j], ac_r.at[ch, j], cpeer)
+        return far(ref, ref, going("ac", ch, j), coming("ac", ch, j), cpeer)
 
     def kc(ch, j):
-        return far(dv.at[ch, t1 if j else t3], rc.at[ch, j], k_s.at[ch, j], k_r.at[ch, j], cpeer)
+        return far(dv.at[ch, t1 if j else t3], rc.at[ch, j], ss.at[0], rs.at[ch * 2 + j], cpeer)
 
     a_slot = {ch: i for i, ch in enumerate(c for c in range(NCH) if WAY_OUT[c] == "A")}
     b_slot = {ch: i for i, ch in enumerate(c for c in range(NCH) if WAY_OUT[c] == "B")}
     c_slot = {ch: i for i, ch in enumerate(c for c in range(NCH) if WAY_OUT[c] == "C")}
 
     def ya(ch):
-        return far(dv.at[ch, t2], ry.at[a_slot[ch]], p_s.at[ch, 0], p_r.at[ch, 0], ypeer)
+        return far(dv.at[ch, t2], ry.at[a_slot[ch]], going("p", ch, 0), coming("p", ch, 0), ypeer)
 
     def xa(ch):
-        return far(dv.at[ch, t, :, 1 - x], r3.at[ch], q_s.at[ch], q_r.at[ch], xpeer)
+        return far(dv.at[ch, t, :, 1 - x], r3.at[ch], going("q", ch), coming("q", ch), xpeer)
 
     def piece_of(d):
         return far_first(d)[0] if d < nz - 1 else z
@@ -257,61 +339,54 @@
     def xp1(ch, d):
         zz = piece_of(d)
         src, dst = dv.at[ch, t, zz, 1 - x], rx.at[b_slot[ch], 1, zz]
-        return far(src, dst, px_s.at[ch, d], px_r.at[ch, d], xpeer)
+        return far(src, dst, going("px", ch, d), coming("px", ch, d), xpeer)
 
     def xb(ch, j):
         src = dv.at[ch, t if j else t2, :, 1 - x]
-        return far(src, rx.at[b_slot[ch], j], p_s.at[ch, j], p_r.at[ch, j], xpeer)
+        return far(src, rx.at[b_slot[ch], j], going("p", ch, j), coming("p", ch, j), xpeer)
 
     def yb2(ch):
-        return far(dv.at[ch, t2, :, x], r3.at[ch], q_s.at[ch], q_r.at[ch], ypeer)
-
-    def zr(ch, d):
-        src = dv.at[ch, t, lax.rem(z + d + 1, nz), x]
-        return far(src, rz.at[ch, d], rz_s.at[ch, d], rz_r.at[ch, d], zs[d])
-
-    def zc(ch, d, j):
-        src, i = dv.at[ch, t if j else t2, lax.rem(z + d + 1, nz)], c_slot[ch]
-        return far(src, rzc.at[i, d, j], zc_s.at[i, d, j], zc_r.at[i, d, j], zs[d])
+        return far(dv.at[ch, t2, :, x], r3.at[ch], going("q", ch), coming("q", ch), ypeer)
 
     def zc_start(ch, j):
         i = c_slot[ch]
         for k in range(nz - 1):
             zz, d = far_first(k)
             src, peer = dv.at[ch, t if j else t2, zz], (zz * 2 + x, t)
-            far(src, rzc.at[i, d, j], zc_s.at[i, d, j], zc_r.at[i, d, j], peer).start()
+            far(src, rzc.at[i, d, j], going("zc", ch, k, j), coming("zc", ch), peer).start()
 
     def xc(ch, j):
         src, i = dv.at[ch, t if j else t2, z, 1 - x], c_slot[ch]
-        return far(src, rxc.at[i, j], xc_s.at[i, j], xc_r.at[i, j], xpeer)
+        return far(src, rxc.at[i, j], going("xc", ch, j), coming("xc", ch), xpeer)
 
     def yc(ch):
         i = c_slot[ch]
-        return far(dv.at[ch, t2, z, x], rxc.at[i, 2], xc_s.at[i, 2], xc_r.at[i, 2], ypeer)
+        return far(dv.at[ch, t2, z, x], rxc.at[i, 2], going("xc", ch, 2), coming("yc", ch), ypeer)
 
     def small_t(d):
-        return far(small.at[ts[d][1]], scr.at[d], sm_s.at[d], sm_r.at[d], ts[d])
+        return far(small.at[ts[d][1]], scr.at[d], ss.at[len(totals) + 5], coming("st"), ts[d])
 
     def small_z(d):
-        return far(zb.at[z], zb.at[z], sm_s.at[3 + d], sm_r.at[3 + d], zs[d])
+        return far(zb.at[z], zb.at[z], ss.at[len(totals) + 6], coming("sz"), zs[d])
 
     def small_x():
-        return far(sx, syr, sm_s.at[2 + nz], sm_r.at[2 + nz], xpeer)
+        return far(sx, syr, ss.at[len(totals) + 7], coming("sx"), xpeer)
 
     def lanes(ch, i, size):
         return gw.at[ch, t, z, x, :, pl.ds(i * size, size)]
 
-    loads = [(wq, lanes(0, 0, LANES)), (wo, lanes(0, 1, LANES))]
-    loads += [(wk, lanes(1, 0, LANES)), (wv, lanes(1, 1, LANES))]
+    loads = [(wq, lanes(0, 0, LANES), 0), (wo, lanes(0, 1, LANES), 0)]
+    loads += [(wk, lanes(1, 0, LANES), 0), (wv, lanes(1, 1, LANES), 0)]
     for i in range(2):
-        loads += [(wh.at[:, pl.ds(i * CW, CW)], gw.at[2 + i, t, z, x])]
-        loads += [(wd.at[:, pl.ds(i * CW, CW)], gw.at[4 + i, t, z, x])]
-    loads += list(zip(outside, inside))
-    loads = [pltpu.make_async_copy(*pair, ld.at[i]) for i, pair in enumerate(loads)]
-    for copy in loads:
-        copy.start()
-    for copy in loads:
-        copy.wait()
+        loads += [(wh.at[:, pl.ds(i * CW, CW)], gw.at[2 + i, t, z, x], 1)]
+        loads += [(wd.at[:, pl.ds(i * CW, CW)], gw.at[4 + i, t, z, x], 1)]
+    loads += [(src, dst, 2 + i) for i, (src, dst) in enumerate(zip(outside, inside))]
+    for src, dst, i in loads:
+        pltpu.make_async_copy(src, dst, ld.at[i]).start()
+    await_bytes(gw.at[0, 0, 0], ld.at[0])
+    await_bytes(gw.at[0, 0, pl.ds(0, 2)], ld.at[1])
+    for src, dst, i in loads[8:]:
+        pltpu.make_async_copy(src, dst, ld.at[i]).wait()
     for i, ref in enumerate((g1, s1, bq, bv, bo, g2, s2, bd)):
         vg[t, i : i + 1, :] = ref[...]
     vg[t, 8:12, :] = bh[...]
@@ -332,10 +407,10 @@
     for d in range(3):
         tok_copy(2, d).start()
     az_start(1)
-    ax(1, z).start()
-    ay(1, z).start()
+    ax(1, z, 0).start()
+    ay(1, z, 0).start()
     az_start(0)
-    ax(0, z).start()
+    ax(0, z, 0).start()
     for d in range(3):
         tok_copy(0, d).start()
     for ch in early:
@@ -422,36 +497,38 @@
     def tok_all(i):
         return [tok_copy(i, d) for d in range(3)]
 
-    def arrivals(name):
+    def await_tok(i):
+        await_bytes((xg, cg, vg)[i].at[pl.ds(0, 3)], coming("tok", i))
+
+    def await_name(name):
         kind, ch = name[:-1], int(name[-1])
         if kind == "x":
-            return [ax(ch, zz) for zz in range(nz)]
-        if kind == "ay":
-            return [ay(ch, zz) for zz in range(nz)]
-        if kind == "z":
-            return az_all(ch)
-        if kind in ("xo", "xt"):
-            return [bx(ch, int(kind == "xt"))]
-        if kind == "yo":
-            return [by(ch)]
-        if kind in ("k0", "k1"):
-            return [ac(ch, int(kind == "k1"))]
-        if kind in ("r0", "r1"):
-            return [kc(ch, int(kind == "r1"))]
-        if kind == "ya":
-            return [ya(ch)]
-        if kind == "xa":
-            return [xa(ch)]
-        if kind == "xbt":
-            return [xb(ch, 0)]
-        if kind == "xbo":
-            return [xb(ch, 1)]
-        if kind == "yb":
-            return [yb2(ch)]
-        if kind == "zc":
-            return [zc(ch, d, j) for d in range(nz - 1) for j in range(2)]
-        assert kind == "xc"
-        return [xc(ch, 0), xc(ch, 1)]
+            await_bytes(r3.at[0], coming("ax", ch))
+        elif kind == "ay":
+            await_bytes(r3.at[0] if ch else gw.at[0, 0], coming("ay", ch))
+        elif kind == "z":
+            az_await(ch)
+        elif kind in ("xo", "xt"):
+            bx(ch, int(kind == "xt")).wait_recv()
+        elif kind == "yo":
+            by(ch).wait_recv()
+        elif kind in ("k0", "k1"):
+            ac(ch, int(kind == "k1")).wait_recv()
+        elif kind in ("r0", "r1"):
+            kc(ch, int(kind == "r1")).wait_recv()
+        elif kind == "ya":
+            ya(ch).wait_recv()
+        elif kind == "xa":
+            xa(ch).wait_recv()
+        elif kind in ("xbt", "xbo"):
+            xb(ch, int(kind == "xbo")).wait_recv()
+        elif kind == "yb":
+            yb2(ch).wait_recv()
+        elif kind == "zc":
+            await_bytes(rzc.at[0], coming("zc", ch))
+        else:
+            assert kind == "xc"
+            await_bytes(gw.at[0, 0, 0], coming("xc", ch))
 
     def own_of(ch):
         return ("z%d" if WAY_IN[ch] == "C" else "xo%d") % ch
@@ -494,8 +571,7 @@
     def arrive(entry):
         for name in waits_of(entry):
             if first_use[name] == entry:
-                for copy in arrivals(name):
-                    copy.wait_recv()
+                await_name(name)
 
     def act(entry):
         arrive(entry)
@@ -511,10 +587,10 @@
         way = WAY_OUT[ch]
         if kind == "ay":
             for zz in range(nz):
-                ay(ch, zz).start()
+                ay(ch, zz, zz).start()
         elif kind == "az":
-            for j in range(2 if WAY_IN[ch] == "C" else 0):
-                cx(ch, j).wait_recv()
+            if WAY_IN[ch] == "C":
+                await_bytes(gw.at[0, 0, 0], coming("cx", ch))
             az_start(ch)
         elif kind == "zx":
             bx(ch, 0).start()
@@ -583,8 +659,8 @@
             fin[ch] = dv[ch, t, z, x].astype(F32) + rxc[c_slot[ch], 2].astype(F32)
             return
         value = dv[ch, t, z, x].astype(F32)
+        await_bytes(rz.at[0], coming("zr", ch))
         for d in range(nz - 1):
-            zr(ch, d).wait_recv()
             value = value + rz[ch, d].astype(F32)
         fin[ch] = value
 
@@ -615,20 +691,18 @@
     for ch in (1, 0):
         for k in range(nz - 1):
             zz, _ = far_first(nz - 2 - k)
-            az_from(ch, zz).wait_recv()
-            ax(ch, zz).start()
+            az_from(ch, zz)
+            ax(ch, zz, k + 1).start()
             if ch == 1:
-                ay(ch, zz).start()
+                ay(ch, zz, k + 1).start()
     for ch in early:
         if ch not in first:
             cross(ch)
     run("h1")
-    for copy in tok_all(2):
-        copy.wait_recv()
+    await_tok(2)
     for tt in range(nt):
         bias_of(tt)
-    for d in range(3):
-        tok_copy(0, d).wait_recv()
+    await_tok(0)
     spread(xg, xp)
     gain1, shift1 = wide(0), wide(1)
 
@@ -696,8 +770,7 @@
 
     lax.fori_loop(0, nt, attend, 0)
     own_cot.wait()
-    for d in range(3):
-        tok_copy(1, d).wait_recv()
+    await_tok(1)
     spread(cg, gy)
     b_out, gain2, shift2 = wide(4), wide(5), wide(6)
 
@@ -864,14 +937,12 @@
     own_g.start()
     run("t1")
     run("t2")
-    for d in range(3):
-        small_t(d).wait_recv()
+    await_bytes(scr, coming("st"))
     zb[z] = small[t] + scr[0] + (scr[1] + scr[2])
     for d in range(nz - 1):
         small_z(d).start()
     run("t3")
-    for d in range(nz - 1):
-        small_z(d).wait_recv()
+    await_bytes(zb.at[pl.ds(0, nz - 1)], coming("sz"))
     value = zb[0]
     for zz in range(1, nz):
         value = value + zb[zz]
@@ -884,36 +955,14 @@
     small_x().wait_recv()
     tot[...] = sx[...] + syr[...]
     for i in range(2):
-        for d in range(3):
-            out_copy(i, d).wait_recv()
-    sent = [tok_copy(i, d) for i in range(3) for d in range(3)]
-    sent += [out_copy(i, d) for i in range(2) for d in range(3)]
-    for ch in range(NCH):
-        sent += [ac(ch, j) for j in range(2)] + [kc(ch, j) for j in range(2)]
-        if ch < 2:
-            sent += [ax(ch, zz) for zz in range(nz)] + [ay(ch, zz) for zz in range(nz)]
-            sent += [az(ch, d) for d in range(nz - 1)] + ([bx(1, 1)] if ch else [])
-        else:
-            sent += az_all(ch)
-            sent += [cy(ch)] if WAY_IN[ch] in "CE" else [by(ch)]
-            if WAY_IN[ch] == "C":
-                sent += [cx(ch, 0), cx(ch, 1)]
-            else:
-                sent += [bx(ch, 0)] + ([] if WAY_IN[ch] == "A" else [bx(ch, 1)])
-        if WAY_OUT[ch] == "C":
-            sent += [zc(ch, d, j) for d in range(nz - 1) for j in range(2)]
-            sent += [xc(ch, 0), xc(ch, 1), yc(ch)]
-            continue
-        sent += [zr(ch, d) for d in range(nz - 1)]
-        if WAY_OUT[ch] == "A":
-            sent += [ya(ch), xa(ch)]
-        else:
-            sent += [xb(ch, 0), yb2(ch)]
-            sent += [xp1(ch, d) for d in range(nz)] if ch < 2 else [xb(ch, 1)]
-    sent += [small_t(d) for d in range(3)] + [small_x()]
-    sent += [small_z(d) for d in range(nz - 1)]
-    for copy in sent:
-        copy.wait_send()
+        await_bytes((yb, gb)[i].at[pl.ds(0, 3)], coming("out", i))
+    for i, n in enumerate(totals):
+        await_bytes(blocks(n), ss.at[i])
+    three = (xg, cg, vg, yb, gb, small)
+    for i, ref in enumerate(three):
+        await_bytes(ref.at[pl.ds(0, 3)], ss.at[len(totals) + i])
+    await_bytes(zb.at[pl.ds(0, nz - 1)], ss.at[len(totals) + 6])
+    await_bytes(sx, ss.at[len(totals) + 7])
     own_y.wait()
     own_g.wait()
 
@@ -927,9 +976,6 @@
 
     def vm(shape, kind=BF16):
         return pltpu.VMEM(shape, kind)
-
-    def pair(*shape):
-        return [DMA(shape), DMA(shape)]
 
     small = (SROWS, LANES)
     n_c = max(1, WAY_OUT.count("C"))
@@ -992,24 +1038,10 @@
             vm((rows, LANES)),
             vm((PAD, wide), F32),
             DMA((4,)),
-            DMA((20,)),
-        ]
-        + pair(3, 3)
-        + pair(2, 3)
-        + pair(NCH, nz - 1, 2)
-        + pair(2, nz)
-        + pair(2, nz)
-        + pair(NCH, 2)
-        + pair(NCH, 2)
-        + pair(NCH)
-        + pair(2, nz)
-        + pair(n_c, nz - 1, 2)
-        + pair(n_c, 3)
-        + pair(NCH, 2)
-        + pair(NCH, 2)
-        + pair(NCH)
-        + pair(NCH, nz - 1)
-        + pair(3 + nz),
+            DMA((14,)),
+            DMA((len(arrival_table(nz)),)),
+            DMA((len(send_table(nt, nz)[1]) + 8,)),
+        ],
         compiler_params=pltpu.CompilerParams(
             collective_id=0, has_side_effects=True, vmem_limit_bytes=60 * 2**20
         ),
@@ -1033,18 +1065,27 @@
     loads[0].wait()
     loads[1].wait()
     spell_rest(fin, tot, *held[2:])
-    stores = [pltpu.make_async_copy(held[k], outs[k], put.at[k]) for k in range(2, n)]
-    for copy in stores:
-        copy.start()
+    like = {}
+    for k in range(2, n):
+        slot = 2 + list(like).index(held[k].shape) if held[k].shape in like else 2 + len(like)
+        like.setdefault(held[k].shape, []).append(k)
+        pltpu.make_async_copy(held[k], outs[k], put.at[slot]).start()
     for i in range(steps):
         for j, ref in enumerate((y_in, g_in)):
             loads[2 + 2 * i + j].wait()
             held[j][i] = ref[i].astype(F32)
-            copy = pltpu.make_async_copy(held[j].at[i], outs[j].at[i], put.at[n + 2 * i + j])
-            copy.start()
-            stores.append(copy)
-    for copy in stores:
-        copy.wait()
+            pltpu.make_async_copy(held[j].at[i], outs[j].at[i], put.at[j]).start()
+    for j in range(2):
+        pltpu.make_async_copy(held[j], outs[j], put.at[j]).wait()
+    for slot, (shape, ks) in enumerate(like.items()):
+        size = len(ks) * shape[0] * shape[1]
+        if len(ks) == 1:
+            ref = held[ks[0]]
+        elif shape[0] == 1:
+            ref = tot.at[pl.ds(0, len(ks))]
+        else:
+            ref = fin.at[pl.ds(0, size // (fin.shape[1] * fin.shape[2]))]
+        pltpu.make_async_copy(ref, ref, put.at[2 + slot]).wait()
 
 
 def spell_rest(fin, tot, *outs):
@@ -1076,7 +1117,7 @@
         out_shape=outs,
         in_specs=[ANY] * 4,
         out_specs=(ANY,) * n,
-        scratch_shapes=held + [DMA((2 + 2 * steps,)), DMA((n + 2 * steps,))],
+        scratch_shapes=held + [DMA((2 + 2 * steps,)), DMA((2 + len({v.shape for v in outs[2:]}),))],
         compiler_params=pltpu.CompilerParams(vmem_limit_bytes=60 * 2**20),
     )(*args)
 

time: 84.8 us -> 81.8 us (0.965)
  Pallas kernels: 83.2 us -> 80.1 us
    pallas_call x1, Pallas kernels: 80.5 us -> 77.7 us  [block_call(): pl.pallas_call(functools.partial(block, nt, nz, slots), name='block', out...]
where the time goes in v6:
time: 81.8 us; the launch traced here: 81.5 us
  Pallas kernels  80.1 us (98%)
  between operations  1.32 us (2%)
    pallas_call x1, Pallas kernels, block_call(): pl.pallas_call(functools.partial(block, nt, nz, slots), name='block', out...  77.7 us
    pallas_call x1, Pallas kernels, spell_call(): pl.pallas_call(functools.partial(spell, n), name='spell', out_shape=outs,...  2.47 us

profile of v6, /device:TPU:0, one launch (start us, length us, event | category | flops | bytes accessed | tf_op | source)
XLA Modules:
  0.0 81.5 jit_solution(13157343275847734281)
XLA Ops:
  1.3 77.7 %block.1 = (bf16[4,392,128]{2,1,0:T(8,128)(2,1)}, bf16[4,392,128]{2,1,0:T(8,128)(2,1)}, f32[6,64,256]{2,1,0:T(8,128)}, f32[24,128]{1,0:T(8,128)}) custom-call(s32[1]{0:T(128)S(6)} %copy.39.refs_0_, bf16[4,392,128]{2,1,0:T(8,128)(2,1)} %bitcast.28, bf16[4,392,128]{2,1,0:T(8,128)(2,1)} %bitcast.29, bf16[64,128]{1,0:T(8,128)(2,1)} %refs_3_.1, ...), custom_call_target="tpu_custom_call" | custom-call | tf_op jit(solution)/shard_map/block/pallas_call | solution.py:982
  79.0 2.5 %spell.1 = (f32[4,392,128]{2,1,0:T(8,128)}, f32[4,392,128]{2,1,0:T(8,128)}, f32[1,128]{1,0:T(1,128)}, f32[1,128]{1,0:T(1,128)}, f32[64,128]{1,0:T(8,128)}, /*ind...) custom-call(bf16[4,392,128]{2,1,0:T(8,128)(2,1)} %get-tuple-element., ...), custom_call_target="tpu_custom_call" | custom-call | tf_op jit(solution)/shard_map/spell/pallas_call | solution.py:1114

commit v7 on v6

--- a/solution.py
+++ b/solution.py
@@ -38,7 +38,7 @@
     "h3": ("az3",),
     "a0f": ("c11", "cot",),
     "a1f": ("zt4", "az5", "xy2", "zx4",),
-    "a1s": ("c02", "zy3", "c10",),
+    "a1s": ("c02", "zy3",),
     "a3f": ("zx3",),
     "a3s": ("c04",),
     "m1": ("yx3", "c03",),
@@ -53,13 +53,14 @@
     "b1d": ("ot1", "o25", "ot0",),
     "b2d": ("o34",),
     "b3f": ("o21",),
-    "b3d": ("oo1", "oo0",),
+    "b3d": ("oo0",),
     "b3s": ("o35",),
     "t1": ("o20", "o23",),
-    "t2": ("g",),
-    "t3": ("o31", "o30",),
-    "t4": ("o33",),
+    "t2": ("g", "o31",),
+    "t3": ("o33", "o30",),
     "m0": ("c12", "c14",),
+    "b3e": ("oo1",),
+    "a2f": ("c10",),
 }
 
 
@@ -75,7 +76,7 @@
         out += [f"use_m{k}"] + list(sched.get(f"m{k}", ()))
     out += sched.get("turn", ())
     for i in range(4):
-        for part in "fds":
+        for part in "feds":
             out += sched.get(f"b{i}{part}", ())
     for i in range(1, 6):
         out += sched.get(f"t{i}", ())
@@ -888,6 +889,7 @@
         lax.fori_loop(0, 2, four, 0)
         gk_gv = gkv[:, :CW]
         put_grad(1, tt, nn(h1t[...], gk_gv))
+        run_at(i, "b%de", nt)
 
         left = nn(h1t[...], gq[...]) * SCALE
         put_grad(0, tt, jnp.concatenate([left, nn(h2t[...], att[tt])], axis=1))

time: 81.8 us -> 81 us (level)
  no operation moved by 1% of the time
where the time goes in v7:
time: 81 us; the launch traced here: 80.7 us
  Pallas kernels  79.4 us (98%)
  between operations  1.32 us (2%)
    pallas_call x1, Pallas kernels, block_call(): pl.pallas_call(functools.partial(block, nt, nz, slots), name='block', out...  76.9 us
    pallas_call x1, Pallas kernels, spell_call(): pl.pallas_call(functools.partial(spell, n), name='spell', out_shape=outs,...  2.47 us

profile of v7, /device:TPU:0, one launch (start us, length us, event | category | flops | bytes accessed | tf_op | source)
XLA Modules:
  0.0 80.7 jit_solution(7416313360082395665)
XLA Ops:
  1.3 76.9 %block.1 = (bf16[4,392,128]{2,1,0:T(8,128)(2,1)}, bf16[4,392,128]{2,1,0:T(8,128)(2,1)}, f32[6,64,256]{2,1,0:T(8,128)}, f32[24,128]{1,0:T(8,128)}) custom-call(s32[1]{0:T(128)S(6)} %copy.39.refs_0_, bf16[4,392,128]{2,1,0:T(8,128)(2,1)} %bitcast.28, bf16[4,392,128]{2,1,0:T(8,128)(2,1)} %bitcast.29, bf16[64,128]{1,0:T(8,128)(2,1)} %refs_3_.1, ...), custom_call_target="tpu_custom_call" | custom-call | tf_op jit(solution)/shard_map/block/pallas_call | solution.py:984
  78.3 2.5 %spell.1 = (f32[4,392,128]{2,1,0:T(8,128)}, f32[4,392,128]{2,1,0:T(8,128)}, f32[1,128]{1,0:T(1,128)}, f32[1,128]{1,0:T(1,128)}, f32[64,128]{1,0:T(8,128)}, /*ind...) custom-call(bf16[4,392,128]{2,1,0:T(8,128)(2,1)} %get-tuple-element., ...), custom_call_target="tpu_custom_call" | custom-call | tf_op jit(solution)/shard_map/spell/pallas_call | solution.py:1116

commit v8 on v7

--- a/solution.py
+++ b/solution.py
@@ -47,7 +47,7 @@
     "m4": ("o14", "c13", "ot2", "oo2",),
     "m7": ("o22", "oo3", "oo5",),
     "turn": ("ot3",),
-    "b0f": ("ot5", "yout",),
+    "b0f": ("ot5",),
     "b0d": ("o24",),
     "b0s": ("o32",),
     "b1d": ("ot1", "o25", "ot0",),
@@ -61,6 +61,7 @@
     "m0": ("c12", "c14",),
     "b3e": ("oo1",),
     "a2f": ("c10",),
+    "b1f": ("yout",),
 }
 
 

time: 81 us -> 81 us (level)
  no operation moved by 1% of the time
where the time goes in v8:
time: 81 us; the launch traced here: 80.7 us
  Pallas kernels  79.4 us (98%)
  between operations  1.32 us (2%)
    pallas_call x1, Pallas kernels, block_call(): pl.pallas_call(functools.partial(block, nt, nz, slots), name='block', out...  76.9 us
    pallas_call x1, Pallas kernels, spell_call(): pl.pallas_call(functools.partial(spell, n), name='spell', out_shape=outs,...  2.47 us

profile of v8, /device:TPU:0, one launch (start us, length us, event | category | flops | bytes accessed | tf_op | source)
XLA Modules:
  0.0 80.7 jit_solution(10699620956632101616)
XLA Ops:
  1.3 76.9 %block.1 = (bf16[4,392,128]{2,1,0:T(8,128)(2,1)}, bf16[4,392,128]{2,1,0:T(8,128)(2,1)}, f32[6,64,256]{2,1,0:T(8,128)}, f32[24,128]{1,0:T(8,128)}) custom-call(s32[1]{0:T(128)S(6)} %copy.39.refs_0_, bf16[4,392,128]{2,1,0:T(8,128)(2,1)} %bitcast.28, bf16[4,392,128]{2,1,0:T(8,128)(2,1)} %bitcast.29, bf16[64,128]{1,0:T(8,128)(2,1)} %refs_3_.1, ...), custom_call_target="tpu_custom_call" | custom-call | tf_op jit(solution)/shard_map/block/pallas_call | solution.py:985
  78.2 2.5 %spell.1 = (f32[4,392,128]{2,1,0:T(8,128)}, f32[4,392,128]{2,1,0:T(8,128)}, f32[1,128]{1,0:T(1,128)}, f32[1,128]{1,0:T(1,128)}, f32[64,128]{1,0:T(8,128)}, /*ind...) custom-call(bf16[4,392,128]{2,1,0:T(8,128)(2,1)} %get-tuple-element., ...), custom_call_target="tpu_custom_call" | custom-call | tf_op jit(solution)/shard_map/spell/pallas_call | solution.py:1117
